TPU v7x, 8 devices: a whole 2x2x1 slice. The times are simulated.
8 devices in a mesh: rep: 1 (over z), dp: 8 (over x, y, core).
Axes of the slice: x: 2, y: 2, z: 1, core: 2. Of those that a mesh axis runs over, the one named last changes fastest.
Arguments:
- g_w_gate: bfloat16 [8, 2, 1280, 5120], P(('rep', 'dp'))
- g_w_up: bfloat16 [8, 2, 1280, 5120], P(('rep', 'dp'))
- g_w_down: bfloat16 [8, 2, 5120, 1280], P(('rep', 'dp'))
- w_gate: bfloat16 [2, 1280, 5120], replicated
- w_up: bfloat16 [2, 1280, 5120], replicated
- w_down: bfloat16 [2, 5120, 1280], replicated
- m_w_gate: float32 [2, 1280, 5120], P(None, 'dp')
- m_w_up: float32 [2, 1280, 5120], P(None, 'dp')
- m_w_down: float32 [2, 5120, 1280], P(None, 'dp')
- v_w_gate: float32 [2, 1280, 5120], P(None, 'dp')
- v_w_up: float32 [2, 1280, 5120], P(None, 'dp')
- v_w_down: float32 [2, 5120, 1280], P(None, 'dp')
Outputs:
- output 1: bfloat16 [2, 1280, 5120], P('rep')
- output 2: bfloat16 [2, 1280, 5120], P('rep')
- output 3: bfloat16 [2, 5120, 1280], P('rep')
- output 4: float32 [2, 1280, 5120], P('rep', 'dp')
- output 5: float32 [2, 1280, 5120], P('rep', 'dp')
- output 6: float32 [2, 5120, 1280], P('rep', 'dp')
- output 7: float32 [2, 1280, 5120], P('rep', 'dp')
- output 8: float32 [2, 1280, 5120], P('rep', 'dp')
- output 9: float32 [2, 5120, 1280], P('rep', 'dp')
All inputs are finite; a program needn't handle non-finite values.
Results may differ from a plain program's by a relative error of at most 0.022.
Values are sent between devices in bfloat16 or wider.
A program may use at most 2 GiB of HBM per device.

v0:
```python
import jax
import jax.numpy as jnp
from jax import lax
from jax.sharding import PartitionSpec as P


def adamw(w, m, v, g):
    m = 0.9 * m + 0.1 * g
    v = 0.95 * v + 0.05 * g * g
    step = m * lax.rsqrt(v + 1e-8) + 0.1 * w
    return (w - 0.02 * step).astype(jnp.bfloat16), m, v


def clipped(gradients, sum_of_squares, count):
    factor = jnp.minimum(1.0, 0.5 * lax.rsqrt(sum_of_squares / count + 1e-30))
    return [g * factor for g in gradients]


def solution(mesh):
    def step(*arrays):
        terms, weights, m, v = (arrays[i : i + 3] for i in (0, 3, 6, 9))
        gradients = [lax.psum_scatter(t[0], "dp", scatter_dimension=1, tiled=True).astype(jnp.float32) for t in terms]
        squares = lax.psum(sum(jnp.sum(g * g) for g in gradients), "dp")
        gradients = clipped(gradients, squares, lax.psum(1, "dp") * sum(g.size for g in gradients))
        me = lax.axis_index("dp")
        own = [lax.dynamic_slice_in_dim(w, me * one.shape[1], one.shape[1], 1).astype(jnp.float32) for w, one in zip(weights, m, strict=True)]
        new = [adamw(w, m, v, g) for w, m, v, g in zip(own, m, v, gradients, strict=True)]
        whole = [lax.all_gather(one[0], "dp", axis=1, tiled=True) for one in new]
        return (*whole, *(one[1] for one in new), *(one[2] for one in new))

    all_of, cut = P(None, None, None), P(None, "dp", None)
    return jax.shard_map(
        step,
        mesh=mesh,
        in_specs=(P(("rep", "dp"), None, None, None),) * 3 + (all_of,) * 3 + (cut,) * 6,
        out_specs=(P("rep", None, None),) * 3 + (P("rep", "dp", None),) * 6,
        check_vma=False,
    )
```

profile of v0, /device:TPU:0, one launch (start us, length us, event | category | flops | bytes accessed | tf_op | source)
XLA Modules:
  0.0 955.7 jit_solution(16427179186246910789)
XLA Ops:
  7.2 0.0 reduce-scatter.4.cloned.1.call-start
  7.2 0.7 reduce-scatter.4.cloned.1.call-update
  7.9 0.0 reduce-scatter.6.cloned.1.call-start
  8.0 0.7 reduce-scatter.6.cloned.1.call-update
  8.7 0.0 reduce-scatter.8.cloned.1.call-start
  8.7 0.7 reduce-scatter.8.cloned.1.call-update
  9.4 0.0 all-gather.8.cloned.1.call-start
  9.4 156.1 %reduce-scatter.4.cloned.1.call-done = bf16[2,160,5120]{2,1,0:T(8,128)(2,1)} async-done(((bf16[2,1280,5120]{2,1,0:T(8,128)(2,1)}), bf16[2,160,5120]{2,1,0:T(8,128)(2,1)}) %reduce-scatter.4.cloned.1.call-update) | async-done | bytes 3276816 | tf_op jit(solution)/shard_map/reduce_scatter | solution.py:22
  165.6 4.2 fusion.9
  169.8 150.6 %reduce-scatter.6.cloned.1.call-done = bf16[2,160,5120]{2,1,0:T(8,128)(2,1)} async-done(((bf16[2,1280,5120]{2,1,0:T(8,128)(2,1)}), bf16[2,160,5120]{2,1,0:T(8,128)(2,1)}) %reduce-scatter.6.cloned.1.call-update) | async-done | bytes 3276816 | tf_op jit(solution)/shard_map/reduce_scatter | solution.py:22
  320.4 4.2 fusion.10
  325.9 149.3 %reduce-scatter.8.cloned.1.call-done = bf16[2,640,1280]{2,1,0:T(8,128)(2,1)} async-done(((bf16[2,5120,1280]{2,1,0:T(8,128)(2,1)}), bf16[2,640,1280]{2,1,0:T(8,128)(2,1)}) %reduce-scatter.8.cloned.1.call-update) | async-done | bytes 3276816 | tf_op jit(solution)/shard_map/reduce_scatter | solution.py:22
  475.2 4.2 fusion.11
  480.0 22.3 %psum.7 = f32[]{:T(128)} all-reduce(f32[]{:T(128)S(6)} %add.65), channel_id=1, replica_groups=mesh['rep'=1,'dp'=8] {'dp'}, use_global_device_ids=true, to_apply=%region_6.0 | all-reduce | flops 1 | bytes 8 | tf_op jit(solution)/shard_map/psum | solution.py:23
  503.0 13.4 %fusion.17 = (bf16[2,640,1280]{2,1,0:T(8,128)(2,1)}, f32[2,640,1280]{2,1,0:T(8,128)}, f32[2,640,1280]{2,1,0:T(8,128)}) fusion(bf16[2,5120,1280]{2,1,0:T(8,128)(2,1)} %param.17, s32[]{:T(128)S(6)} %select_n.8, f32[]{:T(128)S(6)} %min_shard_map.3, bf16[2,640,1280]{2,1,0:T(8,128)(2,1)} %reduce-scatter.8.cloned.1.call-done, f32[2,640,1280]{2,1,0:T(8,128)} %param.23, ...), kind=kLoop, calls=%fused_computation.32 | loop fusion | flops 27852800 | bytes 36044808 | tf_op jit(solution)/shard_map/convert_element_type | solution.py:11
  516.4 0.0 all-gather.8.cloned.1.call-update
  516.4 0.0 all-gather.4.cloned.1.call-start
  516.5 0.0 copy-start.1
  516.5 13.6 %fusion.8 = (bf16[2,160,5120]{2,1,0:T(8,128)(2,1)}, f32[2,160,5120]{2,1,0:T(8,128)}, f32[2,160,5120]{2,1,0:T(8,128)}) fusion(bf16[2,1280,5120]{2,1,0:T(8,128)(2,1)} %param.15, s32[]{:T(128)S(6)} %select_n.7, f32[]{:T(128)S(6)} %min_shard_map.3, bf16[2,160,5120]{2,1,0:T(8,128)(2,1)} %reduce-scatter.4.cloned.1.call-done, f32[2,160,5120]{2,1,0:T(8,128)} %param.21, ...), kind=kLoop, calls=%fused_computation.23 | loop fusion | flops 27852800 | bytes 36044808 | tf_op jit(solution)/shard_map/convert_element_type | solution.py:11
  530.1 0.0 all-gather.4.cloned.1.call-update
  530.1 0.0 all-gather.6.cloned.1.call-start
  530.2 0.0 copy-done.1
  530.2 11.4 %fusion.14 = (bf16[2,160,5120]{2,1,0:T(8,128)(2,1)}, f32[2,160,5120]{2,1,0:T(8,128)}, f32[2,160,5120]{2,1,0:T(8,128)}) fusion(bf16[2,1280,5120]{2,1,0:T(8,128)(2,1)} %param.16, s32[]{:T(128)S(6)} %select_n.7, f32[]{:T(128)S(6)} %min_shard_map.3, bf16[2,160,5120]{2,1,0:T(8,128)(2,1)S(1)} %copy-done.1, f32[2,160,5120]{2,1,0:T(8,128)} %param.22, ...), kind=kLoop, calls=%fused_computation.29 | loop fusion | flops 27852800 | bytes 36044808 | tf_op jit(solution)/shard_map/convert_element_type | solution.py:11
  541.6 0.0 all-gather.6.cloned.1.call-update
  541.6 101.1 %all-gather.8.cloned.1.call-done = bf16[2,5120,1280]{2,1,0:T(8,128)(2,1)} async-done(((bf16[2,640,1280]{2,1,0:T(8,128)(2,1)}), bf16[2,5120,1280]{2,1,0:T(8,128)(2,1)}) %all-gather.8.cloned.1.call-update) | async-done | bytes 26214416 | tf_op jit(solution)/shard_map/all_gather | solution.py:28
  642.7 126.4 %all-gather.4.cloned.1.call-done = bf16[2,1280,5120]{2,1,0:T(8,128)(2,1)} async-done(((bf16[2,160,5120]{2,1,0:T(8,128)(2,1)}), bf16[2,1280,5120]{2,1,0:T(8,128)(2,1)}) %all-gather.4.cloned.1.call-update) | async-done | bytes 26214416 | tf_op jit(solution)/shard_map/all_gather | solution.py:28
  769.1 126.4 %all-gather.6.cloned.1.call-done = bf16[2,1280,5120]{2,1,0:T(8,128)(2,1)} async-done(((bf16[2,160,5120]{2,1,0:T(8,128)(2,1)}), bf16[2,1280,5120]{2,1,0:T(8,128)(2,1)}) %all-gather.6.cloned.1.call-update) | async-done | bytes 26214416 | tf_op jit(solution)/shard_map/all_gather | solution.py:28
  895.5 0.0 copy-start
  895.5 22.4 %copy.24 = bf16[2,1280,5120]{2,1,0:T(8,128)(2,1)} copy(bf16[2,1280,5120]{2,1,0:T(8,128)(2,1)} %all-gather.4.cloned.1.call-done) | data formatting | bytes 52428800
  917.9 3.4 copy-done
  921.3 9.3 copy.25
  930.6 18.3 %copy.26 = bf16[2,5120,1280]{2,1,0:T(8,128)(2,1)} copy(bf16[2,5120,1280]{2,1,0:T(8,128)(2,1)} %all-gather.8.cloned.1.call-done) | data formatting | bytes 52428800
Async XLA Ops:
  7.2 158.4 %reduce-scatter.4.cloned.1.call-start = ((), (), s32[]{:S(2)}) async-start(), calls=%async_computation.3 | async-start | bytes 29491200 | tf_op jit(solution)/shard_map/reduce_scatter | solution.py:22
  7.9 312.4 %reduce-scatter.6.cloned.1.call-start = ((), (), s32[]{:S(2)}) async-start(), calls=%async_computation.4 | async-start | bytes 29491200 | tf_op jit(solution)/shard_map/reduce_scatter | solution.py:22
  8.7 466.5 %reduce-scatter.8.cloned.1.call-start = ((), (), s32[]{:S(2)}) async-start(), calls=%async_computation.5 | async-start | bytes 29491200 | tf_op jit(solution)/shard_map/reduce_scatter | solution.py:22
  9.4 633.3 %all-gather.8.cloned.1.call-start = ((), (), s32[]{:S(2)}) async-start(), calls=%async_computation.8 | async-start | bytes 29491200 | tf_op jit(solution)/shard_map/all_gather | solution.py:28
  516.4 252.7 %all-gather.4.cloned.1.call-start = ((), (), s32[]{:S(2)}) async-start(), calls=%async_computation.6 | async-start | bytes 29491200 | tf_op jit(solution)/shard_map/all_gather | solution.py:28
  516.5 13.7 %copy-start.1 = (bf16[2,160,5120]{2,1,0:T(8,128)(2,1)S(1)}, bf16[2,160,5120]{2,1,0:T(8,128)(2,1)}, u32[]{:S(2)}) copy-start(bf16[2,160,5120]{2,1,0:T(8,128)(2,1)} %reduce-scatter.6.cloned.1.call-done) | copy-start | bytes 9830404
  530.1 365.4 %all-gather.6.cloned.1.call-start = ((), (), s32[]{:S(2)}) async-start(), calls=%async_computation.7 | async-start | bytes 29491200 | tf_op jit(solution)/shard_map/all_gather | solution.py:28
  895.5 25.8 %copy-start = (bf16[2,1280,5120]{2,1,0:T(8,128)(2,1)S(1)}, bf16[2,1280,5120]{2,1,0:T(8,128)(2,1)}, u32[]{:S(2)}) copy-start(bf16[2,1280,5120]{2,1,0:T(8,128)(2,1)} %all-gather.6.cloned.1.call-done) | copy-start | bytes 78643200
Sparse Core Ops, SparseCore 0:
  11.6 153.9 reduce-scatter.3
  169.2 151.1 reduce-scatter.5
  324.0 151.1 reduce-scatter.7
  516.6 126.1 all-gather.7
  645.0 124.0 all-gather.3
  771.4 124.0 all-gather.5
where the time goes:
time: 956 us
  waiting for transfers between devices  812 us (85%)
  local copies, waits for them, and re-layouts  53.4 us (6%)
  other arithmetic  51.1 us (5%)
  blocking collectives  22.3 us (2%)
  between operations  16.8 us (2%)
    reduce_scatter x3, waiting for transfers between devices, step(): lax.psum_scatter(t[0], 'dp', scatter_dimension=1, tiled=True)  456 us
    all_gather x3, waiting for transfers between devices, step(): whole = [lax.all_gather(one[0], 'dp', axis=1, tiled=True) for one in new]  354 us
    unnamed x7, local copies, waits for them, and re-layouts  53.4 us
    convert_element_type x3, other arithmetic, adamw(): return ((w - 0.02 * step).astype(jnp.bfloat16), m, v)  38.4 us
    psum x1, blocking collectives, step(): squares = lax.psum(sum((jnp.sum(g * g) for g in gradients)), 'dp')  22.3 us
  transfers between devices with their start and end apart: 6, of which 6 were waited for; matrix products, arithmetic and copies ran while one was open for 3% of the time, Pallas kernels for 0%

commit v1 on v0

v1 whole, which is shorter than its diff:
```python
import functools

import jax
import jax.numpy as jnp
from jax import lax
from jax.experimental import pallas as pl
from jax.experimental.pallas import tpu as pltpu
from jax.sharding import PartitionSpec as P

MESH = pl.DeviceIdType.MESH
F32, BF16 = jnp.float32, jnp.bfloat16
CHIPS = ((1, 1), (1, 0), (0, 1), (0, 0))


def adamw(w, m, v, g):
    m = 0.9 * m + 0.1 * g
    v = 0.95 * v + 0.05 * g * g
    step = m * lax.rsqrt(v + 1e-8) + 0.1 * w
    return (w - 0.02 * step).astype(BF16), m, v


def place(dx=0, dy=0, dc=0):
    me = lax.axis_index("dp")
    x, y, c = me // 4, lax.rem(me // 2, 2), lax.rem(me, 2)
    x = 1 - x if dx else x
    y = 1 - y if dy else y
    c = 1 - c if dc else c
    return 4 * x + 2 * y + c


def rows_of(ref, half, total):
    return ref.at[pl.ds(half * total, total)]


def add_into(dst, parts, lanes):
    def body(i, carry):
        s = pl.ds(pl.multiple_of(i * 16, 16), 16)
        total = parts[0][s, :].astype(F32)
        for p in parts[1:]:
            total = total + p[s, :].astype(F32)
        dst[s, :] = total.astype(BF16)
        return carry

    lax.fori_loop(0, dst.shape[0] // 16, body, 0)


def add_square(dst, parts, lanes, acc):
    def body(i, carry):
        s = pl.ds(pl.multiple_of(i * 16, 16), 16)
        total = parts[0][s, :].astype(F32)
        for p in parts[1:]:
            total = total + p[s, :].astype(F32)
        total = total.astype(BF16)
        dst[s, :] = total
        total = total.astype(F32)
        for k in range(lanes // 128):
            one = total[:, k * 128 : (k + 1) * 128]
            carry = carry + one * one
        return carry

    acc[...] += lax.fori_loop(0, dst.shape[0] // 16, body, jnp.zeros((16, 128), F32))


def sum_kernel(shapes, *refs):
    g, refs = refs[:3], refs[3:]
    out, squares, refs = refs[:3], refs[3], refs[4:]
    near, refs = refs[:3], refs[3:]
    snd, rcv, own, par, refs = refs[0:2], refs[2:4], refs[4:6], refs[6:8], refs[8:]
    acc, norms, d2d_s, d2d_r, link_s, link_r, own_sem, par_sem, out_sem, norm_s, norm_r = refs
    layers = g[0].shape[1]
    units = [(a, l) for a in range(3) for l in range(layers)]
    kind = [0, 0, 1]
    slot = {}
    for a, l in units:
        slot[a, l] = sum(1 for u in slot if kind[u[0]] == kind[a])
    me = lax.axis_index("dp")
    rep = lax.axis_index("rep")
    xn, yn, cn = place(dx=1), place(dy=1), place(dc=1)

    barrier = pltpu.get_barrier_semaphore()
    others = [lax.rem(me + k, 8) for k in range(1, 8)]
    for d in others:
        pl.semaphore_signal(barrier, inc=1, device_id=(rep, d), device_id_type=MESH)
    pl.semaphore_wait(barrier, 7)

    def half_of(u, device, h):
        a, l = u
        n = shapes[a][0] // 2
        return g[a].at[0, l, pl.ds(pl.multiple_of(device * (2 * n) + h * n, 16), n)]

    d2d = {}
    for i, u in enumerate(units):
        for s, (dx, dy) in enumerate(CHIPS):
            for h in range(2):
                d2d[i, s, h] = pltpu.make_async_remote_copy(
                    src_ref=half_of(u, place(dx, dy, 1), h),
                    dst_ref=near[u[0]].at[u[1], s, h],
                    send_sem=d2d_s.at[i, s, h],
                    recv_sem=d2d_r.at[i, s, h],
                    device_id=(rep, cn),
                    device_id_type=MESH,
                )
                d2d[i, s, h].start()

    tasks = []
    for i in range(len(units)):
        tasks += [(i, 0, 0, (), 0), (i, 0, 1, (), 1), (i, 1, 0, (), 2), (i, 2, 1, (), 3)]
    for i in range(len(units)):
        tasks += [(i, 1, 1, (1,), 4), (i, 2, 0, (0,), 5)]
    for i in range(len(units)):
        tasks += [(i, 3, 0, (2, 5), None), (i, 3, 1, (3, 4), None)]

    link = {}

    def link_copy(i, j):
        a, l = units[i]
        k = kind[a]
        return pltpu.make_async_remote_copy(
            src_ref=snd[k].at[slot[a, l], j % 4],
            dst_ref=rcv[k].at[slot[a, l], j],
            send_sem=link_s.at[i, j],
            recv_sem=link_r.at[i, j],
            device_id=(rep, xn if j % 2 == 0 else yn),
            device_id_type=MESH,
        )

    loads = {}

    def load(t):
        i, s, h, _, _ = tasks[t]
        a, l = units[i]
        k = kind[a]
        b = t % 2
        mine = pltpu.make_async_copy(half_of(units[i], place(*CHIPS[s], 0), h), own[k].at[b], own_sem.at[b])
        mine.start()
        d2d[i, s, h].wait_recv()
        theirs = pltpu.make_async_copy(near[a].at[l, s, h], par[k].at[b], par_sem.at[b])
        theirs.start()
        loads[t] = (mine, theirs)

    acc[...] = jnp.zeros_like(acc)
    load(0)
    stores = []
    for t, (i, s, h, arrived, j) in enumerate(tasks):
        if t + 1 < len(tasks):
            load(t + 1)
        a, l = units[i]
        k = kind[a]
        lanes = shapes[a][1]
        for one in loads[t]:
            one.wait()
        for r in arrived:
            link_copy(i, r).wait_recv()
        parts = [own[k].at[t % 2], par[k].at[t % 2]] + [rcv[k].at[slot[a, l], r] for r in arrived]
        if j is None:
            dst = snd[k].at[slot[a, l], 2 + h]
            link[i, 2 + h].wait_send()
            add_square(dst, parts, lanes, acc)
            n = shapes[a][0] // 2
            store = pltpu.make_async_copy(dst, out[a].at[l, pl.ds(h * n, n)], out_sem.at[i, h])
            store.start()
            stores.append(store)
        else:
            dst = snd[k].at[slot[a, l], j % 4]
            if j >= 4:
                link[i, j - 4].wait_send()
            add_into(dst, parts, lanes)
            link[i, j] = link_copy(i, j)
            link[i, j].start()

    sent = []
    for k in range(1, 8):
        to = lax.rem(me + k, 8)
        copy = pltpu.make_async_remote_copy(
            src_ref=acc, dst_ref=norms.at[me], send_sem=norm_s.at[k - 1], recv_sem=norm_r.at[k - 1], device_id=(rep, to), device_id_type=MESH
        )
        copy.start()
        sent.append(copy)
    norms[me] = acc[...]
    for copy in sent:
        copy.wait_recv()
    total = norms[0]
    for d in range(1, 8):
        total = total + norms[d]
    squares[...] = jnp.full(squares.shape, jnp.sum(total), F32)
    for copy in sent:
        copy.wait_send()
    for store in stores:
        store.wait()
    for copy in d2d.values():
        copy.wait_send()
    for i in range(len(units)):
        for j in (4, 5):
            link[i, j].wait_send()


def summed(terms):
    layers = terms[0].shape[1]
    shapes = [(t.shape[2] // 8, t.shape[3]) for t in terms]
    halves = [(shapes[0][0] // 2, shapes[0][1]), (shapes[2][0] // 2, shapes[2][1])]
    count = [2 * layers, layers]
    any_ = pl.BlockSpec(memory_space=pl.ANY)
    outs = pl.pallas_call(
        functools.partial(sum_kernel, shapes),
        out_shape=[jax.ShapeDtypeStruct((layers, *s), BF16) for s in shapes]
        + [jax.ShapeDtypeStruct((8, 128), F32)]
        + [jax.ShapeDtypeStruct((layers, 4, 2, s[0] // 2, s[1]), BF16) for s in shapes],
        in_specs=[any_] * 3,
        out_specs=[any_] * 3 + [pl.BlockSpec(memory_space=pltpu.VMEM)] + [any_] * 3,
        scratch_shapes=[pltpu.VMEM((n, 4, *s), BF16) for n, s in zip(count, halves)]
        + [pltpu.VMEM((n, 6, *s), BF16) for n, s in zip(count, halves)]
        + [pltpu.VMEM((2, *s), BF16) for s in halves] * 2
        + [
            pltpu.VMEM((16, 128), F32),
            pltpu.VMEM((8, 16, 128), F32),
            pltpu.SemaphoreType.DMA((3 * layers, 4, 2)),
            pltpu.SemaphoreType.DMA((3 * layers, 4, 2)),
            pltpu.SemaphoreType.DMA((3 * layers, 6)),
            pltpu.SemaphoreType.DMA((3 * layers, 6)),
            pltpu.SemaphoreType.DMA((2,)),
            pltpu.SemaphoreType.DMA((2,)),
            pltpu.SemaphoreType.DMA((3 * layers, 2)),
            pltpu.SemaphoreType.DMA((7,)),
            pltpu.SemaphoreType.DMA((7,)),
        ],
        compiler_params=pltpu.CompilerParams(collective_id=0, has_side_effects=True, vmem_limit_bytes=62 * 1024 * 1024),
        name="sum_terms",
    )(*terms)
    return outs[:3], outs[3][0, 0]


def clipped(gradients, sum_of_squares, count):
    factor = jnp.minimum(1.0, 0.5 * lax.rsqrt(sum_of_squares / count + 1e-30))
    return [g * factor for g in gradients]


def solution(mesh):
    def step(*arrays):
        terms, weights, m, v = (arrays[i : i + 3] for i in (0, 3, 6, 9))
        gradients, squares = summed(terms)
        gradients = [g.astype(F32) for g in gradients]
        gradients = clipped(gradients, squares, 8 * sum(g.size for g in gradients))
        me = lax.axis_index("dp")
        own = [lax.dynamic_slice_in_dim(w, me * one.shape[1], one.shape[1], 1).astype(F32) for w, one in zip(weights, m)]
        new = [adamw(w, m, v, g) for w, m, v, g in zip(own, m, v, gradients)]
        whole = [lax.all_gather(one[0], "dp", axis=1, tiled=True) for one in new]
        return (*whole, *(one[1] for one in new), *(one[2] for one in new))

    all_of, cut = P(None, None, None), P(None, "dp", None)
    return jax.shard_map(
        step,
        mesh=mesh,
        in_specs=(P(("rep", "dp"), None, None, None),) * 3 + (all_of,) * 3 + (cut,) * 6,
        out_specs=(P("rep", None, None),) * 3 + (P("rep", "dp", None),) * 6,
        check_vma=False,
    )
```

time: 956 us -> 794 us (0.83)
  waiting for transfers between devices: 812 us -> 352 us
  Pallas kernels: 0 us -> 334 us
  blocking collectives: 22.3 us -> 0 us
  other arithmetic: 51.1 us -> 38.6 us
    reduce_scatter x3 -> x0, waiting for transfers between devices: 456 us -> none  [step(): lax.psum_scatter(t[0], 'dp', scatter_dimension=1, tiled=True)]
    pallas_call x0 -> x1, Pallas kernels: none -> 334 us  [summed(): pl.pallas_call(functools.partial(sum_kernel, shapes), out_shape=[jax.Shap...]
    psum x1 -> x0, blocking collectives: 22.3 us -> none  [step(): squares = lax.psum(sum((jnp.sum(g * g) for g in gradients)), 'dp')]
    reduce_sum x3 -> x0, other arithmetic: 12.6 us -> none  [step(): squares = lax.psum(sum((jnp.sum(g * g) for g in gradients)), 'dp')]
  transfers between devices with their start and end apart: 6 -> 3, of which waited for: 6 -> 3; matrix products, arithmetic and copies ran while one was open for 3% -> 3% of each run, Pallas kernels for 0% -> 0%
where the time goes in v1:
time: 794 us
  waiting for transfers between devices  352 us (44%)
  Pallas kernels  334 us (42%)
  local copies, waits for them, and re-layouts  54.6 us (7%)
  other arithmetic  38.6 us (5%)
  between operations  14.5 us (2%)
    all_gather x3, waiting for transfers between devices, step(): whole = [lax.all_gather(one[0], 'dp', axis=1, tiled=True) for one in new]  352 us
    pallas_call x1, Pallas kernels, summed(): pl.pallas_call(functools.partial(sum_kernel, shapes), out_shape=[jax.Shap...  334 us
    unnamed x7, local copies, waits for them, and re-layouts  53.4 us
    convert_element_type x3, other arithmetic, adamw(): return ((w - 0.02 * step).astype(BF16), m, v)  38.6 us
  transfers between devices with their start and end apart: 3, of which 3 were waited for; matrix products, arithmetic and copies ran while one was open for 3% of the time, Pallas kernels for 0%

profile of v1, /device:TPU:0, one launch (start us, length us, event | category | flops | bytes accessed | tf_op | source)
XLA Modules:
  0.0 793.8 jit_solution(15367838065918833950)
XLA Ops:
  7.2 0.0 all-gather.4.cloned.1.call-start
  7.2 334.0 %sum_terms.1 = (bf16[2,160,5120]{2,1,0:T(8,128)(2,1)}, bf16[2,160,5120]{2,1,0:T(8,128)(2,1)}, bf16[2,640,1280]{2,1,0:T(8,128)(2,1)}, f32[8,128]{1,0:T(8,128)}, b...) custom-call(bf16[1,2,1280,5120]{3,2,1,0:T(8,128)(2,1)} %refs_0_.1, ...), custom_call_target="tpu_custom_call" | custom-call | tf_op jit(solution)/shard_map/sum_terms/pallas_call | solution.py:203
  341.2 1.2 slice.3
  343.1 13.5 %fusion.2 = (bf16[2,160,5120]{2,1,0:T(8,128)(2,1)}, f32[2,160,5120]{2,1,0:T(8,128)}, f32[2,160,5120]{2,1,0:T(8,128)}) fusion(bf16[2,1280,5120]{2,1,0:T(8,128)(2,1)} %param.15, s32[]{:T(128)S(6)} %select_n.7, f32[]{:T(128)} %bitcast, bf16[2,160,5120]{2,1,0:T(8,128)(2,1)} %get-tuple-element.13, f32[2,160,5120]{2,1,0:T(8,128)} %param.21, f32[2,160,5120]{2,1,0:T(8,128)} %param.18), kind=kLoop, calls=%fused_computation.11 | loop fusion | flops 27852800 | bytes 36044808 | tf_op jit(solution)/shard_map/convert_element_type | solution.py:19
  356.6 0.0 all-gather.4.cloned.1.call-update
  356.6 0.0 all-gather.8.cloned.1.call-start
  356.7 0.0 copy-start.1
  356.7 13.7 %fusion.8 = (bf16[2,640,1280]{2,1,0:T(8,128)(2,1)}, f32[2,640,1280]{2,1,0:T(8,128)}, f32[2,640,1280]{2,1,0:T(8,128)}) fusion(bf16[2,5120,1280]{2,1,0:T(8,128)(2,1)} %param.17, s32[]{:T(128)S(6)} %select_n.8, f32[]{:T(128)} %bitcast, bf16[2,640,1280]{2,1,0:T(8,128)(2,1)} %get-tuple-element.16, f32[2,640,1280]{2,1,0:T(8,128)} %param.23, f32[2,640,1280]{2,1,0:T(8,128)} %param.20), kind=kLoop, calls=%fused_computation.17 | loop fusion | flops 27852800 | bytes 36044808 | tf_op jit(solution)/shard_map/convert_element_type | solution.py:19
  370.4 0.0 all-gather.8.cloned.1.call-update
  370.4 0.0 all-gather.6.cloned.1.call-start
  370.5 0.0 copy-done.1
  370.5 11.4 %fusion.5 = (bf16[2,160,5120]{2,1,0:T(8,128)(2,1)}, f32[2,160,5120]{2,1,0:T(8,128)}, f32[2,160,5120]{2,1,0:T(8,128)}) fusion(bf16[2,1280,5120]{2,1,0:T(8,128)(2,1)} %param.16, s32[]{:T(128)S(6)} %select_n.7, f32[]{:T(128)} %bitcast, bf16[2,160,5120]{2,1,0:T(8,128)(2,1)S(1)} %copy-done.1, f32[2,160,5120]{2,1,0:T(8,128)} %param.22, f32[2,160,5120]{2,1,0:T(8,128)} %param.19), kind=kLoop, calls=%fused_computation.14 | loop fusion | flops 27852800 | bytes 36044808 | tf_op jit(solution)/shard_map/convert_element_type | solution.py:19
  381.9 0.0 all-gather.6.cloned.1.call-update
  381.9 98.9 %all-gather.4.cloned.1.call-done = bf16[2,1280,5120]{2,1,0:T(8,128)(2,1)} async-done(((bf16[2,160,5120]{2,1,0:T(8,128)(2,1)}), bf16[2,1280,5120]{2,1,0:T(8,128)(2,1)}) %all-gather.4.cloned.1.call-update) | async-done | bytes 26214416 | tf_op jit(solution)/shard_map/all_gather | solution.py:246
  480.8 126.5 %all-gather.8.cloned.1.call-done = bf16[2,5120,1280]{2,1,0:T(8,128)(2,1)} async-done(((bf16[2,640,1280]{2,1,0:T(8,128)(2,1)}), bf16[2,5120,1280]{2,1,0:T(8,128)(2,1)}) %all-gather.8.cloned.1.call-update) | async-done | bytes 26214416 | tf_op jit(solution)/shard_map/all_gather | solution.py:246
  607.3 126.5 %all-gather.6.cloned.1.call-done = bf16[2,1280,5120]{2,1,0:T(8,128)(2,1)} async-done(((bf16[2,160,5120]{2,1,0:T(8,128)(2,1)}), bf16[2,1280,5120]{2,1,0:T(8,128)(2,1)}) %all-gather.6.cloned.1.call-update) | async-done | bytes 26214416 | tf_op jit(solution)/shard_map/all_gather | solution.py:246
  733.9 0.0 copy-start
  733.9 22.4 %copy.24 = bf16[2,1280,5120]{2,1,0:T(8,128)(2,1)} copy(bf16[2,1280,5120]{2,1,0:T(8,128)(2,1)} %all-gather.4.cloned.1.call-done) | data formatting | bytes 52428800
  756.3 3.4 copy-done
  759.7 9.3 %copy.25 = bf16[2,1280,5120]{2,1,0:T(8,128)(2,1)} copy(bf16[2,1280,5120]{2,1,0:T(8,128)(2,1)S(1)} %copy-done) | data formatting | bytes 52428800
  768.9 18.3 %copy.26 = bf16[2,5120,1280]{2,1,0:T(8,128)(2,1)} copy(bf16[2,5120,1280]{2,1,0:T(8,128)(2,1)} %all-gather.8.cloned.1.call-done) | data formatting | bytes 52428800
Async XLA Ops:
  7.2 473.6 %all-gather.4.cloned.1.call-start = ((), (), s32[]{:S(2)}) async-start(), calls=%async_computation | async-start | bytes 29491200 | tf_op jit(solution)/shard_map/all_gather | solution.py:246
  356.6 250.7 %all-gather.8.cloned.1.call-start = ((), (), s32[]{:S(2)}) async-start(), calls=%async_computation.2 | async-start | bytes 29491200 | tf_op jit(solution)/shard_map/all_gather | solution.py:246
  356.7 13.8 %copy-start.1 = (bf16[2,160,5120]{2,1,0:T(8,128)(2,1)S(1)}, bf16[2,160,5120]{2,1,0:T(8,128)(2,1)}, u32[]{:S(2)}) copy-start(bf16[2,160,5120]{2,1,0:T(8,128)(2,1)} %get-tuple-element.15) | copy-start | bytes 9830404
  370.4 363.4 %all-gather.6.cloned.1.call-start = ((), (), s32[]{:S(2)}) async-start(), calls=%async_computation.1 | async-start | bytes 29491200 | tf_op jit(solution)/shard_map/all_gather | solution.py:246
  733.9 25.8 %copy-start = (bf16[2,1280,5120]{2,1,0:T(8,128)(2,1)S(1)}, bf16[2,1280,5120]{2,1,0:T(8,128)(2,1)}, u32[]{:S(2)}) copy-start(bf16[2,1280,5120]{2,1,0:T(8,128)(2,1)} %all-gather.6.cloned.1.call-done) | copy-start | bytes 78643200
Sparse Core Ops, SparseCore 0:
  356.7 124.0 all-gather.3
  483.2 124.0 all-gather.7
  609.7 124.0 all-gather.5

commit v2 on v1

--- a/solution.py
+++ b/solution.py
@@ -7,16 +7,10 @@
 from jax.experimental.pallas import tpu as pltpu
 from jax.sharding import PartitionSpec as P
 
+
 MESH = pl.DeviceIdType.MESH
 F32, BF16 = jnp.float32, jnp.bfloat16
 CHIPS = ((1, 1), (1, 0), (0, 1), (0, 0))
-
-
-def adamw(w, m, v, g):
-    m = 0.9 * m + 0.1 * g
-    v = 0.95 * v + 0.05 * g * g
-    step = m * lax.rsqrt(v + 1e-8) + 0.1 * w
-    return (w - 0.02 * step).astype(BF16), m, v
 
 
 def place(dx=0, dy=0, dc=0):
@@ -28,11 +22,7 @@
     return 4 * x + 2 * y + c
 
 
-def rows_of(ref, half, total):
-    return ref.at[pl.ds(half * total, total)]
-
-
-def add_into(dst, parts, lanes):
+def add_into(dst, parts):
     def body(i, carry):
         s = pl.ds(pl.multiple_of(i * 16, 16), 16)
         total = parts[0][s, :].astype(F32)
@@ -164,7 +154,7 @@
             dst = snd[k].at[slot[a, l], j % 4]
             if j >= 4:
                 link[i, j - 4].wait_send()
-            add_into(dst, parts, lanes)
+            add_into(dst, parts)
             link[i, j] = link_copy(i, j)
             link[i, j].start()
 
@@ -226,25 +216,114 @@
         compiler_params=pltpu.CompilerParams(collective_id=0, has_side_effects=True, vmem_limit_bytes=62 * 1024 * 1024),
         name="sum_terms",
     )(*terms)
-    return outs[:3], outs[3][0, 0]
-
-
-def clipped(gradients, sum_of_squares, count):
-    factor = jnp.minimum(1.0, 0.5 * lax.rsqrt(sum_of_squares / count + 1e-30))
-    return [g * factor for g in gradients]
+    return outs[:3], outs[3]
+
+
+def step_kernel(count, me, squares, g, w, m, v, *rest):
+    new_w, new_m, new_v = rest[-3:]
+    factor = jnp.minimum(1.0, 0.5 * lax.rsqrt(squares[:1, :1] / count + 1e-30))
+    g = g[0].astype(F32) * factor
+    m = 0.9 * m[0] + 0.1 * g
+    v = 0.95 * v[0] + 0.05 * g * g
+    w = w[0].astype(F32)
+    step = m * lax.rsqrt(v + 1e-8) + 0.1 * w
+    new_w[...] = (w - 0.02 * step).astype(BF16)
+    new_m[0] = m
+    new_v[0] = v
+
+
+def stepped(me, squares, count, layer, g, w, m, v, before):
+    rows, lanes = g.shape[1:]
+    n = rows // 5
+    here = pl.BlockSpec((1, n, lanes), lambda i, me: (layer, i, 0))
+    specs = [
+        pl.BlockSpec((8, 128), lambda i, me: (0, 0)),
+        here,
+        pl.BlockSpec((1, n, lanes), lambda i, me: (layer, me[0] * 5 + i, 0)),
+        here,
+        here,
+    ]
+    moment = jax.ShapeDtypeStruct(m.shape, F32)
+    return pl.pallas_call(
+        functools.partial(step_kernel, count),
+        out_shape=[jax.ShapeDtypeStruct((rows, lanes), BF16), moment, moment],
+        grid_spec=pltpu.PrefetchScalarGridSpec(
+            num_scalar_prefetch=1,
+            grid=(5,),
+            in_specs=specs + [pl.BlockSpec(memory_space=pl.ANY)] * len(before),
+            out_specs=[pl.BlockSpec((n, lanes), lambda i, me: (i, 0)), here, here],
+        ),
+        input_output_aliases={6 + i: 1 + i for i in range(len(before))},
+        cost_estimate=pl.CostEstimate(flops=15 * rows * lanes, bytes_accessed=22 * rows * lanes, transcendentals=rows * lanes),
+        name="adamw",
+    )(me, squares, g, w, m, v, *before)
+
+
+def place_kernel(layer, offsets, n_before, *refs):
+    n = len(offsets)
+    blocks, out = refs[:n], refs[n + n_before]
+    held, in_sem, out_sem = refs[n + n_before + 1 :]
+    rows = blocks[0].shape[0]
+    loads = [pltpu.make_async_copy(b, held.at[i], in_sem.at[i]) for i, b in enumerate(blocks)]
+    for one in loads:
+        one.start()
+    stores = []
+    for i, offset in enumerate(offsets):
+        loads[i].wait()
+        at = pl.multiple_of(place(*offset) * rows, 16)
+        stores.append(pltpu.make_async_copy(held.at[i], out.at[layer, pl.ds(at, rows)], out_sem.at[i]))
+        stores[-1].start()
+    for one in stores:
+        one.wait()
+
+
+def placed(blocks, offsets, layer, shape, before):
+    n = len(blocks)
+    any_ = pl.BlockSpec(memory_space=pl.ANY)
+    return pl.pallas_call(
+        functools.partial(place_kernel, layer, offsets, len(before)),
+        out_shape=jax.ShapeDtypeStruct(shape, BF16),
+        in_specs=[any_] * (n + len(before)),
+        out_specs=any_,
+        scratch_shapes=[pltpu.VMEM((n, *blocks[0].shape), BF16), pltpu.SemaphoreType.DMA((n,)), pltpu.SemaphoreType.DMA((n,))],
+        input_output_aliases={n: 0} if before else {},
+        cost_estimate=pl.CostEstimate(flops=0, bytes_accessed=4 * n * blocks[0].size, transcendentals=0),
+        name="place",
+    )(*blocks, *before)
+
+
+def send(block, dx=0, dy=0, dc=0):
+    flip = 4 * dx + 2 * dy + dc
+    return lax.ppermute(block, "dp", [(d, d ^ flip) for d in range(8)])
 
 
 def solution(mesh):
     def step(*arrays):
         terms, weights, m, v = (arrays[i : i + 3] for i in (0, 3, 6, 9))
         gradients, squares = summed(terms)
-        gradients = [g.astype(F32) for g in gradients]
-        gradients = clipped(gradients, squares, 8 * sum(g.size for g in gradients))
-        me = lax.axis_index("dp")
-        own = [lax.dynamic_slice_in_dim(w, me * one.shape[1], one.shape[1], 1).astype(F32) for w, one in zip(weights, m)]
-        new = [adamw(w, m, v, g) for w, m, v, g in zip(own, m, v, gradients)]
-        whole = [lax.all_gather(one[0], "dp", axis=1, tiled=True) for one in new]
-        return (*whole, *(one[1] for one in new), *(one[2] for one in new))
+        count = 8 * sum(g.size for g in gradients)
+        me = lax.axis_index("dp")[None]
+        layers = weights[0].shape[0]
+        new_m, new_v, whole = [()] * 3, [()] * 3, [()] * 3
+        units = [(a, l) for a in range(3) for l in range(layers)]
+        first, second = [], []
+        for a, l in units:
+            before = (new_m[a], new_v[a]) if l else ()
+            own, new_m[a], new_v[a] = stepped(me, squares, count, l, gradients[a], weights[a], m[a], v[a], before)
+            first.append((own, send(own, dx=1), send(own, dy=1), send(own, dc=1)))
+        for i, (own, x, y, c) in enumerate(first):
+            far = send(y, dx=1) if i % 2 else send(x, dy=1)
+            second.append((far, send(x, dc=1), send(y, dc=1)))
+        for i, (a, l) in enumerate(units):
+            own, x, y, c = first[i]
+            far, xc, yc = second[i]
+            places = ((0, 0, 0), (1, 0, 0), (0, 1, 0), (0, 0, 1), (1, 0, 1), (0, 1, 1))
+            whole[a] = placed([own, x, y, c, xc, yc], places, l, weights[a].shape, (whole[a],) if l else ())
+        for i, (a, l) in enumerate(units):
+            far = second[i][0]
+            both = [far, send(far, dc=1)]
+            whole[a] = placed(both, ((1, 1, 0), (1, 1, 1)), l, weights[a].shape, (whole[a],))
+        return (*whole, *new_m, *new_v)
 
     all_of, cut = P(None, None, None), P(None, "dp", None)
     return jax.shard_map(

time: 794 us -> 742 us (0.935)
  Pallas kernels: 334 us -> 453 us
  waiting for transfers between devices: 352 us -> 267 us
  local copies, waits for them, and re-layouts: 54.6 us -> 1.25 us
  other arithmetic: 38.6 us -> 0 us
  starting transfers between devices: 0.12 us -> 18.6 us
  between operations: 14.5 us -> 1.06 us
    all_gather x3 -> x0, waiting for transfers between devices: 352 us -> none  [step(): whole = [lax.all_gather(one[0], 'dp', axis=1, tiled=True) for one in new]]
    ppermute x0 -> x42, waiting for transfers between devices: none -> 267 us  [send(): return lax.ppermute(block, 'dp', [(d, d ^ flip) for d in range(8)])]
    pallas_call x0 -> x18, Pallas kernels: none -> 119 us  [the longest x12 64.9 us: placed(): pl.pallas_call(functools.partial(place_kernel, layer, offsets, len(before...]
    unnamed x7 -> x46, local copies, waits for them, and re-layouts: 53.4 us -> 1.25 us
    convert_element_type x3 -> x0, other arithmetic: 38.6 us -> none  [adamw(): return ((w - 0.02 * step).astype(BF16), m, v)]
    ppermute x0 -> x42, starting transfers between devices: none -> 18.6 us  [send(): return lax.ppermute(block, 'dp', [(d, d ^ flip) for d in range(8)])]
  transfers between devices with their start and end apart: 3 -> 42, of which waited for: 3 -> 18; matrix products, arithmetic and copies ran while one was open for 3% -> 0% of each run, Pallas kernels for 0% -> 14%
where the time goes in v2:
time: 742 us; the launch traced here: 741 us
  Pallas kernels  453 us (61%)
  waiting for transfers between devices  267 us (36%)
  starting transfers between devices  18.6 us (3%)
    pallas_call x1, Pallas kernels, summed(): pl.pallas_call(functools.partial(sum_kernel, shapes), out_shape=[jax.Shap...  334 us
    ppermute x42, waiting for transfers between devices, send(): return lax.ppermute(block, 'dp', [(d, d ^ flip) for d in range(8)])  267 us
    pallas_call x12, Pallas kernels, placed(): pl.pallas_call(functools.partial(place_kernel, layer, offsets, len(before...  64.9 us
    pallas_call x6, Pallas kernels, stepped(): pl.pallas_call(functools.partial(step_kernel, count), out_shape=[jax.Shap...  53.6 us
    ppermute x42, starting transfers between devices, send(): return lax.ppermute(block, 'dp', [(d, d ^ flip) for d in range(8)])  18.6 us
  transfers between devices with their start and end apart: 42, of which 18 were waited for; matrix products, arithmetic and copies ran while one was open for 0% of the time, Pallas kernels for 14%

profile of v2, /device:TPU:0, one launch (start us, length us, event | category | flops | bytes accessed | tf_op | source)
XLA Modules:
  0.0 741.3 jit_solution(17226063836725369809)
XLA Ops:
  0.6 334.4 %sum_terms.1 = (bf16[2,160,5120]{2,1,0:T(8,128)(2,1)}, bf16[2,160,5120]{2,1,0:T(8,128)(2,1)}, bf16[2,640,1280]{2,1,0:T(8,128)(2,1)}, f32[8,128]{1,0:T(8,128)}, b...) custom-call(bf16[1,2,1280,5120]{3,2,1,0:T(8,128)(2,1)} %refs_0_.1, ...), custom_call_target="tpu_custom_call" | custom-call | tf_op jit(solution)/shard_map/sum_terms/pallas_call | solution.py:193
  335.0 8.9 %adamw.10 = (bf16[640,1280]{1,0:T(8,128)(2,1)}, f32[2,640,1280]{2,1,0:T(8,128)}, f32[2,640,1280]{2,1,0:T(8,128)}) custom-call(s32[1]{0:T(128)} %bitcast.me, f32[8,128]{1,0:T(8,128)} %get-tuple-element.31.squares, bf16[2,640,1280]{2,1,0:T(8,128)(2,1)} %get-tuple-element.42.g, bf16[2,5120,1280]{2,1,0:T(8,128)(2,1)} %w.11, f32[2,640,1280]{2,1,0:T(8,128)} %m.11, ...), custom_call_target="tpu_custom_call" | custom-call | flops 12288000 | bytes 18022400 | tf_op jit(solution)/shard_map/adamw/pallas_call | solution.py:247
  344.0 1.3 collective-permute-start.31
  345.2 0.8 collective-permute-start.38
  346.0 8.9 %adamw.11 = (bf16[640,1280]{1,0:T(8,128)(2,1)}, f32[2,640,1280]{2,1,0:T(8,128)}, f32[2,640,1280]{2,1,0:T(8,128)}) custom-call(s32[1]{0:T(128)} %bitcast.me, f32[8,128]{1,0:T(8,128)} %get-tuple-element.31.squares, bf16[2,640,1280]{2,1,0:T(8,128)(2,1)} %get-tuple-element.42.g, ...), custom_call_target="tpu_custom_call", output_to_operand_aliasing={{1}: (6, {}), {2}: (7, {})} | custom-call | flops 12288000 | bytes 18022400 | tf_op jit(solution)/shard_map/adamw/pallas_call | solution.py:247
  354.9 1.3 collective-permute-start.28
  356.1 0.8 collective-permute-start.34
  356.9 9.0 %adamw.8 = (bf16[160,5120]{1,0:T(8,128)(2,1)}, f32[2,160,5120]{2,1,0:T(8,128)}, f32[2,160,5120]{2,1,0:T(8,128)}) custom-call(s32[1]{0:T(128)} %bitcast.me, f32[8,128]{1,0:T(8,128)} %get-tuple-element.31.squares, bf16[2,160,5120]{2,1,0:T(8,128)(2,1)} %get-tuple-element.37.g, bf16[2,1280,5120]{2,1,0:T(8,128)(2,1)} %w.9, f32[2,160,5120]{2,1,0:T(8,128)} %m.9, ...), custom_call_target="tpu_custom_call" | custom-call | flops 12288000 | bytes 18022400 | tf_op jit(solution)/shard_map/adamw/pallas_call | solution.py:247
  365.9 17.0 %collective-permute-done.31.refs_1_ = bf16[640,1280]{1,0:T(8,128)(2,1)} collective-permute-done((bf16[640,1280]{1,0:T(8,128)(2,1)}, bf16[640,1280]{1,0:T(8,128)(2,1)}, u32[]{:S(2)}, u32[]{:S(2)}) %collective-permute-start.31) | collective-permute-done | bytes 1638432 | tf_op jit(solution)/shard_map/ppermute | solution.py:297
  382.9 1.3 collective-permute-done.38.refs_2_
  384.2 0.8 collective-permute-start.17
  385.0 8.9 %adamw.9 = (bf16[160,5120]{1,0:T(8,128)(2,1)}, f32[2,160,5120]{2,1,0:T(8,128)}, f32[2,160,5120]{2,1,0:T(8,128)}) custom-call(s32[1]{0:T(128)} %bitcast.me, f32[8,128]{1,0:T(8,128)} %get-tuple-element.31.squares, bf16[2,160,5120]{2,1,0:T(8,128)(2,1)} %get-tuple-element.37.g, bf16[2,1280,5120]{2,1,0:T(8,128)(2,1)} %w.9, ...), custom_call_target="tpu_custom_call", output_to_operand_aliasing={{1}: (6, {}), {2}: (7, {})} | custom-call | flops 12288000 | bytes 18022400 | tf_op jit(solution)/shard_map/adamw/pallas_call | solution.py:247
  393.9 0.6 collective-permute-start.24
  394.5 24.7 %collective-permute-done.28.refs_2_ = bf16[640,1280]{1,0:T(8,128)(2,1)S(1)} collective-permute-done((bf16[640,1280]{1,0:T(8,128)(2,1)}, bf16[640,1280]{1,0:T(8,128)(2,1)S(1)}, u32[]{:S(2)}, u32[]{:S(2)}) %collective-permute-start.28) | collective-permute-done | bytes 1638432 | tf_op jit(solution)/shard_map/ppermute | solution.py:297
  419.2 0.8 collective-permute-start.14
  420.0 0.6 collective-permute-start.20
  420.6 32.6 %collective-permute-done.17.refs_1_ = bf16[160,5120]{1,0:T(8,128)(2,1)} collective-permute-done((bf16[160,5120]{1,0:T(8,128)(2,1)}, bf16[160,5120]{1,0:T(8,128)(2,1)}, u32[]{:S(2)}, u32[]{:S(2)}) %collective-permute-start.17) | collective-permute-done | bytes 1638432 | tf_op jit(solution)/shard_map/ppermute | solution.py:297
  453.2 8.9 %adamw.6 = (bf16[160,5120]{1,0:T(8,128)(2,1)}, f32[2,160,5120]{2,1,0:T(8,128)}, f32[2,160,5120]{2,1,0:T(8,128)}) custom-call(s32[1]{0:T(128)} %bitcast.me, f32[8,128]{1,0:T(8,128)} %get-tuple-element.31.squares, bf16[2,160,5120]{2,1,0:T(8,128)(2,1)} %get-tuple-element.32.g, bf16[2,1280,5120]{2,1,0:T(8,128)(2,1)} %w.7, f32[2,160,5120]{2,1,0:T(8,128)} %m.7, ...), custom_call_target="tpu_custom_call" | custom-call | flops 12288000 | bytes 18022400 | tf_op jit(solution)/shard_map/adamw/pallas_call | solution.py:247
  462.1 8.9 %adamw.7 = (bf16[160,5120]{1,0:T(8,128)(2,1)}, f32[2,160,5120]{2,1,0:T(8,128)}, f32[2,160,5120]{2,1,0:T(8,128)}) custom-call(s32[1]{0:T(128)} %bitcast.me, f32[8,128]{1,0:T(8,128)} %get-tuple-element.31.squares, bf16[2,160,5120]{2,1,0:T(8,128)(2,1)} %get-tuple-element.32.g, bf16[2,1280,5120]{2,1,0:T(8,128)(2,1)} %w.7, ...), custom_call_target="tpu_custom_call", output_to_operand_aliasing={{1}: (6, {}), {2}: (7, {})} | custom-call | flops 12288000 | bytes 18022400 | tf_op jit(solution)/shard_map/adamw/pallas_call | solution.py:247
  471.0 1.3 collective-permute-start.3
  472.3 0.8 collective-permute-start.10
  473.1 16.5 %collective-permute-done.14.refs_2_ = bf16[160,5120]{1,0:T(8,128)(2,1)} collective-permute-done((bf16[160,5120]{1,0:T(8,128)(2,1)}, bf16[160,5120]{1,0:T(8,128)(2,1)}, u32[]{:S(2)}, u32[]{:S(2)}) %collective-permute-start.14) | collective-permute-done | bytes 1638432 | tf_op jit(solution)/shard_map/ppermute | solution.py:297
  489.5 0.8 collective-permute-start
  490.3 0.6 collective-permute-start.6
  490.9 32.4 %collective-permute-done.3.refs_1_ = bf16[160,5120]{1,0:T(8,128)(2,1)S(1)} collective-permute-done((bf16[160,5120]{1,0:T(8,128)(2,1)}, bf16[160,5120]{1,0:T(8,128)(2,1)S(1)}, u32[]{:S(2)}, u32[]{:S(2)}) %collective-permute-start.3) | collective-permute-done | bytes 1638432 | tf_op jit(solution)/shard_map/ppermute | solution.py:297
  523.3 1.3 collective-permute-done.10.refs_2_
  524.6 0.5 collective-permute-start.41
  525.1 33.5 %collective-permute-done.refs_2_ = bf16[160,5120]{1,0:T(8,128)(2,1)S(1)} collective-permute-done((bf16[160,5120]{1,0:T(8,128)(2,1)}, bf16[160,5120]{1,0:T(8,128)(2,1)S(1)}, u32[]{:S(2)}, u32[]{:S(2)}) %collective-permute-start) | collective-permute-done | bytes 1638432 | tf_op jit(solution)/shard_map/ppermute | solution.py:297
  558.5 0.5 collective-permute-start.36
  559.0 0.8 collective-permute-start.32
  559.8 0.6 collective-permute-start.29
  560.4 1.6 collective-permute-done.37.refs_5_
  562.0 0.1 collective-permute-start.27
  562.2 2.2 collective-permute-done.36.refs_4_
  564.4 0.1 collective-permute-start.23
  564.5 32.5 %collective-permute-done.32.refs_0_ = bf16[640,1280]{1,0:T(8,128)(2,1)S(1)} collective-permute-done((bf16[640,1280]{1,0:T(8,128)(2,1)}, bf16[640,1280]{1,0:T(8,128)(2,1)S(1)}, u32[]{:S(2)}, u32[]{:S(2)}) %collective-permute-start.32) | collective-permute-done | bytes 1638432 | tf_op jit(solution)/shard_map/ppermute | solution.py:297
  597.0 0.4 collective-permute-done.29.refs_0_
  597.4 1.3 collective-permute-start.18
  598.7 0.8 collective-permute-start.15
  599.5 0.5 collective-permute-start.13
  599.9 0.6 collective-permute-done.22.refs_4_
  600.5 0.1 collective-permute-start.9
  600.6 34.9 %collective-permute-done.18.refs_0_ = bf16[160,5120]{1,0:T(8,128)(2,1)} collective-permute-done((bf16[160,5120]{1,0:T(8,128)(2,1)}, bf16[160,5120]{1,0:T(8,128)(2,1)}, u32[]{:S(2)}, u32[]{:S(2)}) %collective-permute-start.18) | collective-permute-done | bytes 1638432 | tf_op jit(solution)/shard_map/ppermute | solution.py:297
  635.5 0.5 collective-permute-done.15.refs_0_
  636.0 1.3 collective-permute-start.4
  637.3 0.8 collective-permute-start.1
  638.1 0.5 collective-permute-start.30
  638.6 0.4 collective-permute-done.8.refs_4_
  639.2 34.7 %collective-permute-done.4.refs_0_ = bf16[160,5120]{1,0:T(8,128)(2,1)} collective-permute-done((bf16[160,5120]{1,0:T(8,128)(2,1)S(1)}, bf16[160,5120]{1,0:T(8,128)(2,1)}, u32[]{:S(2)}, u32[]{:S(2)}) %collective-permute-start.4) | collective-permute-done | bytes 1638432 | tf_op jit(solution)/shard_map/ppermute | solution.py:297
  673.9 0.5 collective-permute-done.1.refs_0_
  674.5 1.2 copy-done.22
  675.7 0.5 collective-permute-start.2
  676.2 7.6 %place.20.refs_6_ = bf16[2,5120,1280]{2,1,0:T(8,128)(2,1)} custom-call(bf16[640,1280]{1,0:T(8,128)(2,1)} %get-tuple-element.46.refs_0_, bf16[640,1280]{1,0:T(8,128)(2,1)} %collective-permute-done.31.refs_1_, bf16[640,1280]{1,0:T(8,128)(2,1)} %collective-permute-done.38.refs_2_, bf16[640,1280]{1,0:T(8,128)(2,1)} %collective-permute-done.39.refs_3_, ...), custom_call_target="tpu_custom_call" | custom-call | bytes 19660800 | tf_op jit(solution)/shard_map/place/pallas_call | solution.py:283
  683.9 7.7 %place.16.refs_6_ = bf16[2,1280,5120]{2,1,0:T(8,128)(2,1)} custom-call(bf16[160,5120]{1,0:T(8,128)(2,1)} %get-tuple-element.41.refs_0_, bf16[160,5120]{1,0:T(8,128)(2,1)} %collective-permute-done.17.refs_1_, bf16[160,5120]{1,0:T(8,128)(2,1)} %collective-permute-done.24.refs_2_, bf16[160,5120]{1,0:T(8,128)(2,1)} %collective-permute-done.25.refs_3_, ...), custom_call_target="tpu_custom_call" | custom-call | bytes 19660800 | tf_op jit(solution)/shard_map/place/pallas_call | solution.py:283
  691.5 7.7 %place.12.refs_6_ = bf16[2,1280,5120]{2,1,0:T(8,128)(2,1)} custom-call(bf16[160,5120]{1,0:T(8,128)(2,1)} %get-tuple-element.36.refs_0_, bf16[160,5120]{1,0:T(8,128)(2,1)} %copy-done.4, bf16[160,5120]{1,0:T(8,128)(2,1)} %copy-done.6, bf16[160,5120]{1,0:T(8,128)(2,1)} %copy-done.8, bf16[160,5120]{1,0:T(8,128)(2,1)} %copy-done.19, bf16[160,5120]{1,0:T(8,128)(2,1)} %copy-done.20), custom_call_target="tpu_custom_call" | custom-call | bytes 19660800 | tf_op jit(solution)/shard_map/place/pallas_call | solution.py:283
  699.2 7.7 %place.21.refs_2_ = bf16[2,5120,1280]{2,1,0:T(8,128)(2,1)} custom-call(bf16[640,1280]{1,0:T(8,128)(2,1)} %get-tuple-element.45.refs_0_, bf16[640,1280]{1,0:T(8,128)(2,1)} %collective-permute-done.34.refs_1_, bf16[640,1280]{1,0:T(8,128)(2,1)} %copy-done.1, bf16[640,1280]{1,0:T(8,128)(2,1)} %collective-permute-done.35.refs_3_, ...), custom_call_target="tpu_custom_call", output_to_operand_aliasing={{}: (6, {})} | custom-call | bytes 19660800 | tf_op jit(solution)/shard_map/place/pallas_call | solution.py:283
  706.9 7.7 %place.17.refs_2_ = bf16[2,1280,5120]{2,1,0:T(8,128)(2,1)} custom-call(bf16[160,5120]{1,0:T(8,128)(2,1)} %get-tuple-element.40.refs_0_, bf16[160,5120]{1,0:T(8,128)(2,1)} %copy-done.2, bf16[160,5120]{1,0:T(8,128)(2,1)} %collective-permute-done.14.refs_2_, bf16[160,5120]{1,0:T(8,128)(2,1)} %collective-permute-done.21.refs_3_, ...), custom_call_target="tpu_custom_call", output_to_operand_aliasing={{}: (6, {})} | custom-call | bytes 19660800 | tf_op jit(solution)/shard_map/place/pallas_call | solution.py:283
  714.5 7.7 %place.13.refs_2_ = bf16[2,1280,5120]{2,1,0:T(8,128)(2,1)} custom-call(bf16[160,5120]{1,0:T(8,128)(2,1)} %get-tuple-element.35.refs_0_, bf16[160,5120]{1,0:T(8,128)(2,1)} %copy-done.5, bf16[160,5120]{1,0:T(8,128)(2,1)} %copy-done.3, bf16[160,5120]{1,0:T(8,128)(2,1)} %copy-done.7, bf16[160,5120]{1,0:T(8,128)(2,1)} %copy-done.18, ...), custom_call_target="tpu_custom_call", output_to_operand_aliasing={{}: (6, {})} | custom-call | bytes 19660800 | tf_op jit(solution)/shard_map/place/pallas_call | solution.py:283
  722.2 3.2 place.22.refs_2_
  725.4 3.2 place.23
  728.6 3.2 place.18.refs_2_
  731.8 3.2 place.19
  734.9 3.2 place.14.refs_2_
  738.1 3.2 place.15
  (85 shorter events, 0.3 us)
Async XLA Ops:
  344.0 39.0 %collective-permute-start.31 = (bf16[640,1280]{1,0:T(8,128)(2,1)}, bf16[640,1280]{1,0:T(8,128)(2,1)}, u32[]{:S(2)}, u32[]{:S(2)}) collective-permute-start(bf16[640,1280]{1,0:T(8,128)(2,1)} %get-tuple-element.46.refs_0_), channel_id=1, source_target_pairs={{0,4},{1,5},{2,6},{3,7},{4,0},{5,1},{6,2},{7,3}} | collective-permute-start | bytes 4915208 | tf_op jit(solution)/shard_map/ppermute | solution.py:297
  345.2 39.0 %collective-permute-start.38 = (bf16[640,1280]{1,0:T(8,128)(2,1)}, bf16[640,1280]{1,0:T(8,128)(2,1)}, u32[]{:S(2)}, u32[]{:S(2)}) collective-permute-start(bf16[640,1280]{1,0:T(8,128)(2,1)} %get-tuple-element.46.refs_0_), channel_id=1, source_target_pairs={{0,2},{1,3},{2,0},{3,1},{4,6},{5,7},{6,4},{7,5}} | collective-permute-start | bytes 4915208 | tf_op jit(solution)/shard_map/ppermute | solution.py:297
  346.0 47.9 %collective-permute-start.39 = (bf16[640,1280]{1,0:T(8,128)(2,1)}, bf16[640,1280]{1,0:T(8,128)(2,1)}, u32[]{:S(2)}, u32[]{:S(2)}) collective-permute-start(bf16[640,1280]{1,0:T(8,128)(2,1)} %get-tuple-element.46.refs_0_), channel_id=1, source_target_pairs={{0,1},{1,0},{2,3},{3,2},{4,5},{5,4},{6,7},{7,6}} | collective-permute-start | bytes 4915208 | tf_op jit(solution)/shard_map/ppermute | solution.py:297
  354.9 64.3 %collective-permute-start.28 = (bf16[640,1280]{1,0:T(8,128)(2,1)}, bf16[640,1280]{1,0:T(8,128)(2,1)S(1)}, u32[]{:S(2)}, u32[]{:S(2)}) collective-permute-start(bf16[640,1280]{1,0:T(8,128)(2,1)} %get-tuple-element.45.refs_0_), channel_id=1, source_target_pairs={{0,2},{1,3},{2,0},{3,1},{4,6},{5,7},{6,4},{7,5}} | collective-permute-start | bytes 4915208 | tf_op jit(solution)/shard_map/ppermute | solution.py:297
  356.1 63.1 %collective-permute-start.34 = (bf16[640,1280]{1,0:T(8,128)(2,1)}, bf16[640,1280]{1,0:T(8,128)(2,1)}, u32[]{:S(2)}, u32[]{:S(2)}) collective-permute-start(bf16[640,1280]{1,0:T(8,128)(2,1)} %get-tuple-element.45.refs_0_), channel_id=1, source_target_pairs={{0,4},{1,5},{2,6},{3,7},{4,0},{5,1},{6,2},{7,3}} | collective-permute-start | bytes 4915208 | tf_op jit(solution)/shard_map/ppermute | solution.py:297
  356.9 26.0 %copy-start = (bf16[640,1280]{1,0:T(8,128)(2,1)S(1)}, bf16[640,1280]{1,0:T(8,128)(2,1)}, u32[]{:S(2)}) copy-start(bf16[640,1280]{1,0:T(8,128)(2,1)} %get-tuple-element.45.refs_0_) | copy-start | bytes 4915204
  382.9 37.1 %collective-permute-start.35 = (bf16[640,1280]{1,0:T(8,128)(2,1)S(1)}, bf16[640,1280]{1,0:T(8,128)(2,1)}, u32[]{:S(2)}, u32[]{:S(2)}) collective-permute-start(bf16[640,1280]{1,0:T(8,128)(2,1)S(1)} %copy-done), channel_id=1, source_target_pairs={{0,1},{1,0},{2,3},{3,2},{4,5},{5,4},{6,7},{7,6}} | collective-permute-start | bytes 4915208 | tf_op jit(solution)/shard_map/ppermute | solution.py:297
  384.2 69.0 %collective-permute-start.17 = (bf16[160,5120]{1,0:T(8,128)(2,1)}, bf16[160,5120]{1,0:T(8,128)(2,1)}, u32[]{:S(2)}, u32[]{:S(2)}) collective-permute-start(bf16[160,5120]{1,0:T(8,128)(2,1)} %get-tuple-element.41.refs_0_), channel_id=1, source_target_pairs={{0,4},{1,5},{2,6},{3,7},{4,0},{5,1},{6,2},{7,3}} | collective-permute-start | bytes 4915208 | tf_op jit(solution)/shard_map/ppermute | solution.py:297
  393.9 77.1 %collective-permute-start.24 = (bf16[160,5120]{1,0:T(8,128)(2,1)}, bf16[160,5120]{1,0:T(8,128)(2,1)}, u32[]{:S(2)}, u32[]{:S(2)}) collective-permute-start(bf16[160,5120]{1,0:T(8,128)(2,1)} %get-tuple-element.41.refs_0_), channel_id=1, source_target_pairs={{0,2},{1,3},{2,0},{3,1},{4,6},{5,7},{6,4},{7,5}} | collective-permute-start | bytes 4915208 | tf_op jit(solution)/shard_map/ppermute | solution.py:297
  419.2 140.6 %copy-start.1 = (bf16[640,1280]{1,0:T(8,128)(2,1)}, bf16[640,1280]{1,0:T(8,128)(2,1)S(1)}, u32[]{:S(2)}) copy-start(bf16[640,1280]{1,0:T(8,128)(2,1)S(1)} %collective-permute-done.28.refs_2_) | copy-start | bytes 4915204
  419.2 53.1 %collective-permute-start.25 = (bf16[160,5120]{1,0:T(8,128)(2,1)}, bf16[160,5120]{1,0:T(8,128)(2,1)}, u32[]{:S(2)}, u32[]{:S(2)}) collective-permute-start(bf16[160,5120]{1,0:T(8,128)(2,1)} %get-tuple-element.41.refs_0_), channel_id=1, source_target_pairs={{0,1},{1,0},{2,3},{3,2},{4,5},{5,4},{6,7},{7,6}} | collective-permute-start | bytes 4915208 | tf_op jit(solution)/shard_map/ppermute | solution.py:297
  419.2 70.3 %collective-permute-start.14 = (bf16[160,5120]{1,0:T(8,128)(2,1)}, bf16[160,5120]{1,0:T(8,128)(2,1)}, u32[]{:S(2)}, u32[]{:S(2)}) collective-permute-start(bf16[160,5120]{1,0:T(8,128)(2,1)} %get-tuple-element.40.refs_0_), channel_id=1, source_target_pairs={{0,2},{1,3},{2,0},{3,1},{4,6},{5,7},{6,4},{7,5}} | collective-permute-start | bytes 4915208 | tf_op jit(solution)/shard_map/ppermute | solution.py:297
  420.0 69.5 %collective-permute-start.20 = (bf16[160,5120]{1,0:T(8,128)(2,1)}, bf16[160,5120]{1,0:T(8,128)(2,1)S(1)}, u32[]{:S(2)}, u32[]{:S(2)}) collective-permute-start(bf16[160,5120]{1,0:T(8,128)(2,1)} %get-tuple-element.40.refs_0_), channel_id=1, source_target_pairs={{0,4},{1,5},{2,6},{3,7},{4,0},{5,1},{6,2},{7,3}} | collective-permute-start | bytes 4915208 | tf_op jit(solution)/shard_map/ppermute | solution.py:297
  453.2 37.2 %collective-permute-start.21 = (bf16[160,5120]{1,0:T(8,128)(2,1)}, bf16[160,5120]{1,0:T(8,128)(2,1)}, u32[]{:S(2)}, u32[]{:S(2)}) collective-permute-start(bf16[160,5120]{1,0:T(8,128)(2,1)} %get-tuple-element.40.refs_0_), channel_id=1, source_target_pairs={{0,1},{1,0},{2,3},{3,2},{4,5},{5,4},{6,7},{7,6}} | collective-permute-start | bytes 4915208 | tf_op jit(solution)/shard_map/ppermute | solution.py:297
  471.0 52.3 %collective-permute-start.3 = (bf16[160,5120]{1,0:T(8,128)(2,1)}, bf16[160,5120]{1,0:T(8,128)(2,1)S(1)}, u32[]{:S(2)}, u32[]{:S(2)}) collective-permute-start(bf16[160,5120]{1,0:T(8,128)(2,1)} %get-tuple-element.36.refs_0_), channel_id=1, source_target_pairs={{0,4},{1,5},{2,6},{3,7},{4,0},{5,1},{6,2},{7,3}} | collective-permute-start | bytes 4915208 | tf_op jit(solution)/shard_map/ppermute | solution.py:297
  472.3 52.2 %collective-permute-start.10 = (bf16[160,5120]{1,0:T(8,128)(2,1)}, bf16[160,5120]{1,0:T(8,128)(2,1)S(1)}, u32[]{:S(2)}, u32[]{:S(2)}) collective-permute-start(bf16[160,5120]{1,0:T(8,128)(2,1)} %get-tuple-element.36.refs_0_), channel_id=1, source_target_pairs={{0,2},{1,3},{2,0},{3,1},{4,6},{5,7},{6,4},{7,5}} | collective-permute-start | bytes 4915208 | tf_op jit(solution)/shard_map/ppermute | solution.py:297
  489.5 35.0 %collective-permute-start.11 = (bf16[160,5120]{1,0:T(8,128)(2,1)}, bf16[160,5120]{1,0:T(8,128)(2,1)S(1)}, u32[]{:S(2)}, u32[]{:S(2)}) collective-permute-start(bf16[160,5120]{1,0:T(8,128)(2,1)} %get-tuple-element.36.refs_0_), channel_id=1, source_target_pairs={{0,1},{1,0},{2,3},{3,2},{4,5},{5,4},{6,7},{7,6}} | collective-permute-start | bytes 4915208 | tf_op jit(solution)/shard_map/ppermute | solution.py:297
  489.5 194.3 %copy-start.2 = (bf16[160,5120]{1,0:T(8,128)(2,1)}, bf16[160,5120]{1,0:T(8,128)(2,1)S(1)}, u32[]{:S(2)}) copy-start(bf16[160,5120]{1,0:T(8,128)(2,1)S(1)} %collective-permute-done.20.refs_1_) | copy-start | bytes 4915204
  489.5 69.0 %collective-permute-start = (bf16[160,5120]{1,0:T(8,128)(2,1)}, bf16[160,5120]{1,0:T(8,128)(2,1)S(1)}, u32[]{:S(2)}, u32[]{:S(2)}) collective-permute-start(bf16[160,5120]{1,0:T(8,128)(2,1)} %get-tuple-element.35.refs_0_), channel_id=1, source_target_pairs={{0,2},{1,3},{2,0},{3,1},{4,6},{5,7},{6,4},{7,5}} | collective-permute-start | bytes 4915208 | tf_op jit(solution)/shard_map/ppermute | solution.py:297
  490.3 68.2 %collective-permute-start.6 = (bf16[160,5120]{1,0:T(8,128)(2,1)}, bf16[160,5120]{1,0:T(8,128)(2,1)S(1)}, u32[]{:S(2)}, u32[]{:S(2)}) collective-permute-start(bf16[160,5120]{1,0:T(8,128)(2,1)} %get-tuple-element.35.refs_0_), channel_id=1, source_target_pairs={{0,4},{1,5},{2,6},{3,7},{4,0},{5,1},{6,2},{7,3}} | collective-permute-start | bytes 4915208 | tf_op jit(solution)/shard_map/ppermute | solution.py:297
  523.3 151.1 %copy-start.4 = (bf16[160,5120]{1,0:T(8,128)(2,1)}, bf16[160,5120]{1,0:T(8,128)(2,1)S(1)}, u32[]{:S(2)}) copy-start(bf16[160,5120]{1,0:T(8,128)(2,1)S(1)} %collective-permute-done.3.refs_1_) | copy-start | bytes 4915204
  523.3 35.8 %collective-permute-start.7 = (bf16[160,5120]{1,0:T(8,128)(2,1)}, bf16[160,5120]{1,0:T(8,128)(2,1)S(1)}, u32[]{:S(2)}, u32[]{:S(2)}) collective-permute-start(bf16[160,5120]{1,0:T(8,128)(2,1)} %get-tuple-element.35.refs_0_), channel_id=1, source_target_pairs={{0,1},{1,0},{2,3},{3,2},{4,5},{5,4},{6,7},{7,6}} | collective-permute-start | bytes 4915208 | tf_op jit(solution)/shard_map/ppermute | solution.py:297
  524.5 149.8 %copy-start.6 = (bf16[160,5120]{1,0:T(8,128)(2,1)}, bf16[160,5120]{1,0:T(8,128)(2,1)S(1)}, u32[]{:S(2)}) copy-start(bf16[160,5120]{1,0:T(8,128)(2,1)S(1)} %collective-permute-done.10.refs_2_) | copy-start | bytes 4915204
  524.5 35.3 %collective-permute-start.40 = (bf16[640,1280]{1,0:T(8,128)(2,1)}, bf16[640,1280]{1,0:T(8,128)(2,1)S(1)}, u32[]{:S(2)}, u32[]{:S(2)}) collective-permute-start(bf16[640,1280]{1,0:T(8,128)(2,1)} %collective-permute-done.31.refs_1_), channel_id=1, source_target_pairs={{0,1},{1,0},{2,3},{3,2},{4,5},{5,4},{6,7},{7,6}} | collective-permute-start | bytes 4915208 | tf_op jit(solution)/shard_map/ppermute | solution.py:297
  524.5 149.8 %copy-start.8 = (bf16[160,5120]{1,0:T(8,128)(2,1)}, bf16[160,5120]{1,0:T(8,128)(2,1)S(1)}, u32[]{:S(2)}) copy-start(bf16[160,5120]{1,0:T(8,128)(2,1)S(1)} %collective-permute-done.11.refs_3_) | copy-start | bytes 4915204
  524.6 35.8 %collective-permute-start.41 = (bf16[640,1280]{1,0:T(8,128)(2,1)}, bf16[640,1280]{1,0:T(8,128)(2,1)S(1)}, u32[]{:S(2)}, u32[]{:S(2)}) collective-permute-start(bf16[640,1280]{1,0:T(8,128)(2,1)} %collective-permute-done.38.refs_2_), channel_id=1, source_target_pairs={{0,1},{1,0},{2,3},{3,2},{4,5},{5,4},{6,7},{7,6}} | collective-permute-start | bytes 4915208 | tf_op jit(solution)/shard_map/ppermute | solution.py:297
  558.5 78.8 %copy-start.3 = (bf16[160,5120]{1,0:T(8,128)(2,1)}, bf16[160,5120]{1,0:T(8,128)(2,1)S(1)}, u32[]{:S(2)}) copy-start(bf16[160,5120]{1,0:T(8,128)(2,1)S(1)} %collective-permute-done.refs_2_) | copy-start | bytes 4915204
  558.5 3.5 collective-permute-start.37
  558.5 115.8 %copy-start.5 = (bf16[160,5120]{1,0:T(8,128)(2,1)}, bf16[160,5120]{1,0:T(8,128)(2,1)S(1)}, u32[]{:S(2)}) copy-start(bf16[160,5120]{1,0:T(8,128)(2,1)S(1)} %collective-permute-done.6.refs_1_) | copy-start | bytes 4915204
  558.5 5.8 collective-permute-start.36
  559.0 115.4 %copy-start.7 = (bf16[160,5120]{1,0:T(8,128)(2,1)}, bf16[160,5120]{1,0:T(8,128)(2,1)S(1)}, u32[]{:S(2)}) copy-start(bf16[160,5120]{1,0:T(8,128)(2,1)S(1)} %collective-permute-done.7.refs_3_) | copy-start | bytes 4915204
  559.0 38.0 %collective-permute-start.32 = (bf16[640,1280]{1,0:T(8,128)(2,1)}, bf16[640,1280]{1,0:T(8,128)(2,1)S(1)}, u32[]{:S(2)}, u32[]{:S(2)}) collective-permute-start(bf16[640,1280]{1,0:T(8,128)(2,1)} %collective-permute-done.31.refs_1_), channel_id=1, source_target_pairs={{0,2},{1,3},{2,0},{3,1},{4,6},{5,7},{6,4},{7,5}} | collective-permute-start | bytes 4915208 | tf_op jit(solution)/shard_map/ppermute | solution.py:297
  559.8 114.6 %copy-start.11 = (bf16[640,1280]{1,0:T(8,128)(2,1)}, bf16[640,1280]{1,0:T(8,128)(2,1)S(1)}, u32[]{:S(2)}) copy-start(bf16[640,1280]{1,0:T(8,128)(2,1)S(1)} %collective-permute-done.40.refs_4_) | copy-start | bytes 4915204
  559.8 37.6 %collective-permute-start.29 = (bf16[640,1280]{1,0:T(8,128)(2,1)S(1)}, bf16[640,1280]{1,0:T(8,128)(2,1)}, u32[]{:S(2)}, u32[]{:S(2)}) collective-permute-start(bf16[640,1280]{1,0:T(8,128)(2,1)S(1)} %collective-permute-done.28.refs_2_), channel_id=1, source_target_pairs={{0,4},{1,5},{2,6},{3,7},{4,0},{5,1},{6,2},{7,3}} | collective-permute-start | bytes 4915208 | tf_op jit(solution)/shard_map/ppermute | solution.py:297
  560.4 114.0 %copy-start.12 = (bf16[640,1280]{1,0:T(8,128)(2,1)}, bf16[640,1280]{1,0:T(8,128)(2,1)S(1)}, u32[]{:S(2)}) copy-start(bf16[640,1280]{1,0:T(8,128)(2,1)S(1)} %collective-permute-done.41.refs_5_) | copy-start | bytes 4915204
  560.4 38.3 %collective-permute-start.26 = (bf16[160,5120]{1,0:T(8,128)(2,1)}, bf16[160,5120]{1,0:T(8,128)(2,1)S(1)}, u32[]{:S(2)}, u32[]{:S(2)}) collective-permute-start(bf16[160,5120]{1,0:T(8,128)(2,1)} %collective-permute-done.17.refs_1_), channel_id=1, source_target_pairs={{0,1},{1,0},{2,3},{3,2},{4,5},{5,4},{6,7},{7,6}} | collective-permute-start | bytes 4915208 | tf_op jit(solution)/shard_map/ppermute | solution.py:297
  562.0 112.4 %copy-start.9 = (bf16[640,1280]{1,0:T(8,128)(2,1)}, bf16[640,1280]{1,0:T(8,128)(2,1)S(1)}, u32[]{:S(2)}) copy-start(bf16[640,1280]{1,0:T(8,128)(2,1)S(1)} %collective-permute-done.37.refs_5_) | copy-start | bytes 4915204
  562.0 37.4 %collective-permute-start.27 = (bf16[160,5120]{1,0:T(8,128)(2,1)}, bf16[160,5120]{1,0:T(8,128)(2,1)S(1)}, u32[]{:S(2)}, u32[]{:S(2)}) collective-permute-start(bf16[160,5120]{1,0:T(8,128)(2,1)} %collective-permute-done.24.refs_2_), channel_id=1, source_target_pairs={{0,1},{1,0},{2,3},{3,2},{4,5},{5,4},{6,7},{7,6}} | collective-permute-start | bytes 4915208 | tf_op jit(solution)/shard_map/ppermute | solution.py:297
  564.4 110.1 %copy-start.10 = (bf16[640,1280]{1,0:T(8,128)(2,1)}, bf16[640,1280]{1,0:T(8,128)(2,1)S(1)}, u32[]{:S(2)}) copy-start(bf16[640,1280]{1,0:T(8,128)(2,1)S(1)} %collective-permute-done.36.refs_4_) | copy-start | bytes 4915204
  564.4 35.1 %collective-permute-start.23 = (bf16[160,5120]{1,0:T(8,128)(2,1)}, bf16[160,5120]{1,0:T(8,128)(2,1)S(1)}, u32[]{:S(2)}, u32[]{:S(2)}) collective-permute-start(bf16[160,5120]{1,0:T(8,128)(2,1)} %collective-permute-done.14.refs_2_), channel_id=1, source_target_pairs={{0,1},{1,0},{2,3},{3,2},{4,5},{5,4},{6,7},{7,6}} | collective-permute-start | bytes 4915208 | tf_op jit(solution)/shard_map/ppermute | solution.py:297
  597.0 77.5 %copy-start.21 = (bf16[640,1280]{1,0:T(8,128)(2,1)}, bf16[640,1280]{1,0:T(8,128)(2,1)S(1)}, u32[]{:S(2)}) copy-start(bf16[640,1280]{1,0:T(8,128)(2,1)S(1)} %collective-permute-done.32.refs_0_) | copy-start | bytes 4915204
  597.0 3.5 collective-permute-start.22
  597.4 38.1 %collective-permute-start.18 = (bf16[160,5120]{1,0:T(8,128)(2,1)}, bf16[160,5120]{1,0:T(8,128)(2,1)}, u32[]{:S(2)}, u32[]{:S(2)}) collective-permute-start(bf16[160,5120]{1,0:T(8,128)(2,1)} %collective-permute-done.17.refs_1_), channel_id=1, source_target_pairs={{0,2},{1,3},{2,0},{3,1},{4,6},{5,7},{6,4},{7,5}} | collective-permute-start | bytes 4915208 | tf_op jit(solution)/shard_map/ppermute | solution.py:297
  598.7 75.8 %copy-start.15 = (bf16[160,5120]{1,0:T(8,128)(2,1)}, bf16[160,5120]{1,0:T(8,128)(2,1)S(1)}, u32[]{:S(2)}) copy-start(bf16[160,5120]{1,0:T(8,128)(2,1)S(1)} %collective-permute-done.26.refs_4_) | copy-start | bytes 4915204
  598.7 37.4 %collective-permute-start.15 = (bf16[160,5120]{1,0:T(8,128)(2,1)}, bf16[160,5120]{1,0:T(8,128)(2,1)}, u32[]{:S(2)}, u32[]{:S(2)}) collective-permute-start(bf16[160,5120]{1,0:T(8,128)(2,1)} %collective-permute-done.14.refs_2_), channel_id=1, source_target_pairs={{0,4},{1,5},{2,6},{3,7},{4,0},{5,1},{6,2},{7,3}} | collective-permute-start | bytes 4915208 | tf_op jit(solution)/shard_map/ppermute | solution.py:297
  599.4 75.0 %copy-start.16 = (bf16[160,5120]{1,0:T(8,128)(2,1)}, bf16[160,5120]{1,0:T(8,128)(2,1)S(1)}, u32[]{:S(2)}) copy-start(bf16[160,5120]{1,0:T(8,128)(2,1)S(1)} %collective-permute-done.27.refs_5_) | copy-start | bytes 4915204
  599.4 37.9 %collective-permute-start.12 = (bf16[160,5120]{1,0:T(8,128)(2,1)S(1)}, bf16[160,5120]{1,0:T(8,128)(2,1)S(1)}, u32[]{:S(2)}, u32[]{:S(2)}) collective-permute-start(bf16[160,5120]{1,0:T(8,128)(2,1)S(1)} %collective-permute-done.3.refs_1_), channel_id=1, source_target_pairs={{0,1},{1,0},{2,3},{3,2},{4,5},{5,4},{6,7},{7,6}} | collective-permute-start | bytes 4915208 | tf_op jit(solution)/shard_map/ppermute | solution.py:297
  599.4 75.0 %copy-start.13 = (bf16[160,5120]{1,0:T(8,128)(2,1)}, bf16[160,5120]{1,0:T(8,128)(2,1)S(1)}, u32[]{:S(2)}) copy-start(bf16[160,5120]{1,0:T(8,128)(2,1)S(1)} %collective-permute-done.23.refs_5_) | copy-start | bytes 4915204
  599.5 38.6 %collective-permute-start.13 = (bf16[160,5120]{1,0:T(8,128)(2,1)S(1)}, bf16[160,5120]{1,0:T(8,128)(2,1)S(1)}, u32[]{:S(2)}, u32[]{:S(2)}) collective-permute-start(bf16[160,5120]{1,0:T(8,128)(2,1)S(1)} %collective-permute-done.10.refs_2_), channel_id=1, source_target_pairs={{0,1},{1,0},{2,3},{3,2},{4,5},{5,4},{6,7},{7,6}} | collective-permute-start | bytes 4915208 | tf_op jit(solution)/shard_map/ppermute | solution.py:297
  600.5 74.0 %copy-start.14 = (bf16[160,5120]{1,0:T(8,128)(2,1)}, bf16[160,5120]{1,0:T(8,128)(2,1)S(1)}, u32[]{:S(2)}) copy-start(bf16[160,5120]{1,0:T(8,128)(2,1)S(1)} %collective-permute-done.22.refs_4_) | copy-start | bytes 4915204
  600.5 37.6 %collective-permute-start.9 = (bf16[160,5120]{1,0:T(8,128)(2,1)S(1)}, bf16[160,5120]{1,0:T(8,128)(2,1)S(1)}, u32[]{:S(2)}, u32[]{:S(2)}) collective-permute-start(bf16[160,5120]{1,0:T(8,128)(2,1)S(1)} %collective-permute-done.refs_2_), channel_id=1, source_target_pairs={{0,1},{1,0},{2,3},{3,2},{4,5},{5,4},{6,7},{7,6}} | collective-permute-start | bytes 4915208 | tf_op jit(solution)/shard_map/ppermute | solution.py:297
  635.5 3.5 collective-permute-start.8
  636.0 37.8 %collective-permute-start.4 = (bf16[160,5120]{1,0:T(8,128)(2,1)S(1)}, bf16[160,5120]{1,0:T(8,128)(2,1)}, u32[]{:S(2)}, u32[]{:S(2)}) collective-permute-start(bf16[160,5120]{1,0:T(8,128)(2,1)S(1)} %collective-permute-done.3.refs_1_), channel_id=1, source_target_pairs={{0,2},{1,3},{2,0},{3,1},{4,6},{5,7},{6,4},{7,5}} | collective-permute-start | bytes 4915208 | tf_op jit(solution)/shard_map/ppermute | solution.py:297
  637.3 37.2 %copy-start.19 = (bf16[160,5120]{1,0:T(8,128)(2,1)}, bf16[160,5120]{1,0:T(8,128)(2,1)S(1)}, u32[]{:S(2)}) copy-start(bf16[160,5120]{1,0:T(8,128)(2,1)S(1)} %collective-permute-done.12.refs_4_) | copy-start | bytes 4915204
  637.3 37.1 %collective-permute-start.1 = (bf16[160,5120]{1,0:T(8,128)(2,1)S(1)}, bf16[160,5120]{1,0:T(8,128)(2,1)}, u32[]{:S(2)}, u32[]{:S(2)}) collective-permute-start(bf16[160,5120]{1,0:T(8,128)(2,1)S(1)} %collective-permute-done.refs_2_), channel_id=1, source_target_pairs={{0,4},{1,5},{2,6},{3,7},{4,0},{5,1},{6,2},{7,3}} | collective-permute-start | bytes 4915208 | tf_op jit(solution)/shard_map/ppermute | solution.py:297
  638.1 36.4 %copy-start.20 = (bf16[160,5120]{1,0:T(8,128)(2,1)}, bf16[160,5120]{1,0:T(8,128)(2,1)S(1)}, u32[]{:S(2)}) copy-start(bf16[160,5120]{1,0:T(8,128)(2,1)S(1)} %collective-permute-done.13.refs_5_) | copy-start | bytes 4915204
  638.1 36.3 %collective-permute-start.33 = (bf16[640,1280]{1,0:T(8,128)(2,1)S(1)}, bf16[640,1280]{1,0:T(8,128)(2,1)S(1)}, u32[]{:S(2)}, u32[]{:S(2)}) collective-permute-start(bf16[640,1280]{1,0:T(8,128)(2,1)S(1)} %collective-permute-done.32.refs_0_), channel_id=1, source_target_pairs={{0,1},{1,0},{2,3},{3,2},{4,5},{5,4},{6,7},{7,6}} | collective-permute-start | bytes 4915208 | tf_op jit(solution)/shard_map/ppermute | solution.py:297
  638.1 45.8 %copy-start.17 = (bf16[160,5120]{1,0:T(8,128)(2,1)}, bf16[160,5120]{1,0:T(8,128)(2,1)S(1)}, u32[]{:S(2)}) copy-start(bf16[160,5120]{1,0:T(8,128)(2,1)S(1)} %collective-permute-done.9.refs_5_) | copy-start | bytes 4915204
  638.1 87.3 %collective-permute-start.30 = (bf16[640,1280]{1,0:T(8,128)(2,1)}, bf16[640,1280]{1,0:T(8,128)(2,1)}, u32[]{:S(2)}, u32[]{:S(2)}) collective-permute-start(bf16[640,1280]{1,0:T(8,128)(2,1)} %collective-permute-done.29.refs_0_), channel_id=1, source_target_pairs={{0,1},{1,0},{2,3},{3,2},{4,5},{5,4},{6,7},{7,6}} | collective-permute-start | bytes 4915208 | tf_op jit(solution)/shard_map/ppermute | solution.py:297
  639.0 35.5 %copy-start.18 = (bf16[160,5120]{1,0:T(8,128)(2,1)}, bf16[160,5120]{1,0:T(8,128)(2,1)S(1)}, u32[]{:S(2)}) copy-start(bf16[160,5120]{1,0:T(8,128)(2,1)S(1)} %collective-permute-done.8.refs_4_) | copy-start | bytes 4915204
  639.0 89.5 %collective-permute-start.19 = (bf16[160,5120]{1,0:T(8,128)(2,1)}, bf16[160,5120]{1,0:T(8,128)(2,1)}, u32[]{:S(2)}, u32[]{:S(2)}) collective-permute-start(bf16[160,5120]{1,0:T(8,128)(2,1)} %collective-permute-done.18.refs_0_), channel_id=1, source_target_pairs={{0,1},{1,0},{2,3},{3,2},{4,5},{5,4},{6,7},{7,6}} | collective-permute-start | bytes 4915208 | tf_op jit(solution)/shard_map/ppermute | solution.py:297
  673.9 57.9 %collective-permute-start.16 = (bf16[160,5120]{1,0:T(8,128)(2,1)}, bf16[160,5120]{1,0:T(8,128)(2,1)}, u32[]{:S(2)}, u32[]{:S(2)}) collective-permute-start(bf16[160,5120]{1,0:T(8,128)(2,1)} %collective-permute-done.15.refs_0_), channel_id=1, source_target_pairs={{0,1},{1,0},{2,3},{3,2},{4,5},{5,4},{6,7},{7,6}} | collective-permute-start | bytes 4915208 | tf_op jit(solution)/shard_map/ppermute | solution.py:297
  674.4 60.6 %collective-permute-start.5 = (bf16[160,5120]{1,0:T(8,128)(2,1)}, bf16[160,5120]{1,0:T(8,128)(2,1)}, u32[]{:S(2)}, u32[]{:S(2)}) collective-permute-start(bf16[160,5120]{1,0:T(8,128)(2,1)} %collective-permute-done.4.refs_0_), channel_id=1, source_target_pairs={{0,1},{1,0},{2,3},{3,2},{4,5},{5,4},{6,7},{7,6}} | collective-permute-start | bytes 4915208 | tf_op jit(solution)/shard_map/ppermute | solution.py:297
  675.7 62.4 %collective-permute-start.2 = (bf16[160,5120]{1,0:T(8,128)(2,1)}, bf16[160,5120]{1,0:T(8,128)(2,1)}, u32[]{:S(2)}, u32[]{:S(2)}) collective-permute-start(bf16[160,5120]{1,0:T(8,128)(2,1)} %collective-permute-done.1.refs_0_), channel_id=1, source_target_pairs={{0,1},{1,0},{2,3},{3,2},{4,5},{5,4},{6,7},{7,6}} | collective-permute-start | bytes 4915208 | tf_op jit(solution)/shard_map/ppermute | solution.py:297
  (1 other events, 1.2 us)

commit v3 on v2

--- a/solution.py
+++ b/solution.py
@@ -219,37 +219,43 @@
     return outs[:3], outs[3]
 
 
-def step_kernel(count, me, squares, g, w, m, v, *rest):
+def step_kernel(count, with_weight, me, squares, g, w, m, v, *rest):
     new_w, new_m, new_v = rest[-3:]
-    factor = jnp.minimum(1.0, 0.5 * lax.rsqrt(squares[:1, :1] / count + 1e-30))
-    g = g[0].astype(F32) * factor
-    m = 0.9 * m[0] + 0.1 * g
-    v = 0.95 * v[0] + 0.05 * g * g
-    w = w[0].astype(F32)
-    step = m * lax.rsqrt(v + 1e-8) + 0.1 * w
-    new_w[...] = (w - 0.02 * step).astype(BF16)
+    w, m, v = stepped_block(squares[:1, :1], count, g[0], w[0], m[0], v[0])
+    if with_weight:
+        new_w[...] = w
     new_m[0] = m
     new_v[0] = v
 
 
-def stepped(me, squares, count, layer, g, w, m, v, before):
-    rows, lanes = g.shape[1:]
+def stepped_block(squares, count, g, w, m, v):
+    g = g.astype(F32) * jnp.minimum(1.0, 0.5 * lax.rsqrt(squares / count + 1e-30))
+    m = 0.9 * m + 0.1 * g
+    v = 0.95 * v + 0.05 * g * g
+    w = w.astype(F32)
+    step = m * lax.rsqrt(v + 1e-8) + 0.1 * w
+    return (w - 0.02 * step).astype(BF16), m, v
+
+
+def stepped(me, squares, count, unit, g, w, m, v, before):
+    layer, start, rows = unit
+    whole, lanes = g.shape[1:]
     n = rows // 5
-    here = pl.BlockSpec((1, n, lanes), lambda i, me: (layer, i, 0))
+    here = pl.BlockSpec((1, n, lanes), lambda i, me: (layer, start // n + i, 0))
     specs = [
         pl.BlockSpec((8, 128), lambda i, me: (0, 0)),
         here,
-        pl.BlockSpec((1, n, lanes), lambda i, me: (layer, me[0] * 5 + i, 0)),
+        pl.BlockSpec((1, n, lanes), lambda i, me: (layer, me[0] * (whole // n) + start // n + i, 0)),
         here,
         here,
     ]
     moment = jax.ShapeDtypeStruct(m.shape, F32)
     return pl.pallas_call(
-        functools.partial(step_kernel, count),
+        functools.partial(step_kernel, count, True),
         out_shape=[jax.ShapeDtypeStruct((rows, lanes), BF16), moment, moment],
         grid_spec=pltpu.PrefetchScalarGridSpec(
             num_scalar_prefetch=1,
-            grid=(5,),
+            grid=(rows // n,),
             in_specs=specs + [pl.BlockSpec(memory_space=pl.ANY)] * len(before),
             out_specs=[pl.BlockSpec((n, lanes), lambda i, me: (i, 0)), here, here],
         ),
@@ -259,35 +265,43 @@
     )(me, squares, g, w, m, v, *before)
 
 
-def place_kernel(layer, offsets, n_before, *refs):
-    n = len(offsets)
+def place_kernel(places, n_before, in_vmem, *refs):
+    n = len(places)
     blocks, out = refs[:n], refs[n + n_before]
-    held, in_sem, out_sem = refs[n + n_before + 1 :]
-    rows = blocks[0].shape[0]
-    loads = [pltpu.make_async_copy(b, held.at[i], in_sem.at[i]) for i, b in enumerate(blocks)]
+    out_sem, refs = refs[n + n_before + 1], refs[n + n_before + 2 :]
+    loads = []
+    if not in_vmem:
+        held, in_sem = refs[:n], refs[n]
+        loads = [pltpu.make_async_copy(b, h, in_sem.at[i]) for i, (b, h) in enumerate(zip(blocks, held))]
+        blocks = held
     for one in loads:
         one.start()
     stores = []
-    for i, offset in enumerate(offsets):
-        loads[i].wait()
-        at = pl.multiple_of(place(*offset) * rows, 16)
-        stores.append(pltpu.make_async_copy(held.at[i], out.at[layer, pl.ds(at, rows)], out_sem.at[i]))
+    for i, (offset, layer, start) in enumerate(places):
+        if loads:
+            loads[i].wait()
+        at = pl.multiple_of(place(*offset) * (out.shape[1] // 8) + start, 16)
+        stores.append(pltpu.make_async_copy(blocks[i], out.at[layer, pl.ds(at, blocks[i].shape[0])], out_sem.at[i]))
         stores[-1].start()
     for one in stores:
         one.wait()
 
 
-def placed(blocks, offsets, layer, shape, before):
+def placed(blocks, places, shape, before, in_vmem=False):
     n = len(blocks)
     any_ = pl.BlockSpec(memory_space=pl.ANY)
+    scratch = [pltpu.SemaphoreType.DMA((n,))]
+    if not in_vmem:
+        scratch += [pltpu.VMEM(b.shape, BF16) for b in blocks] + [pltpu.SemaphoreType.DMA((n,))]
     return pl.pallas_call(
-        functools.partial(place_kernel, layer, offsets, len(before)),
+        functools.partial(place_kernel, places, len(before), in_vmem),
         out_shape=jax.ShapeDtypeStruct(shape, BF16),
-        in_specs=[any_] * (n + len(before)),
+        in_specs=[pl.BlockSpec(memory_space=pltpu.VMEM) if in_vmem else any_] * n + [any_] * len(before),
         out_specs=any_,
-        scratch_shapes=[pltpu.VMEM((n, *blocks[0].shape), BF16), pltpu.SemaphoreType.DMA((n,)), pltpu.SemaphoreType.DMA((n,))],
+        scratch_shapes=scratch,
         input_output_aliases={n: 0} if before else {},
-        cost_estimate=pl.CostEstimate(flops=0, bytes_accessed=4 * n * blocks[0].size, transcendentals=0),
+        compiler_params=pltpu.CompilerParams(vmem_limit_bytes=16 * 1024 * 1024) if in_vmem else None,
+        cost_estimate=pl.CostEstimate(flops=0, bytes_accessed=4 * sum(b.size for b in blocks), transcendentals=0),
         name="place",
     )(*blocks, *before)
 
@@ -297,32 +311,52 @@
     return lax.ppermute(block, "dp", [(d, d ^ flip) for d in range(8)])
 
 
+def parts_of(layers, shapes):
+    units = []
+    for a, (rows, _) in enumerate(shapes):
+        for l in range(layers):
+            cuts = 2 if (a, l) == (0, 0) else 4 if (a, l) == (2, layers - 1) else 1
+            units += [(a, l, i * rows // cuts, rows // cuts) for i in range(cuts)]
+    return units
+
+
 def solution(mesh):
+    layers, shapes = 2, [(160, 5120), (160, 5120), (640, 1280)]
+    units = parts_of(layers, shapes)
+    groups = []
+    for i, (a, l, _, rows) in enumerate(units):
+        if groups and len(groups[-1]) == 1 and units[i - 1][:2] == (a, l):
+            groups[-1].append(i)
+        else:
+            groups.append([i])
+
     def step(*arrays):
         terms, weights, m, v = (arrays[i : i + 3] for i in (0, 3, 6, 9))
         gradients, squares = summed(terms)
         count = 8 * sum(g.size for g in gradients)
         me = lax.axis_index("dp")[None]
-        layers = weights[0].shape[0]
         new_m, new_v, whole = [()] * 3, [()] * 3, [()] * 3
-        units = [(a, l) for a in range(3) for l in range(layers)]
         first, second = [], []
-        for a, l in units:
-            before = (new_m[a], new_v[a]) if l else ()
-            own, new_m[a], new_v[a] = stepped(me, squares, count, l, gradients[a], weights[a], m[a], v[a], before)
+        for a, *unit in units:
+            before = (new_m[a], new_v[a]) if len(new_m[a]) else ()
+            own, new_m[a], new_v[a] = stepped(me, squares, count, unit, gradients[a], weights[a], m[a], v[a], before)
             first.append((own, send(own, dx=1), send(own, dy=1), send(own, dc=1)))
         for i, (own, x, y, c) in enumerate(first):
             far = send(y, dx=1) if i % 2 else send(x, dy=1)
             second.append((far, send(x, dc=1), send(y, dc=1)))
-        for i, (a, l) in enumerate(units):
+        for i, (a, l, start, _) in enumerate(units):
             own, x, y, c = first[i]
             far, xc, yc = second[i]
-            places = ((0, 0, 0), (1, 0, 0), (0, 1, 0), (0, 0, 1), (1, 0, 1), (0, 1, 1))
-            whole[a] = placed([own, x, y, c, xc, yc], places, l, weights[a].shape, (whole[a],) if l else ())
-        for i, (a, l) in enumerate(units):
-            far = second[i][0]
-            both = [far, send(far, dc=1)]
-            whole[a] = placed(both, ((1, 1, 0), (1, 1, 1)), l, weights[a].shape, (whole[a],))
+            places = [(at, l, start) for at in ((0, 0, 0), (1, 0, 0), (0, 1, 0), (0, 0, 1), (1, 0, 1), (0, 1, 1))]
+            whole[a] = placed([own, x, y, c, xc, yc], places, weights[a].shape, (whole[a],) if len(whole[a]) else ())
+        for group in groups:
+            blocks, places = [], []
+            for i in group:
+                a, l, start, _ = units[i]
+                far = second[i][0]
+                blocks += [far, send(far, dc=1)]
+                places += [((1, 1, 0), l, start), ((1, 1, 1), l, start)]
+            whole[a] = placed(blocks, places, weights[a].shape, (whole[a],), in_vmem=True)
         return (*whole, *new_m, *new_v)
 
     all_of, cut = P(None, None, None), P(None, "dp", None)

time: 742 us -> 806 us (1.086)
  waiting for transfers between devices: 267 us -> 289 us
  starting transfers between devices: 18.6 us -> 36.1 us
  Pallas kernels: 453 us -> 466 us
  local copies, waits for them, and re-layouts: 1.25 us -> 10.8 us
    ppermute x42 -> x70, waiting for transfers between devices: 267 us -> 289 us  [send(): return lax.ppermute(block, 'dp', [(d, d ^ flip) for d in range(8)])]
    ppermute x42 -> x70, starting transfers between devices: 18.6 us -> 36.1 us  [send(): return lax.ppermute(block, 'dp', [(d, d ^ flip) for d in range(8)])]
    pallas_call x18 -> x27, Pallas kernels: 119 us -> 132 us  [the longest x10 67.2 us: stepped(): pl.pallas_call(functools.partial(step_kernel, count, True), out_shape=[ja...]
    unnamed x46 -> x104, local copies, waits for them, and re-layouts: 1.25 us -> 10.8 us
  transfers between devices with their start and end apart: 42 -> 70, of which waited for: 18 -> 28; matrix products, arithmetic and copies ran while one was open for 0% -> 0% of each run, Pallas kernels for 14% -> 14%
where the time goes in v3:
time: 806 us; the launch traced here: 804 us
  Pallas kernels  466 us (58%)
  waiting for transfers between devices  289 us (36%)
  starting transfers between devices  36.1 us (4%)
  local copies, waits for them, and re-layouts  10.8 us (1%)
    pallas_call x1, Pallas kernels, summed(): pl.pallas_call(functools.partial(sum_kernel, shapes), out_shape=[jax.Shap...  334 us
    ppermute x70, waiting for transfers between devices, send(): return lax.ppermute(block, 'dp', [(d, d ^ flip) for d in range(8)])  289 us
    pallas_call x10, Pallas kernels, stepped(): pl.pallas_call(functools.partial(step_kernel, count, True), out_shape=[ja...  67.2 us
    pallas_call x17, Pallas kernels, placed(): pl.pallas_call(functools.partial(place_kernel, places, len(before), in_vm...  64.6 us
    ppermute x70, starting transfers between devices, send(): return lax.ppermute(block, 'dp', [(d, d ^ flip) for d in range(8)])  36.1 us
  transfers between devices with their start and end apart: 70, of which 28 were waited for; matrix products, arithmetic and copies ran while one was open for 0% of the time, Pallas kernels for 14%

profile of v3, /device:TPU:0, one launch (start us, length us, event | category | flops | bytes accessed | tf_op | source)
XLA Modules:
  0.0 803.9 jit_solution(6951685810929689162)
XLA Ops:
  0.6 334.3 %sum_terms.1 = (bf16[2,160,5120]{2,1,0:T(8,128)(2,1)}, bf16[2,160,5120]{2,1,0:T(8,128)(2,1)}, bf16[2,640,1280]{2,1,0:T(8,128)(2,1)}, f32[8,128]{1,0:T(8,128)}, b...) custom-call(bf16[1,2,1280,5120]{3,2,1,0:T(8,128)(2,1)} %refs_0_.1, ...), custom_call_target="tpu_custom_call" | custom-call | tf_op jit(solution)/shard_map/sum_terms/pallas_call | solution.py:193
  335.0 9.0 %adamw.15 = (bf16[640,1280]{1,0:T(8,128)(2,1)}, f32[2,640,1280]{2,1,0:T(8,128)}, f32[2,640,1280]{2,1,0:T(8,128)}) custom-call(s32[1]{0:T(128)} %bitcast.me, f32[8,128]{1,0:T(8,128)} %get-tuple-element.43.squares, bf16[2,640,1280]{2,1,0:T(8,128)(2,1)} %get-tuple-element.57.g, bf16[2,5120,1280]{2,1,0:T(8,128)(2,1)} %w.19, f32[2,640,1280]{2,1,0:T(8,128)} %m.19, ...), custom_call_target="tpu_custom_call" | custom-call | flops 12288000 | bytes 18022400 | tf_op jit(solution)/shard_map/adamw/pallas_call | solution.py:253
  344.0 4.7 adamw.16
  348.7 1.3 collective-permute-start.41
  350.7 4.7 adamw.17
  355.4 1.3 collective-permute-start.44
  357.4 4.7 adamw.18
  364.3 4.7 adamw.19
  369.1 2.2 collective-permute-done.44.refs_2_
  372.7 6.1 collective-permute-done.35.refs_1_
  378.7 1.4 collective-permute-done.54.refs_2_
  380.7 6.1 collective-permute-done.50.refs_1_
  392.4 6.2 adamw.10
  398.6 6.2 adamw.11
  405.8 1.3 collective-permute-start.17
  407.8 2.7 collective-permute-done.39.refs_2_
  411.3 24.7 %collective-permute-done.36.refs_0_ = bf16[160,1280]{1,0:T(8,128)(2,1)} collective-permute-done((bf16[160,1280]{1,0:T(8,128)(2,1)}, bf16[160,1280]{1,0:T(8,128)(2,1)}, u32[]{:S(2)}, u32[]{:S(2)}) %collective-permute-start.36) | collective-permute-done | bytes 409632 | tf_op jit(solution)/shard_map/ppermute | solution.py:311
  437.1 9.1 %adamw.13 = (bf16[160,5120]{1,0:T(8,128)(2,1)}, f32[2,160,5120]{2,1,0:T(8,128)}, f32[2,160,5120]{2,1,0:T(8,128)}) custom-call(s32[1]{0:T(128)} %bitcast.me, f32[8,128]{1,0:T(8,128)} %get-tuple-element.43.squares, bf16[2,160,5120]{2,1,0:T(8,128)(2,1)} %get-tuple-element.52.g, bf16[2,1280,5120]{2,1,0:T(8,128)(2,1)} %w.14, f32[2,160,5120]{2,1,0:T(8,128)} %m.14, ...), custom_call_target="tpu_custom_call" | custom-call | flops 12288000 | bytes 18022400 | tf_op jit(solution)/shard_map/adamw/pallas_call | solution.py:253
  446.2 1.3 collective-permute-start.47
  448.4 5.1 collective-permute-done.6.refs_2_
  453.6 1.3 collective-permute-start.24
  454.8 2.6 collective-permute-done.13.refs_1_
  457.4 2.7 collective-permute-done.14.refs_3_
  461.2 9.0 %adamw.14 = (bf16[160,5120]{1,0:T(8,128)(2,1)}, f32[2,160,5120]{2,1,0:T(8,128)}, f32[2,160,5120]{2,1,0:T(8,128)}) custom-call(s32[1]{0:T(128)} %bitcast.me, f32[8,128]{1,0:T(8,128)} %get-tuple-element.43.squares, bf16[2,160,5120]{2,1,0:T(8,128)(2,1)} %get-tuple-element.52.g, ...), custom_call_target="tpu_custom_call", output_to_operand_aliasing={{1}: (6, {}), {2}: (7, {})} | custom-call | flops 12288000 | bytes 18022400 | tf_op jit(solution)/shard_map/adamw/pallas_call | solution.py:253
  470.1 18.5 %collective-permute-done.47.refs_2_ = bf16[640,1280]{1,0:T(8,128)(2,1)} collective-permute-done((bf16[640,1280]{1,0:T(8,128)(2,1)S(1)}, bf16[640,1280]{1,0:T(8,128)(2,1)}, u32[]{:S(2)}, u32[]{:S(2)}) %collective-permute-start.47) | collective-permute-done | bytes 1638432 | tf_op jit(solution)/shard_map/ppermute | solution.py:311
  488.7 3.9 collective-permute-done.66.refs_1_
  493.6 1.3 collective-permute-start.27
  494.9 28.9 %collective-permute-done.24.refs_2_ = bf16[160,5120]{1,0:T(8,128)(2,1)} collective-permute-done((bf16[160,5120]{1,0:T(8,128)(2,1)}, bf16[160,5120]{1,0:T(8,128)(2,1)}, u32[]{:S(2)}, u32[]{:S(2)}) %collective-permute-start.24) | collective-permute-done | bytes 1638432 | tf_op jit(solution)/shard_map/ppermute | solution.py:311
  523.8 9.0 %adamw.12 = (bf16[160,5120]{1,0:T(8,128)(2,1)}, f32[2,160,5120]{2,1,0:T(8,128)}, f32[2,160,5120]{2,1,0:T(8,128)}) custom-call(s32[1]{0:T(128)} %bitcast.me, f32[8,128]{1,0:T(8,128)} %get-tuple-element.43.squares, bf16[2,160,5120]{2,1,0:T(8,128)(2,1)} %get-tuple-element.44.g, ...), custom_call_target="tpu_custom_call", output_to_operand_aliasing={{1}: (6, {}), {2}: (7, {})} | custom-call | flops 12288000 | bytes 18022400 | tf_op jit(solution)/shard_map/adamw/pallas_call | solution.py:253
  534.0 28.7 %collective-permute-done.21.refs_1_ = bf16[160,5120]{1,0:T(8,128)(2,1)} collective-permute-done((bf16[160,5120]{1,0:T(8,128)(2,1)}, bf16[160,5120]{1,0:T(8,128)(2,1)}, u32[]{:S(2)}, u32[]{:S(2)}) %collective-permute-start.21) | collective-permute-done | bytes 1638432 | tf_op jit(solution)/shard_map/ppermute | solution.py:311
  563.3 1.3 collective-permute-start.9
  567.6 1.3 collective-permute-start.4
  568.9 28.8 %collective-permute-done.refs_1_ = bf16[160,5120]{1,0:T(8,128)(2,1)S(1)} collective-permute-done((bf16[160,5120]{1,0:T(8,128)(2,1)}, bf16[160,5120]{1,0:T(8,128)(2,1)S(1)}, u32[]{:S(2)}, u32[]{:S(2)}) %collective-permute-start) | collective-permute-done | bytes 1638432 | tf_op jit(solution)/shard_map/ppermute | solution.py:311
  597.8 12.8 %collective-permute-done.7.refs_2_ = bf16[80,5120]{1,0:T(8,128)(2,1)S(1)} collective-permute-done((bf16[80,5120]{1,0:T(8,128)(2,1)}, bf16[80,5120]{1,0:T(8,128)(2,1)S(1)}, u32[]{:S(2)}, u32[]{:S(2)}) %collective-permute-start.7) | collective-permute-done | bytes 819232 | tf_op jit(solution)/shard_map/ppermute | solution.py:311
  610.6 8.7 %collective-permute-done.4.refs_0_ = bf16[80,5120]{1,0:T(8,128)(2,1)S(1)} collective-permute-done((bf16[80,5120]{1,0:T(8,128)(2,1)}, bf16[80,5120]{1,0:T(8,128)(2,1)S(1)}, u32[]{:S(2)}, u32[]{:S(2)}) %collective-permute-start.4) | collective-permute-done | bytes 819232 | tf_op jit(solution)/shard_map/ppermute | solution.py:311
  622.1 1.8 collective-permute-done.68.refs_4_
  624.1 33.7 %collective-permute-done.48.refs_0_ = bf16[640,1280]{1,0:T(8,128)(2,1)S(1)} collective-permute-done((bf16[640,1280]{1,0:T(8,128)(2,1)}, bf16[640,1280]{1,0:T(8,128)(2,1)S(1)}, u32[]{:S(2)}, u32[]{:S(2)}) %collective-permute-start.48) | collective-permute-done | bytes 1638432 | tf_op jit(solution)/shard_map/ppermute | solution.py:311
  658.8 1.3 collective-permute-start.22
  661.3 33.5 %collective-permute-done.25.refs_0_ = bf16[160,5120]{1,0:T(8,128)(2,1)S(1)} collective-permute-done((bf16[160,5120]{1,0:T(8,128)(2,1)}, bf16[160,5120]{1,0:T(8,128)(2,1)S(1)}, u32[]{:S(2)}, u32[]{:S(2)}) %collective-permute-start.25) | collective-permute-done | bytes 1638432 | tf_op jit(solution)/shard_map/ppermute | solution.py:311
  694.9 1.2 copy-done
  696.0 1.7 collective-permute-done.22.refs_0_
  697.7 1.2 copy-done.2
  699.4 1.3 copy-done.4
  700.7 30.2 %collective-permute-done.1.refs_0_ = bf16[160,5120]{1,0:T(8,128)(2,1)} collective-permute-done((bf16[160,5120]{1,0:T(8,128)(2,1)S(1)}, bf16[160,5120]{1,0:T(8,128)(2,1)}, u32[]{:S(2)}, u32[]{:S(2)}) %collective-permute-start.1) | collective-permute-done | bytes 1638432 | tf_op jit(solution)/shard_map/ppermute | solution.py:311
  731.4 1.2 copy-done.6
  732.6 1.2 copy-done.8
  734.3 1.2 copy-done.10
  735.6 4.2 place.17.refs_6_
  739.7 4.2 place.18.refs_6_
  743.9 7.7 place.26.refs_6_
  751.6 7.7 place.22.refs_6_
  759.2 7.7 place.19.refs_4_
  766.9 1.8 place.20.refs_2_
  768.6 2.5 place.27.refs_6_
  771.2 2.5 place.28.refs_6_
  773.7 2.5 place.29.refs_6_
  776.3 2.5 place.30.refs_2_
  778.8 7.8 place.23.refs_2_
  787.2 1.7 place.31.refs_4_
  790.3 1.7 place.24.refs_2_
  793.4 1.7 place.25
  795.1 3.7 place.21
  798.9 2.4 place.32.refs_4_
  801.3 2.4 place.33
  (208 shorter events, 32.8 us)
Async XLA Ops:
  348.7 13.5 %collective-permute-start.41 = (bf16[160,1280]{1,0:T(8,128)(2,1)}, bf16[160,1280]{1,0:T(8,128)(2,1)S(1)}, u32[]{:S(2)}, u32[]{:S(2)}) collective-permute-start(bf16[160,1280]{1,0:T(8,128)(2,1)} %get-tuple-element.68.refs_0_), channel_id=1, source_target_pairs={{0,4},{1,5},{2,6},{3,7},{4,0},{5,1},{6,2},{7,3}} | collective-permute-start | bytes 1228808 | tf_op jit(solution)/shard_map/ppermute | solution.py:311
  350.0 12.6 %collective-permute-start.62 = (bf16[160,1280]{1,0:T(8,128)(2,1)}, bf16[160,1280]{1,0:T(8,128)(2,1)S(1)}, u32[]{:S(2)}, u32[]{:S(2)}) collective-permute-start(bf16[160,1280]{1,0:T(8,128)(2,1)} %get-tuple-element.68.refs_0_), channel_id=1, source_target_pairs={{0,2},{1,3},{2,0},{3,1},{4,6},{5,7},{6,4},{7,5}} | collective-permute-start | bytes 1228808 | tf_op jit(solution)/shard_map/ppermute | solution.py:311
  350.7 12.8 %collective-permute-start.63 = (bf16[160,1280]{1,0:T(8,128)(2,1)}, bf16[160,1280]{1,0:T(8,128)(2,1)S(1)}, u32[]{:S(2)}, u32[]{:S(2)}) collective-permute-start(bf16[160,1280]{1,0:T(8,128)(2,1)} %get-tuple-element.68.refs_0_), channel_id=1, source_target_pairs={{0,1},{1,0},{2,3},{3,2},{4,5},{5,4},{6,7},{7,6}} | collective-permute-start | bytes 1228808 | tf_op jit(solution)/shard_map/ppermute | solution.py:311
  355.4 15.9 %collective-permute-start.44 = (bf16[160,1280]{1,0:T(8,128)(2,1)}, bf16[160,1280]{1,0:T(8,128)(2,1)S(1)}, u32[]{:S(2)}, u32[]{:S(2)}) collective-permute-start(bf16[160,1280]{1,0:T(8,128)(2,1)} %get-tuple-element.69.refs_0_), channel_id=1, source_target_pairs={{0,2},{1,3},{2,0},{3,1},{4,6},{5,7},{6,4},{7,5}} | collective-permute-start | bytes 1228808 | tf_op jit(solution)/shard_map/ppermute | solution.py:311
  356.7 14.6 %collective-permute-start.58 = (bf16[160,1280]{1,0:T(8,128)(2,1)}, bf16[160,1280]{1,0:T(8,128)(2,1)S(1)}, u32[]{:S(2)}, u32[]{:S(2)}) collective-permute-start(bf16[160,1280]{1,0:T(8,128)(2,1)} %get-tuple-element.69.refs_0_), channel_id=1, source_target_pairs={{0,4},{1,5},{2,6},{3,7},{4,0},{5,1},{6,2},{7,3}} | collective-permute-start | bytes 1228808 | tf_op jit(solution)/shard_map/ppermute | solution.py:311
  362.2 9.9 %collective-permute-start.59 = (bf16[160,1280]{1,0:T(8,128)(2,1)S(1)}, bf16[160,1280]{1,0:T(8,128)(2,1)S(1)}, u32[]{:S(2)}, u32[]{:S(2)}) collective-permute-start(bf16[160,1280]{1,0:T(8,128)(2,1)S(1)} %copy-done.38), channel_id=1, source_target_pairs={{0,1},{1,0},{2,3},{3,2},{4,5},{5,4},{6,7},{7,6}} | collective-permute-start | bytes 1228808 | tf_op jit(solution)/shard_map/ppermute | solution.py:311
  362.5 16.2 %collective-permute-start.35 = (bf16[160,1280]{1,0:T(8,128)(2,1)}, bf16[160,1280]{1,0:T(8,128)(2,1)}, u32[]{:S(2)}, u32[]{:S(2)}) collective-permute-start(bf16[160,1280]{1,0:T(8,128)(2,1)} %get-tuple-element.64.refs_0_), channel_id=1, source_target_pairs={{0,4},{1,5},{2,6},{3,7},{4,0},{5,1},{6,2},{7,3}} | collective-permute-start | bytes 1228808 | tf_op jit(solution)/shard_map/ppermute | solution.py:311
  363.6 16.6 %collective-permute-start.54 = (bf16[160,1280]{1,0:T(8,128)(2,1)}, bf16[160,1280]{1,0:T(8,128)(2,1)}, u32[]{:S(2)}, u32[]{:S(2)}) collective-permute-start(bf16[160,1280]{1,0:T(8,128)(2,1)} %get-tuple-element.64.refs_0_), channel_id=1, source_target_pairs={{0,2},{1,3},{2,0},{3,1},{4,6},{5,7},{6,4},{7,5}} | collective-permute-start | bytes 1228808 | tf_op jit(solution)/shard_map/ppermute | solution.py:311
  371.3 8.9 %collective-permute-start.55 = (bf16[160,1280]{1,0:T(8,128)(2,1)S(1)}, bf16[160,1280]{1,0:T(8,128)(2,1)S(1)}, u32[]{:S(2)}, u32[]{:S(2)}) collective-permute-start(bf16[160,1280]{1,0:T(8,128)(2,1)S(1)} %copy-done.40), channel_id=1, source_target_pairs={{0,1},{1,0},{2,3},{3,2},{4,5},{5,4},{6,7},{7,6}} | collective-permute-start | bytes 1228808 | tf_op jit(solution)/shard_map/ppermute | solution.py:311
  371.3 15.5 %collective-permute-start.50 = (bf16[160,1280]{1,0:T(8,128)(2,1)}, bf16[160,1280]{1,0:T(8,128)(2,1)}, u32[]{:S(2)}, u32[]{:S(2)}) collective-permute-start(bf16[160,1280]{1,0:T(8,128)(2,1)} %get-tuple-element.67.refs_0_), channel_id=1, source_target_pairs={{0,4},{1,5},{2,6},{3,7},{4,0},{5,1},{6,2},{7,3}} | collective-permute-start | bytes 1228808 | tf_op jit(solution)/shard_map/ppermute | solution.py:311
  372.1 15.6 %collective-permute-start.38 = (bf16[160,1280]{1,0:T(8,128)(2,1)}, bf16[160,1280]{1,0:T(8,128)(2,1)S(1)}, u32[]{:S(2)}, u32[]{:S(2)}) collective-permute-start(bf16[160,1280]{1,0:T(8,128)(2,1)} %get-tuple-element.67.refs_0_), channel_id=1, source_target_pairs={{0,2},{1,3},{2,0},{3,1},{4,6},{5,7},{6,4},{7,5}} | collective-permute-start | bytes 1228808 | tf_op jit(solution)/shard_map/ppermute | solution.py:311
  378.7 9.0 %collective-permute-start.51 = (bf16[160,1280]{1,0:T(8,128)(2,1)}, bf16[160,1280]{1,0:T(8,128)(2,1)S(1)}, u32[]{:S(2)}, u32[]{:S(2)}) collective-permute-start(bf16[160,1280]{1,0:T(8,128)(2,1)} %get-tuple-element.67.refs_0_), channel_id=1, source_target_pairs={{0,1},{1,0},{2,3},{3,2},{4,5},{5,4},{6,7},{7,6}} | collective-permute-start | bytes 1228808 | tf_op jit(solution)/shard_map/ppermute | solution.py:311
  380.2 8.1 %collective-permute-start.64 = (bf16[160,1280]{1,0:T(8,128)(2,1)S(1)}, bf16[160,1280]{1,0:T(8,128)(2,1)S(1)}, u32[]{:S(2)}, u32[]{:S(2)}) collective-permute-start(bf16[160,1280]{1,0:T(8,128)(2,1)S(1)} %collective-permute-done.41.refs_1_), channel_id=1, source_target_pairs={{0,1},{1,0},{2,3},{3,2},{4,5},{5,4},{6,7},{7,6}} | collective-permute-start | bytes 1228808 | tf_op jit(solution)/shard_map/ppermute | solution.py:311
  380.2 8.1 %collective-permute-start.65 = (bf16[160,1280]{1,0:T(8,128)(2,1)S(1)}, bf16[160,1280]{1,0:T(8,128)(2,1)S(1)}, u32[]{:S(2)}, u32[]{:S(2)}) collective-permute-start(bf16[160,1280]{1,0:T(8,128)(2,1)S(1)} %collective-permute-done.62.refs_2_), channel_id=1, source_target_pairs={{0,1},{1,0},{2,3},{3,2},{4,5},{5,4},{6,7},{7,6}} | collective-permute-start | bytes 1228808 | tf_op jit(solution)/shard_map/ppermute | solution.py:311
  388.2 3.0 collective-permute-start.57
  388.3 16.5 %collective-permute-start.52 = (bf16[160,1280]{1,0:T(8,128)(2,1)}, bf16[160,1280]{1,0:T(8,128)(2,1)}, u32[]{:S(2)}, u32[]{:S(2)}) collective-permute-start(bf16[160,1280]{1,0:T(8,128)(2,1)} %collective-permute-done.50.refs_1_), channel_id=1, source_target_pairs={{0,1},{1,0},{2,3},{3,2},{4,5},{5,4},{6,7},{7,6}} | collective-permute-start | bytes 1228808 | tf_op jit(solution)/shard_map/ppermute | solution.py:311
  388.8 17.0 %collective-permute-start.53 = (bf16[160,1280]{1,0:T(8,128)(2,1)S(1)}, bf16[160,1280]{1,0:T(8,128)(2,1)}, u32[]{:S(2)}, u32[]{:S(2)}) collective-permute-start(bf16[160,1280]{1,0:T(8,128)(2,1)S(1)} %collective-permute-done.38.refs_2_), channel_id=1, source_target_pairs={{0,1},{1,0},{2,3},{3,2},{4,5},{5,4},{6,7},{7,6}} | collective-permute-start | bytes 1228808 | tf_op jit(solution)/shard_map/ppermute | solution.py:311
  389.5 17.6 %collective-permute-start.45 = (bf16[160,1280]{1,0:T(8,128)(2,1)S(1)}, bf16[160,1280]{1,0:T(8,128)(2,1)S(1)}, u32[]{:S(2)}, u32[]{:S(2)}) collective-permute-start(bf16[160,1280]{1,0:T(8,128)(2,1)S(1)} %collective-permute-done.44.refs_2_), channel_id=1, source_target_pairs={{0,4},{1,5},{2,6},{3,7},{4,0},{5,1},{6,2},{7,3}} | collective-permute-start | bytes 1228808 | tf_op jit(solution)/shard_map/ppermute | solution.py:311
  390.4 17.4 %collective-permute-start.42 = (bf16[160,1280]{1,0:T(8,128)(2,1)S(1)}, bf16[160,1280]{1,0:T(8,128)(2,1)S(1)}, u32[]{:S(2)}, u32[]{:S(2)}) collective-permute-start(bf16[160,1280]{1,0:T(8,128)(2,1)S(1)} %collective-permute-done.41.refs_1_), channel_id=1, source_target_pairs={{0,2},{1,3},{2,0},{3,1},{4,6},{5,7},{6,4},{7,5}} | collective-permute-start | bytes 1228808 | tf_op jit(solution)/shard_map/ppermute | solution.py:311
  391.3 19.3 %collective-permute-start.39 = (bf16[160,1280]{1,0:T(8,128)(2,1)S(1)}, bf16[160,1280]{1,0:T(8,128)(2,1)S(1)}, u32[]{:S(2)}, u32[]{:S(2)}) collective-permute-start(bf16[160,1280]{1,0:T(8,128)(2,1)S(1)} %collective-permute-done.38.refs_2_), channel_id=1, source_target_pairs={{0,4},{1,5},{2,6},{3,7},{4,0},{5,1},{6,2},{7,3}} | collective-permute-start | bytes 1228808 | tf_op jit(solution)/shard_map/ppermute | solution.py:311
  404.8 41.4 %collective-permute-start.3 = (bf16[80,5120]{1,0:T(8,128)(2,1)}, bf16[80,5120]{1,0:T(8,128)(2,1)}, u32[]{:S(2)}, u32[]{:S(2)}) collective-permute-start(bf16[80,5120]{1,0:T(8,128)(2,1)} %get-tuple-element.50.refs_0_), channel_id=1, source_target_pairs={{0,4},{1,5},{2,6},{3,7},{4,0},{5,1},{6,2},{7,3}} | collective-permute-start | bytes 2457608 | tf_op jit(solution)/shard_map/ppermute | solution.py:311
  405.8 41.7 %collective-permute-start.17 = (bf16[80,5120]{1,0:T(8,128)(2,1)}, bf16[80,5120]{1,0:T(8,128)(2,1)}, u32[]{:S(2)}, u32[]{:S(2)}) collective-permute-start(bf16[80,5120]{1,0:T(8,128)(2,1)} %get-tuple-element.50.refs_0_), channel_id=1, source_target_pairs={{0,2},{1,3},{2,0},{3,1},{4,6},{5,7},{6,4},{7,5}} | collective-permute-start | bytes 2457608 | tf_op jit(solution)/shard_map/ppermute | solution.py:311
  407.1 28.9 %collective-permute-start.36 = (bf16[160,1280]{1,0:T(8,128)(2,1)}, bf16[160,1280]{1,0:T(8,128)(2,1)}, u32[]{:S(2)}, u32[]{:S(2)}) collective-permute-start(bf16[160,1280]{1,0:T(8,128)(2,1)} %collective-permute-done.35.refs_1_), channel_id=1, source_target_pairs={{0,2},{1,3},{2,0},{3,1},{4,6},{5,7},{6,4},{7,5}} | collective-permute-start | bytes 1228808 | tf_op jit(solution)/shard_map/ppermute | solution.py:311
  407.8 40.6 %collective-permute-start.18 = (bf16[80,5120]{1,0:T(8,128)(2,1)}, bf16[80,5120]{1,0:T(8,128)(2,1)}, u32[]{:S(2)}, u32[]{:S(2)}) collective-permute-start(bf16[80,5120]{1,0:T(8,128)(2,1)} %get-tuple-element.50.refs_0_), channel_id=1, source_target_pairs={{0,1},{1,0},{2,3},{3,2},{4,5},{5,4},{6,7},{7,6}} | collective-permute-start | bytes 2457608 | tf_op jit(solution)/shard_map/ppermute | solution.py:311
  410.6 43.0 %collective-permute-start.6 = (bf16[80,5120]{1,0:T(8,128)(2,1)}, bf16[80,5120]{1,0:T(8,128)(2,1)}, u32[]{:S(2)}, u32[]{:S(2)}) collective-permute-start(bf16[80,5120]{1,0:T(8,128)(2,1)} %get-tuple-element.51.refs_0_), channel_id=1, source_target_pairs={{0,2},{1,3},{2,0},{3,1},{4,6},{5,7},{6,4},{7,5}} | collective-permute-start | bytes 2457608 | tf_op jit(solution)/shard_map/ppermute | solution.py:311
  436.0 21.4 %collective-permute-start.13 = (bf16[80,5120]{1,0:T(8,128)(2,1)}, bf16[80,5120]{1,0:T(8,128)(2,1)}, u32[]{:S(2)}, u32[]{:S(2)}) collective-permute-start(bf16[80,5120]{1,0:T(8,128)(2,1)} %get-tuple-element.51.refs_0_), channel_id=1, source_target_pairs={{0,4},{1,5},{2,6},{3,7},{4,0},{5,1},{6,2},{7,3}} | collective-permute-start | bytes 2457608 | tf_op jit(solution)/shard_map/ppermute | solution.py:311
  446.2 42.5 %collective-permute-start.47 = (bf16[640,1280]{1,0:T(8,128)(2,1)S(1)}, bf16[640,1280]{1,0:T(8,128)(2,1)}, u32[]{:S(2)}, u32[]{:S(2)}) collective-permute-start(bf16[640,1280]{1,0:T(8,128)(2,1)S(1)} %copy-done.18), channel_id=1, source_target_pairs={{0,2},{1,3},{2,0},{3,1},{4,6},{5,7},{6,4},{7,5}} | collective-permute-start | bytes 4915208 | tf_op jit(solution)/shard_map/ppermute | solution.py:311
  447.5 45.1 %collective-permute-start.66 = (bf16[640,1280]{1,0:T(8,128)(2,1)S(1)}, bf16[640,1280]{1,0:T(8,128)(2,1)}, u32[]{:S(2)}, u32[]{:S(2)}) collective-permute-start(bf16[640,1280]{1,0:T(8,128)(2,1)S(1)} %copy-done.18), channel_id=1, source_target_pairs={{0,4},{1,5},{2,6},{3,7},{4,0},{5,1},{6,2},{7,3}} | collective-permute-start | bytes 4915208 | tf_op jit(solution)/shard_map/ppermute | solution.py:311
  448.4 45.2 %collective-permute-start.67 = (bf16[640,1280]{1,0:T(8,128)(2,1)S(1)}, bf16[640,1280]{1,0:T(8,128)(2,1)}, u32[]{:S(2)}, u32[]{:S(2)}) collective-permute-start(bf16[640,1280]{1,0:T(8,128)(2,1)S(1)} %copy-done.18), channel_id=1, source_target_pairs={{0,1},{1,0},{2,3},{3,2},{4,5},{5,4},{6,7},{7,6}} | collective-permute-start | bytes 4915208 | tf_op jit(solution)/shard_map/ppermute | solution.py:311
  453.6 70.2 %collective-permute-start.24 = (bf16[160,5120]{1,0:T(8,128)(2,1)}, bf16[160,5120]{1,0:T(8,128)(2,1)}, u32[]{:S(2)}, u32[]{:S(2)}) collective-permute-start(bf16[160,5120]{1,0:T(8,128)(2,1)} %get-tuple-element.56.refs_0_), channel_id=1, source_target_pairs={{0,2},{1,3},{2,0},{3,1},{4,6},{5,7},{6,4},{7,5}} | collective-permute-start | bytes 4915208 | tf_op jit(solution)/shard_map/ppermute | solution.py:311
  460.1 72.6 %collective-permute-start.31 = (bf16[160,5120]{1,0:T(8,128)(2,1)}, bf16[160,5120]{1,0:T(8,128)(2,1)}, u32[]{:S(2)}, u32[]{:S(2)}) collective-permute-start(bf16[160,5120]{1,0:T(8,128)(2,1)} %get-tuple-element.56.refs_0_), channel_id=1, source_target_pairs={{0,4},{1,5},{2,6},{3,7},{4,0},{5,1},{6,2},{7,3}} | collective-permute-start | bytes 4915208 | tf_op jit(solution)/shard_map/ppermute | solution.py:311
  488.7 45.2 %collective-permute-start.32 = (bf16[160,5120]{1,0:T(8,128)(2,1)}, bf16[160,5120]{1,0:T(8,128)(2,1)}, u32[]{:S(2)}, u32[]{:S(2)}) collective-permute-start(bf16[160,5120]{1,0:T(8,128)(2,1)} %get-tuple-element.56.refs_0_), channel_id=1, source_target_pairs={{0,1},{1,0},{2,3},{3,2},{4,5},{5,4},{6,7},{7,6}} | collective-permute-start | bytes 4915208 | tf_op jit(solution)/shard_map/ppermute | solution.py:311
  492.5 70.2 %collective-permute-start.21 = (bf16[160,5120]{1,0:T(8,128)(2,1)}, bf16[160,5120]{1,0:T(8,128)(2,1)}, u32[]{:S(2)}, u32[]{:S(2)}) collective-permute-start(bf16[160,5120]{1,0:T(8,128)(2,1)} %get-tuple-element.55.refs_0_), channel_id=1, source_target_pairs={{0,4},{1,5},{2,6},{3,7},{4,0},{5,1},{6,2},{7,3}} | collective-permute-start | bytes 4915208 | tf_op jit(solution)/shard_map/ppermute | solution.py:311
  493.6 69.2 %collective-permute-start.27 = (bf16[160,5120]{1,0:T(8,128)(2,1)}, bf16[160,5120]{1,0:T(8,128)(2,1)S(1)}, u32[]{:S(2)}, u32[]{:S(2)}) collective-permute-start(bf16[160,5120]{1,0:T(8,128)(2,1)} %get-tuple-element.55.refs_0_), channel_id=1, source_target_pairs={{0,2},{1,3},{2,0},{3,1},{4,6},{5,7},{6,4},{7,5}} | collective-permute-start | bytes 4915208 | tf_op jit(solution)/shard_map/ppermute | solution.py:311
  523.8 39.5 %collective-permute-start.28 = (bf16[160,5120]{1,0:T(8,128)(2,1)}, bf16[160,5120]{1,0:T(8,128)(2,1)S(1)}, u32[]{:S(2)}, u32[]{:S(2)}) collective-permute-start(bf16[160,5120]{1,0:T(8,128)(2,1)} %get-tuple-element.55.refs_0_), channel_id=1, source_target_pairs={{0,1},{1,0},{2,3},{3,2},{4,5},{5,4},{6,7},{7,6}} | collective-permute-start | bytes 4915208 | tf_op jit(solution)/shard_map/ppermute | solution.py:311
  532.7 65.0 %collective-permute-start = (bf16[160,5120]{1,0:T(8,128)(2,1)}, bf16[160,5120]{1,0:T(8,128)(2,1)S(1)}, u32[]{:S(2)}, u32[]{:S(2)}) collective-permute-start(bf16[160,5120]{1,0:T(8,128)(2,1)} %get-tuple-element.49.refs_0_), channel_id=1, source_target_pairs={{0,4},{1,5},{2,6},{3,7},{4,0},{5,1},{6,2},{7,3}} | collective-permute-start | bytes 4915208 | tf_op jit(solution)/shard_map/ppermute | solution.py:311
  533.8 29.5 %collective-permute-start.19 = (bf16[80,5120]{1,0:T(8,128)(2,1)}, bf16[80,5120]{1,0:T(8,128)(2,1)S(1)}, u32[]{:S(2)}, u32[]{:S(2)}) collective-permute-start(bf16[80,5120]{1,0:T(8,128)(2,1)} %collective-permute-done.3.refs_1_), channel_id=1, source_target_pairs={{0,1},{1,0},{2,3},{3,2},{4,5},{5,4},{6,7},{7,6}} | collective-permute-start | bytes 2457608 | tf_op jit(solution)/shard_map/ppermute | solution.py:311
  562.8 3.7 collective-permute-start.16
  563.3 4.4 collective-permute-start.15
  563.3 55.9 %collective-permute-start.9 = (bf16[160,5120]{1,0:T(8,128)(2,1)}, bf16[160,5120]{1,0:T(8,128)(2,1)S(1)}, u32[]{:S(2)}, u32[]{:S(2)}) collective-permute-start(bf16[160,5120]{1,0:T(8,128)(2,1)} %get-tuple-element.49.refs_0_), channel_id=1, source_target_pairs={{0,2},{1,3},{2,0},{3,1},{4,6},{5,7},{6,4},{7,5}} | collective-permute-start | bytes 4915208 | tf_op jit(solution)/shard_map/ppermute | solution.py:311
  565.3 54.5 %collective-permute-start.10 = (bf16[160,5120]{1,0:T(8,128)(2,1)}, bf16[160,5120]{1,0:T(8,128)(2,1)}, u32[]{:S(2)}, u32[]{:S(2)}) collective-permute-start(bf16[160,5120]{1,0:T(8,128)(2,1)} %get-tuple-element.49.refs_0_), channel_id=1, source_target_pairs={{0,1},{1,0},{2,3},{3,2},{4,5},{5,4},{6,7},{7,6}} | collective-permute-start | bytes 4915208 | tf_op jit(solution)/shard_map/ppermute | solution.py:311
  566.5 44.1 %collective-permute-start.7 = (bf16[80,5120]{1,0:T(8,128)(2,1)}, bf16[80,5120]{1,0:T(8,128)(2,1)S(1)}, u32[]{:S(2)}, u32[]{:S(2)}) collective-permute-start(bf16[80,5120]{1,0:T(8,128)(2,1)} %collective-permute-done.6.refs_2_), channel_id=1, source_target_pairs={{0,4},{1,5},{2,6},{3,7},{4,0},{5,1},{6,2},{7,3}} | collective-permute-start | bytes 2457608 | tf_op jit(solution)/shard_map/ppermute | solution.py:311
  567.6 51.6 %collective-permute-start.4 = (bf16[80,5120]{1,0:T(8,128)(2,1)}, bf16[80,5120]{1,0:T(8,128)(2,1)S(1)}, u32[]{:S(2)}, u32[]{:S(2)}) collective-permute-start(bf16[80,5120]{1,0:T(8,128)(2,1)} %collective-permute-done.3.refs_1_), channel_id=1, source_target_pairs={{0,2},{1,3},{2,0},{3,1},{4,6},{5,7},{6,4},{7,5}} | collective-permute-start | bytes 2457608 | tf_op jit(solution)/shard_map/ppermute | solution.py:311
  597.8 24.0 %collective-permute-start.69 = (bf16[640,1280]{1,0:T(8,128)(2,1)}, bf16[640,1280]{1,0:T(8,128)(2,1)S(1)}, u32[]{:S(2)}, u32[]{:S(2)}) collective-permute-start(bf16[640,1280]{1,0:T(8,128)(2,1)} %collective-permute-done.47.refs_2_), channel_id=1, source_target_pairs={{0,1},{1,0},{2,3},{3,2},{4,5},{5,4},{6,7},{7,6}} | collective-permute-start | bytes 4915208 | tf_op jit(solution)/shard_map/ppermute | solution.py:311
  610.6 10.3 %collective-permute-start.8 = (bf16[80,5120]{1,0:T(8,128)(2,1)S(1)}, bf16[80,5120]{1,0:T(8,128)(2,1)S(1)}, u32[]{:S(2)}, u32[]{:S(2)}) collective-permute-start(bf16[80,5120]{1,0:T(8,128)(2,1)S(1)} %collective-permute-done.7.refs_2_), channel_id=1, source_target_pairs={{0,1},{1,0},{2,3},{3,2},{4,5},{5,4},{6,7},{7,6}} | collective-permute-start | bytes 2457608 | tf_op jit(solution)/shard_map/ppermute | solution.py:311
  619.3 4.7 collective-permute-start.68
  619.8 38.0 %collective-permute-start.48 = (bf16[640,1280]{1,0:T(8,128)(2,1)}, bf16[640,1280]{1,0:T(8,128)(2,1)S(1)}, u32[]{:S(2)}, u32[]{:S(2)}) collective-permute-start(bf16[640,1280]{1,0:T(8,128)(2,1)} %collective-permute-done.47.refs_2_), channel_id=1, source_target_pairs={{0,4},{1,5},{2,6},{3,7},{4,0},{5,1},{6,2},{7,3}} | collective-permute-start | bytes 4915208 | tf_op jit(solution)/shard_map/ppermute | solution.py:311
  620.9 37.9 %collective-permute-start.34 = (bf16[160,5120]{1,0:T(8,128)(2,1)}, bf16[160,5120]{1,0:T(8,128)(2,1)S(1)}, u32[]{:S(2)}, u32[]{:S(2)}) collective-permute-start(bf16[160,5120]{1,0:T(8,128)(2,1)} %collective-permute-done.24.refs_2_), channel_id=1, source_target_pairs={{0,1},{1,0},{2,3},{3,2},{4,5},{5,4},{6,7},{7,6}} | collective-permute-start | bytes 4915208 | tf_op jit(solution)/shard_map/ppermute | solution.py:311
  621.6 38.5 %collective-permute-start.33 = (bf16[160,5120]{1,0:T(8,128)(2,1)}, bf16[160,5120]{1,0:T(8,128)(2,1)S(1)}, u32[]{:S(2)}, u32[]{:S(2)}) collective-permute-start(bf16[160,5120]{1,0:T(8,128)(2,1)} %collective-permute-done.31.refs_1_), channel_id=1, source_target_pairs={{0,1},{1,0},{2,3},{3,2},{4,5},{5,4},{6,7},{7,6}} | collective-permute-start | bytes 4915208 | tf_op jit(solution)/shard_map/ppermute | solution.py:311
  621.7 38.4 %collective-permute-start.29 = (bf16[160,5120]{1,0:T(8,128)(2,1)}, bf16[160,5120]{1,0:T(8,128)(2,1)S(1)}, u32[]{:S(2)}, u32[]{:S(2)}) collective-permute-start(bf16[160,5120]{1,0:T(8,128)(2,1)} %collective-permute-done.21.refs_1_), channel_id=1, source_target_pairs={{0,1},{1,0},{2,3},{3,2},{4,5},{5,4},{6,7},{7,6}} | collective-permute-start | bytes 4915208 | tf_op jit(solution)/shard_map/ppermute | solution.py:311
  623.9 37.0 %collective-permute-start.30 = (bf16[160,5120]{1,0:T(8,128)(2,1)}, bf16[160,5120]{1,0:T(8,128)(2,1)S(1)}, u32[]{:S(2)}, u32[]{:S(2)}) collective-permute-start(bf16[160,5120]{1,0:T(8,128)(2,1)} %copy-done.19), channel_id=1, source_target_pairs={{0,1},{1,0},{2,3},{3,2},{4,5},{5,4},{6,7},{7,6}} | collective-permute-start | bytes 4915208 | tf_op jit(solution)/shard_map/ppermute | solution.py:311
  657.8 37.1 %collective-permute-start.25 = (bf16[160,5120]{1,0:T(8,128)(2,1)}, bf16[160,5120]{1,0:T(8,128)(2,1)S(1)}, u32[]{:S(2)}, u32[]{:S(2)}) collective-permute-start(bf16[160,5120]{1,0:T(8,128)(2,1)} %collective-permute-done.24.refs_2_), channel_id=1, source_target_pairs={{0,4},{1,5},{2,6},{3,7},{4,0},{5,1},{6,2},{7,3}} | collective-permute-start | bytes 4915208 | tf_op jit(solution)/shard_map/ppermute | solution.py:311
  658.8 38.9 %collective-permute-start.22 = (bf16[160,5120]{1,0:T(8,128)(2,1)}, bf16[160,5120]{1,0:T(8,128)(2,1)S(1)}, u32[]{:S(2)}, u32[]{:S(2)}) collective-permute-start(bf16[160,5120]{1,0:T(8,128)(2,1)} %collective-permute-done.21.refs_1_), channel_id=1, source_target_pairs={{0,2},{1,3},{2,0},{3,1},{4,6},{5,7},{6,4},{7,5}} | collective-permute-start | bytes 4915208 | tf_op jit(solution)/shard_map/ppermute | solution.py:311
  660.1 38.8 %collective-permute-start.11 = (bf16[160,5120]{1,0:T(8,128)(2,1)S(1)}, bf16[160,5120]{1,0:T(8,128)(2,1)S(1)}, u32[]{:S(2)}, u32[]{:S(2)}) collective-permute-start(bf16[160,5120]{1,0:T(8,128)(2,1)S(1)} %collective-permute-done.refs_1_), channel_id=1, source_target_pairs={{0,1},{1,0},{2,3},{3,2},{4,5},{5,4},{6,7},{7,6}} | collective-permute-start | bytes 4915208 | tf_op jit(solution)/shard_map/ppermute | solution.py:311
  660.1 70.7 %collective-permute-start.1 = (bf16[160,5120]{1,0:T(8,128)(2,1)S(1)}, bf16[160,5120]{1,0:T(8,128)(2,1)}, u32[]{:S(2)}, u32[]{:S(2)}) collective-permute-start(bf16[160,5120]{1,0:T(8,128)(2,1)S(1)} %collective-permute-done.refs_1_), channel_id=1, source_target_pairs={{0,2},{1,3},{2,0},{3,1},{4,6},{5,7},{6,4},{7,5}} | collective-permute-start | bytes 4915208 | tf_op jit(solution)/shard_map/ppermute | solution.py:311
  660.9 69.9 %collective-permute-start.12 = (bf16[160,5120]{1,0:T(8,128)(2,1)S(1)}, bf16[160,5120]{1,0:T(8,128)(2,1)S(1)}, u32[]{:S(2)}, u32[]{:S(2)}) collective-permute-start(bf16[160,5120]{1,0:T(8,128)(2,1)S(1)} %collective-permute-done.9.refs_2_), channel_id=1, source_target_pairs={{0,1},{1,0},{2,3},{3,2},{4,5},{5,4},{6,7},{7,6}} | collective-permute-start | bytes 4915208 | tf_op jit(solution)/shard_map/ppermute | solution.py:311
  694.8 36.5 %collective-permute-start.49 = (bf16[640,1280]{1,0:T(8,128)(2,1)S(1)}, bf16[640,1280]{1,0:T(8,128)(2,1)S(1)}, u32[]{:S(2)}, u32[]{:S(2)}) collective-permute-start(bf16[640,1280]{1,0:T(8,128)(2,1)S(1)} %collective-permute-done.48.refs_0_), channel_id=1, source_target_pairs={{0,1},{1,0},{2,3},{3,2},{4,5},{5,4},{6,7},{7,6}} | collective-permute-start | bytes 4915208 | tf_op jit(solution)/shard_map/ppermute | solution.py:311
  697.7 34.9 %collective-permute-start.26 = (bf16[160,5120]{1,0:T(8,128)(2,1)S(1)}, bf16[160,5120]{1,0:T(8,128)(2,1)S(1)}, u32[]{:S(2)}, u32[]{:S(2)}) collective-permute-start(bf16[160,5120]{1,0:T(8,128)(2,1)S(1)} %collective-permute-done.25.refs_0_), channel_id=1, source_target_pairs={{0,1},{1,0},{2,3},{3,2},{4,5},{5,4},{6,7},{7,6}} | collective-permute-start | bytes 4915208 | tf_op jit(solution)/shard_map/ppermute | solution.py:311
  698.9 35.4 %collective-permute-start.23 = (bf16[160,5120]{1,0:T(8,128)(2,1)S(1)}, bf16[160,5120]{1,0:T(8,128)(2,1)S(1)}, u32[]{:S(2)}, u32[]{:S(2)}) collective-permute-start(bf16[160,5120]{1,0:T(8,128)(2,1)S(1)} %collective-permute-done.22.refs_0_), channel_id=1, source_target_pairs={{0,1},{1,0},{2,3},{3,2},{4,5},{5,4},{6,7},{7,6}} | collective-permute-start | bytes 4915208 | tf_op jit(solution)/shard_map/ppermute | solution.py:311
  730.9 64.3 %collective-permute-start.2 = (bf16[160,5120]{1,0:T(8,128)(2,1)}, bf16[160,5120]{1,0:T(8,128)(2,1)}, u32[]{:S(2)}, u32[]{:S(2)}) collective-permute-start(bf16[160,5120]{1,0:T(8,128)(2,1)} %collective-permute-done.1.refs_0_), channel_id=1, source_target_pairs={{0,1},{1,0},{2,3},{3,2},{4,5},{5,4},{6,7},{7,6}} | collective-permute-start | bytes 4915208 | tf_op jit(solution)/shard_map/ppermute | solution.py:311
  730.9 68.0 %collective-permute-start.46 = (bf16[160,1280]{1,0:T(8,128)(2,1)}, bf16[160,1280]{1,0:T(8,128)(2,1)}, u32[]{:S(2)}, u32[]{:S(2)}) collective-permute-start(bf16[160,1280]{1,0:T(8,128)(2,1)} %copy-done.12), channel_id=1, source_target_pairs={{0,1},{1,0},{2,3},{3,2},{4,5},{5,4},{6,7},{7,6}} | collective-permute-start | bytes 1228808 | tf_op jit(solution)/shard_map/ppermute | solution.py:311
  732.6 66.3 %collective-permute-start.43 = (bf16[160,1280]{1,0:T(8,128)(2,1)}, bf16[160,1280]{1,0:T(8,128)(2,1)}, u32[]{:S(2)}, u32[]{:S(2)}) collective-permute-start(bf16[160,1280]{1,0:T(8,128)(2,1)} %copy-done.16), channel_id=1, source_target_pairs={{0,1},{1,0},{2,3},{3,2},{4,5},{5,4},{6,7},{7,6}} | collective-permute-start | bytes 1228808 | tf_op jit(solution)/shard_map/ppermute | solution.py:311
  733.8 67.5 %collective-permute-start.40 = (bf16[160,1280]{1,0:T(8,128)(2,1)}, bf16[160,1280]{1,0:T(8,128)(2,1)}, u32[]{:S(2)}, u32[]{:S(2)}) collective-permute-start(bf16[160,1280]{1,0:T(8,128)(2,1)} %copy-done.14), channel_id=1, source_target_pairs={{0,1},{1,0},{2,3},{3,2},{4,5},{5,4},{6,7},{7,6}} | collective-permute-start | bytes 1228808 | tf_op jit(solution)/shard_map/ppermute | solution.py:311
  735.5 65.8 %collective-permute-start.37 = (bf16[160,1280]{1,0:T(8,128)(2,1)}, bf16[160,1280]{1,0:T(8,128)(2,1)}, u32[]{:S(2)}, u32[]{:S(2)}) collective-permute-start(bf16[160,1280]{1,0:T(8,128)(2,1)} %collective-permute-done.36.refs_0_), channel_id=1, source_target_pairs={{0,1},{1,0},{2,3},{3,2},{4,5},{5,4},{6,7},{7,6}} | collective-permute-start | bytes 1228808 | tf_op jit(solution)/shard_map/ppermute | solution.py:311
  (58 other events, 993.8 us)

commit v4 on v3

--- a/solution.py
+++ b/solution.py
@@ -51,14 +51,16 @@
     acc[...] += lax.fori_loop(0, dst.shape[0] // 16, body, jnp.zeros((16, 128), F32))
 
 
-def sum_kernel(shapes, *refs):
-    g, refs = refs[:3], refs[3:]
-    out, squares, refs = refs[:3], refs[3], refs[4:]
+def sum_kernel(shapes, count, head, *refs):
+    g, (w0, m0, v0), refs = refs[:3], refs[3:6], refs[6:]
+    out, squares, new0, refs = refs[:3], refs[3], refs[4], refs[5:]
     near, refs = refs[:3], refs[3:]
     snd, rcv, own, par, refs = refs[0:2], refs[2:4], refs[4:6], refs[6:8], refs[8:]
-    acc, norms, d2d_s, d2d_r, link_s, link_r, own_sem, par_sem, out_sem, norm_s, norm_r = refs
+    first, refs = refs[:4], refs[4:]
+    acc, norms, d2d_s, d2d_r, link_s, link_r, own_sem, par_sem, out_sem, norm_s, norm_r, first_sem = refs
     layers = g[0].shape[1]
     units = [(a, l) for a in range(3) for l in range(layers)]
+    end = len(units) - 1
     kind = [0, 0, 1]
     slot = {}
     for a, l in units:
@@ -71,92 +73,144 @@
     others = [lax.rem(me + k, 8) for k in range(1, 8)]
     for d in others:
         pl.semaphore_signal(barrier, inc=1, device_id=(rep, d), device_id_type=MESH)
-    pl.semaphore_wait(barrier, 7)
-
-    def half_of(u, device, h):
+
+    mine = pl.ds(pl.multiple_of(me * shapes[0][0], 16), head)
+    ahead = [
+        pltpu.make_async_copy(w0.at[0, mine], first[0], first_sem.at[0]),
+        pltpu.make_async_copy(m0.at[0, pl.ds(0, head)], first[1], first_sem.at[1]),
+        pltpu.make_async_copy(v0.at[0, pl.ds(0, head)], first[2], first_sem.at[2]),
+    ]
+
+    def split(i, j):
+        n = shapes[units[i][0]][0] // 2
+        if i == 0 and j < 2:
+            return [(0, 16), (16, n - 16)]
+        if i == end and j >= 4:
+            return [(0, n - n // 5), (n - n // 5, n // 5)]
+        return [(0, n)]
+
+    d2d = {}
+
+    def cut(s, h):
+        return {(0, 0): 0, (0, 1): 1, (1, 0): 2, (2, 1): 3, (1, 1): 4, (2, 0): 5}.get((s, h))
+
+    def rows(u, device, h, piece):
         a, l = u
         n = shapes[a][0] // 2
-        return g[a].at[0, l, pl.ds(pl.multiple_of(device * (2 * n) + h * n, 16), n)]
-
-    d2d = {}
+        return g[a].at[0, l, pl.ds(pl.multiple_of(device * (2 * n) + h * n + piece[0], 16), piece[1])]
+
+    sends = []
     for i, u in enumerate(units):
-        for s, (dx, dy) in enumerate(CHIPS):
-            for h in range(2):
-                d2d[i, s, h] = pltpu.make_async_remote_copy(
-                    src_ref=half_of(u, place(dx, dy, 1), h),
-                    dst_ref=near[u[0]].at[u[1], s, h],
-                    send_sem=d2d_s.at[i, s, h],
-                    recv_sem=d2d_r.at[i, s, h],
-                    device_id=(rep, cn),
-                    device_id_type=MESH,
-                )
-                d2d[i, s, h].start()
+        n = shapes[u[0]][0] // 2
+        halves = [(s, h) for s in range(4) for h in range(2)]
+        todo = [(s, h, p) for s, h in halves for p in (split(i, cut(s, h)) if i == 0 and s == 0 else [(0, n)])]
+        if i == 0:
+            todo.sort(key=lambda one: one[2] != (0, 16))
+        sends += [(i, *one) for one in todo]
+    for k, (i, s, h, p) in enumerate(sends):
+        a, l = units[i]
+        d2d[i, s, h, p] = pltpu.make_async_remote_copy(
+            src_ref=rows(units[i], place(*CHIPS[s], 1), h, p),
+            dst_ref=near[a].at[l, s, h, pl.ds(*p)],
+            send_sem=d2d_s.at[k],
+            recv_sem=d2d_r.at[k],
+            device_id=(rep, cn),
+            device_id_type=MESH,
+        )
 
     tasks = []
-    for i in range(len(units)):
-        tasks += [(i, 0, 0, (), 0), (i, 0, 1, (), 1), (i, 1, 0, (), 2), (i, 2, 1, (), 3)]
-    for i in range(len(units)):
-        tasks += [(i, 1, 1, (1,), 4), (i, 2, 0, (0,), 5)]
-    for i in range(len(units)):
-        tasks += [(i, 3, 0, (2, 5), None), (i, 3, 1, (3, 4), None)]
-
-    link = {}
-
-    def link_copy(i, j):
+    for i in range(end + 1):
+        both = [(i, s, h, p, (), j) for j, s, h in ((0, 0, 0), (1, 0, 1)) for p in split(i, j)]
+        both.sort(key=lambda one: one[3][0])
+        tasks += both + [(i, s, h, p, (), j) for j, s, h in ((2, 1, 0), (3, 2, 1)) for p in split(i, j)]
+    for i in range(end + 1):
+        for p4, p5 in zip(split(i, 4), split(i, 5)):
+            tasks += [(i, 1, 1, p4, (1,), 4), (i, 2, 0, p5, (0,), 5)]
+    for i in range(end + 1):
+        for p4, p5 in zip(split(i, 4), split(i, 5)):
+            tasks += [(i, 3, 0, p5, (2, 5), None), (i, 3, 1, p4, (3, 4), None)]
+
+    numbers = {key: k for k, key in enumerate((i, j, p) for i in range(end + 1) for j in range(6) for p in split(i, j))}
+
+    def link(i, j, p):
         a, l = units[i]
         k = kind[a]
         return pltpu.make_async_remote_copy(
-            src_ref=snd[k].at[slot[a, l], j % 4],
-            dst_ref=rcv[k].at[slot[a, l], j],
-            send_sem=link_s.at[i, j],
-            recv_sem=link_r.at[i, j],
+            src_ref=snd[k].at[slot[a, l], j % 4, pl.ds(*p)],
+            dst_ref=rcv[k].at[slot[a, l], j, pl.ds(*p)],
+            send_sem=link_s.at[numbers[i, j, p]],
+            recv_sem=link_r.at[numbers[i, j, p]],
             device_id=(rep, xn if j % 2 == 0 else yn),
             device_id_type=MESH,
         )
 
+    done = set()
+
+    def once(what, wait):
+        if what not in done:
+            done.add(what)
+            wait()
+
+    def arrived(i, j, piece):
+        for p in split(i, j):
+            if p[0] < piece[0] + piece[1] and piece[0] < p[0] + p[1]:
+                once(("arrived", i, j, p), lambda: link(i, j, p).wait_recv())
+
+    def left(i, j):
+        for p in split(i, j):
+            once(("left", i, j, p), lambda: link(i, j, p).wait_send())
+
     loads = {}
 
-    def load(t):
-        i, s, h, _, _ = tasks[t]
+    def load_mine(t):
+        i, s, h, p, _, _ = tasks[t]
+        k, b = kind[units[i][0]], t % 2
+        loads[t] = [pltpu.make_async_copy(rows(units[i], place(*CHIPS[s], 0), h, p), own[k].at[b, pl.ds(0, p[1])], own_sem.at[b])]
+        loads[t][0].start()
+
+    def load_theirs(t):
+        i, s, h, p, _, _ = tasks[t]
+        a, l = units[i]
+        k, b = kind[a], t % 2
+        whole = p if (i, s, h, p) in d2d else (0, shapes[a][0] // 2)
+        once(("near", i, s, h, whole), d2d[i, s, h, whole].wait_recv)
+        loads[t] += [pltpu.make_async_copy(near[a].at[l, s, h, pl.ds(*p)], par[k].at[b, pl.ds(0, p[1])], par_sem.at[b])]
+        loads[t][1].start()
+
+    load_mine(0)
+    acc[...] = jnp.zeros_like(acc)
+    pl.semaphore_wait(barrier, 7)
+    for one in d2d.values():
+        one.start()
+    for one in ahead:
+        one.start()
+    load_theirs(0)
+    stores = []
+    for t, (i, s, h, p, added, j) in enumerate(tasks):
+        if t + 1 < len(tasks):
+            load_mine(t + 1)
+            load_theirs(t + 1)
         a, l = units[i]
         k = kind[a]
-        b = t % 2
-        mine = pltpu.make_async_copy(half_of(units[i], place(*CHIPS[s], 0), h), own[k].at[b], own_sem.at[b])
-        mine.start()
-        d2d[i, s, h].wait_recv()
-        theirs = pltpu.make_async_copy(near[a].at[l, s, h], par[k].at[b], par_sem.at[b])
-        theirs.start()
-        loads[t] = (mine, theirs)
-
-    acc[...] = jnp.zeros_like(acc)
-    load(0)
-    stores = []
-    for t, (i, s, h, arrived, j) in enumerate(tasks):
-        if t + 1 < len(tasks):
-            load(t + 1)
-        a, l = units[i]
-        k = kind[a]
-        lanes = shapes[a][1]
         for one in loads[t]:
             one.wait()
-        for r in arrived:
-            link_copy(i, r).wait_recv()
-        parts = [own[k].at[t % 2], par[k].at[t % 2]] + [rcv[k].at[slot[a, l], r] for r in arrived]
+        for r in added:
+            arrived(i, r, p)
+        parts = [own[k].at[t % 2, pl.ds(0, p[1])], par[k].at[t % 2, pl.ds(0, p[1])]]
+        parts += [rcv[k].at[slot[a, l], r, pl.ds(*p)] for r in added]
         if j is None:
-            dst = snd[k].at[slot[a, l], 2 + h]
-            link[i, 2 + h].wait_send()
-            add_square(dst, parts, lanes, acc)
-            n = shapes[a][0] // 2
-            store = pltpu.make_async_copy(dst, out[a].at[l, pl.ds(h * n, n)], out_sem.at[i, h])
+            dst = snd[k].at[slot[a, l], 2 + h, pl.ds(*p)]
+            left(i, 2 + h)
+            add_square(dst, parts, shapes[a][1], acc)
+            store = pltpu.make_async_copy(dst, out[a].at[l, pl.ds(h * (shapes[a][0] // 2) + p[0], p[1])], out_sem.at[len(stores)])
             store.start()
             stores.append(store)
         else:
-            dst = snd[k].at[slot[a, l], j % 4]
+            dst = snd[k].at[slot[a, l], j % 4, pl.ds(*p)]
             if j >= 4:
-                link[i, j - 4].wait_send()
+                left(i, j - 4)
             add_into(dst, parts)
-            link[i, j] = link_copy(i, j)
-            link[i, j].start()
+            link(i, j, p).start()
 
     sent = []
     for k in range(1, 8):
@@ -167,65 +221,82 @@
         copy.start()
         sent.append(copy)
     norms[me] = acc[...]
+    for one in ahead:
+        one.wait()
+    for store in stores:
+        store.wait()
+    for copy in d2d.values():
+        copy.wait_send()
+    for i in range(end + 1):
+        for j in range(6):
+            left(i, j)
     for copy in sent:
         copy.wait_recv()
     total = norms[0]
     for d in range(1, 8):
         total = total + norms[d]
-    squares[...] = jnp.full(squares.shape, jnp.sum(total), F32)
+    total = jnp.sum(total, axis=0, keepdims=True)
+    total = jnp.sum(total, axis=1, keepdims=True)
+    squares[...] = jnp.broadcast_to(total, squares.shape)
+
+    half = snd[0].at[slot[0, 0], 2]
+
+    def body(i, carry):
+        r = pl.ds(pl.multiple_of(i * 16, 16), 16)
+        first[3][r, :] = stepped_block(total, count, half[r, :], first[0][r, :], first[1][r, :], first[2][r, :])[0]
+        return carry
+
+    lax.fori_loop(0, head // 16, body, 0)
+    last = pltpu.make_async_copy(first[3], new0, first_sem.at[3])
+    last.start()
     for copy in sent:
         copy.wait_send()
-    for store in stores:
-        store.wait()
-    for copy in d2d.values():
-        copy.wait_send()
-    for i in range(len(units)):
-        for j in (4, 5):
-            link[i, j].wait_send()
-
-
-def summed(terms):
+    last.wait()
+
+
+def summed(terms, count, head, w, m, v):
     layers = terms[0].shape[1]
     shapes = [(t.shape[2] // 8, t.shape[3]) for t in terms]
     halves = [(shapes[0][0] // 2, shapes[0][1]), (shapes[2][0] // 2, shapes[2][1])]
-    count = [2 * layers, layers]
+    counts = [2 * layers, layers]
     any_ = pl.BlockSpec(memory_space=pl.ANY)
     outs = pl.pallas_call(
-        functools.partial(sum_kernel, shapes),
+        functools.partial(sum_kernel, shapes, count, head),
         out_shape=[jax.ShapeDtypeStruct((layers, *s), BF16) for s in shapes]
         + [jax.ShapeDtypeStruct((8, 128), F32)]
+        + [jax.ShapeDtypeStruct((head, shapes[0][1]), BF16)]
         + [jax.ShapeDtypeStruct((layers, 4, 2, s[0] // 2, s[1]), BF16) for s in shapes],
-        in_specs=[any_] * 3,
-        out_specs=[any_] * 3 + [pl.BlockSpec(memory_space=pltpu.VMEM)] + [any_] * 3,
-        scratch_shapes=[pltpu.VMEM((n, 4, *s), BF16) for n, s in zip(count, halves)]
-        + [pltpu.VMEM((n, 6, *s), BF16) for n, s in zip(count, halves)]
+        in_specs=[any_] * 6,
+        out_specs=[any_] * 3 + [pl.BlockSpec(memory_space=pltpu.VMEM)] + [any_] * 4,
+        scratch_shapes=[pltpu.VMEM((n, 4, *s), BF16) for n, s in zip(counts, halves)]
+        + [pltpu.VMEM((n, 6, *s), BF16) for n, s in zip(counts, halves)]
         + [pltpu.VMEM((2, *s), BF16) for s in halves] * 2
+        + [pltpu.VMEM((head, shapes[0][1]), t) for t in (BF16, F32, F32, BF16)]
         + [
             pltpu.VMEM((16, 128), F32),
             pltpu.VMEM((8, 16, 128), F32),
-            pltpu.SemaphoreType.DMA((3 * layers, 4, 2)),
-            pltpu.SemaphoreType.DMA((3 * layers, 4, 2)),
-            pltpu.SemaphoreType.DMA((3 * layers, 6)),
-            pltpu.SemaphoreType.DMA((3 * layers, 6)),
+            pltpu.SemaphoreType.DMA((24 * layers + 2,)),
+            pltpu.SemaphoreType.DMA((24 * layers + 2,)),
+            pltpu.SemaphoreType.DMA((18 * layers + 4,)),
+            pltpu.SemaphoreType.DMA((18 * layers + 4,)),
             pltpu.SemaphoreType.DMA((2,)),
             pltpu.SemaphoreType.DMA((2,)),
-            pltpu.SemaphoreType.DMA((3 * layers, 2)),
+            pltpu.SemaphoreType.DMA((6 * layers + 2,)),
             pltpu.SemaphoreType.DMA((7,)),
             pltpu.SemaphoreType.DMA((7,)),
+            pltpu.SemaphoreType.DMA((4,)),
         ],
         compiler_params=pltpu.CompilerParams(collective_id=0, has_side_effects=True, vmem_limit_bytes=62 * 1024 * 1024),
         name="sum_terms",
-    )(*terms)
-    return outs[:3], outs[3]
+    )(*terms, w, m, v)
+    return outs[:3], outs[3], outs[4]
 
 
 def step_kernel(count, with_weight, me, squares, g, w, m, v, *rest):
-    new_w, new_m, new_v = rest[-3:]
-    w, m, v = stepped_block(squares[:1, :1], count, g[0], w[0], m[0], v[0])
+    new = stepped_block(squares[:1, :1], count, g[0], w[0], m[0], v[0])
+    rest[-2][0], rest[-1][0] = new[1:]
     if with_weight:
-        new_w[...] = w
-    new_m[0] = m
-    new_v[0] = v
+        rest[-3][...] = new[0]
 
 
 def stepped_block(squares, count, g, w, m, v):
@@ -237,7 +308,7 @@
     return (w - 0.02 * step).astype(BF16), m, v
 
 
-def stepped(me, squares, count, unit, g, w, m, v, before):
+def stepped(me, squares, count, unit, g, w, m, v, before, with_weight):
     layer, start, rows = unit
     whole, lanes = g.shape[1:]
     n = rows // 5
@@ -251,15 +322,15 @@
     ]
     moment = jax.ShapeDtypeStruct(m.shape, F32)
     return pl.pallas_call(
-        functools.partial(step_kernel, count, True),
-        out_shape=[jax.ShapeDtypeStruct((rows, lanes), BF16), moment, moment],
+        functools.partial(step_kernel, count, with_weight),
+        out_shape=[jax.ShapeDtypeStruct((rows, lanes), BF16)] * with_weight + [moment, moment],
         grid_spec=pltpu.PrefetchScalarGridSpec(
             num_scalar_prefetch=1,
             grid=(rows // n,),
             in_specs=specs + [pl.BlockSpec(memory_space=pl.ANY)] * len(before),
-            out_specs=[pl.BlockSpec((n, lanes), lambda i, me: (i, 0)), here, here],
+            out_specs=[pl.BlockSpec((n, lanes), lambda i, me: (i, 0))] * with_weight + [here, here],
         ),
-        input_output_aliases={6 + i: 1 + i for i in range(len(before))},
+        input_output_aliases={6 + i: with_weight + i for i in range(len(before))},
         cost_estimate=pl.CostEstimate(flops=15 * rows * lanes, bytes_accessed=22 * rows * lanes, transcendentals=rows * lanes),
         name="adamw",
     )(me, squares, g, w, m, v, *before)
@@ -332,14 +403,15 @@
 
     def step(*arrays):
         terms, weights, m, v = (arrays[i : i + 3] for i in (0, 3, 6, 9))
-        gradients, squares = summed(terms)
-        count = 8 * sum(g.size for g in gradients)
+        count = 8 * sum(one.size for one in m)
+        gradients, squares, head = summed(terms, count, units[0][3], weights[0], m[0], v[0])
         me = lax.axis_index("dp")[None]
         new_m, new_v, whole = [()] * 3, [()] * 3, [()] * 3
         first, second = [], []
-        for a, *unit in units:
+        for i, (a, *unit) in enumerate(units):
             before = (new_m[a], new_v[a]) if len(new_m[a]) else ()
-            own, new_m[a], new_v[a] = stepped(me, squares, count, unit, gradients[a], weights[a], m[a], v[a], before)
+            *own, new_m[a], new_v[a] = stepped(me, squares, count, unit, gradients[a], weights[a], m[a], v[a], before, i > 0)
+            own = own[0] if own else head
             first.append((own, send(own, dx=1), send(own, dy=1), send(own, dc=1)))
         for i, (own, x, y, c) in enumerate(first):
             far = send(y, dx=1) if i % 2 else send(x, dy=1)

time: 806 us -> 798 us (0.990)
  transfers between devices with their start and end apart: 70 -> 70, of which waited for: 28 -> 27; matrix products, arithmetic and copies ran while one was open for 0% -> 0% of each run, Pallas kernels for 14% -> 14%
where the time goes in v4:
time: 798 us; the launch traced here: 796 us
  Pallas kernels  464 us (58%)
  waiting for transfers between devices  284 us (36%)
  starting transfers between devices  36.3 us (5%)
  local copies, waits for them, and re-layouts  10.7 us (1%)
    pallas_call x1, Pallas kernels, summed(): pl.pallas_call(functools.partial(sum_kernel, shapes, count, head), out_sh...  333 us
    ppermute x70, waiting for transfers between devices, send(): return lax.ppermute(block, 'dp', [(d, d ^ flip) for d in range(8)])  284 us
    pallas_call x10, Pallas kernels, stepped(): pl.pallas_call(functools.partial(step_kernel, count, with_weight), out_sh...  66.9 us
    pallas_call x17, Pallas kernels, placed(): pl.pallas_call(functools.partial(place_kernel, places, len(before), in_vm...  64.6 us
    ppermute x70, starting transfers between devices, send(): return lax.ppermute(block, 'dp', [(d, d ^ flip) for d in range(8)])  36.3 us
  transfers between devices with their start and end apart: 70, of which 27 were waited for; matrix products, arithmetic and copies ran while one was open for 0% of the time, Pallas kernels for 14%

profile of v4, /device:TPU:0, one launch (start us, length us, event | category | flops | bytes accessed | tf_op | source)
XLA Modules:
  0.0 796.5 jit_solution(6378270535275463794)
XLA Ops:
  0.6 332.9 %sum_terms.1 = (bf16[2,160,5120]{2,1,0:T(8,128)(2,1)}, bf16[2,160,5120]{2,1,0:T(8,128)(2,1)}, bf16[2,640,1280]{2,1,0:T(8,128)(2,1)}, f32[8,128]{1,0:T(8,128)}, b...) custom-call(bf16[1,2,1280,5120]{3,2,1,0:T(8,128)(2,1)} %refs_0_.1, ...), custom_call_target="tpu_custom_call" | custom-call | tf_op jit(solution)/shard_map/sum_terms/pallas_call | solution.py:263
  333.5 9.0 %adamw.15 = (bf16[640,1280]{1,0:T(8,128)(2,1)}, f32[2,640,1280]{2,1,0:T(8,128)}, f32[2,640,1280]{2,1,0:T(8,128)}) custom-call(s32[1]{0:T(128)} %bitcast.me, f32[8,128]{1,0:T(8,128)} %get-tuple-element.43.squares, bf16[2,640,1280]{2,1,0:T(8,128)(2,1)} %get-tuple-element.57.g, bf16[2,5120,1280]{2,1,0:T(8,128)(2,1)} %w.19, f32[2,640,1280]{2,1,0:T(8,128)} %m.19, ...), custom_call_target="tpu_custom_call" | custom-call | flops 12288000 | bytes 18022400 | tf_op jit(solution)/shard_map/adamw/pallas_call | solution.py:324
  342.5 4.7 adamw.16
  347.2 1.3 collective-permute-start.41
  349.3 4.7 adamw.17
  354.0 1.1 collective-permute-start.58
  356.0 4.7 adamw.18
  362.9 4.7 adamw.19
  368.6 1.3 collective-permute-done.44.refs_2_
  370.6 1.1 collective-permute-start.38
  371.7 5.7 collective-permute-done.35.refs_1_
  377.4 1.3 collective-permute-done.54.refs_2_
  379.2 6.1 collective-permute-done.50.refs_1_
  391.0 5.9 adamw.10
  396.9 6.2 adamw.11
  403.1 1.2 collective-permute-start.6
  406.2 2.9 collective-permute-done.39.refs_2_
  410.1 21.5 %collective-permute-done.36.refs_0_ = bf16[160,1280]{1,0:T(8,128)(2,1)} collective-permute-done((bf16[160,1280]{1,0:T(8,128)(2,1)}, bf16[160,1280]{1,0:T(8,128)(2,1)}, u32[]{:S(2)}, u32[]{:S(2)}) %collective-permute-start.36) | collective-permute-done | bytes 409632 | tf_op jit(solution)/shard_map/ppermute | solution.py:382
  431.6 1.2 collective-permute-start.17
  432.8 9.1 %adamw.13 = (bf16[160,5120]{1,0:T(8,128)(2,1)}, f32[2,160,5120]{2,1,0:T(8,128)}, f32[2,160,5120]{2,1,0:T(8,128)}) custom-call(s32[1]{0:T(128)} %bitcast.me, f32[8,128]{1,0:T(8,128)} %get-tuple-element.43.squares, bf16[2,160,5120]{2,1,0:T(8,128)(2,1)} %get-tuple-element.52.g, bf16[2,1280,5120]{2,1,0:T(8,128)(2,1)} %w.14, f32[2,160,5120]{2,1,0:T(8,128)} %m.14, ...), custom_call_target="tpu_custom_call" | custom-call | flops 12288000 | bytes 18022400 | tf_op jit(solution)/shard_map/adamw/pallas_call | solution.py:324
  443.9 1.1 collective-permute-start.24
  445.0 8.0 %collective-permute-done.17.refs_2_ = bf16[80,5120]{1,0:T(8,128)(2,1)} collective-permute-done((bf16[80,5120]{1,0:T(8,128)(2,1)}, bf16[80,5120]{1,0:T(8,128)(2,1)}, u32[]{:S(2)}, u32[]{:S(2)}) %collective-permute-start.17) | collective-permute-done | bytes 819232 | tf_op jit(solution)/shard_map/ppermute | solution.py:382
  453.1 2.7 collective-permute-done.18.refs_3_
  456.8 9.0 %adamw.14 = (bf16[160,5120]{1,0:T(8,128)(2,1)}, f32[2,160,5120]{2,1,0:T(8,128)}, f32[2,160,5120]{2,1,0:T(8,128)}) custom-call(s32[1]{0:T(128)} %bitcast.me, f32[8,128]{1,0:T(8,128)} %get-tuple-element.43.squares, bf16[2,160,5120]{2,1,0:T(8,128)(2,1)} %get-tuple-element.52.g, ...), custom_call_target="tpu_custom_call", output_to_operand_aliasing={{1}: (6, {}), {2}: (7, {})} | custom-call | flops 12288000 | bytes 18022400 | tf_op jit(solution)/shard_map/adamw/pallas_call | solution.py:324
  465.8 22.4 %collective-permute-done.47.refs_2_ = bf16[640,1280]{1,0:T(8,128)(2,1)} collective-permute-done((bf16[640,1280]{1,0:T(8,128)(2,1)S(1)}, bf16[640,1280]{1,0:T(8,128)(2,1)}, u32[]{:S(2)}, u32[]{:S(2)}) %collective-permute-start.47) | collective-permute-done | bytes 1638432 | tf_op jit(solution)/shard_map/ppermute | solution.py:382
  489.2 1.1 collective-permute-start.27
  490.4 32.9 %collective-permute-done.24.refs_2_ = bf16[160,5120]{1,0:T(8,128)(2,1)} collective-permute-done((bf16[160,5120]{1,0:T(8,128)(2,1)}, bf16[160,5120]{1,0:T(8,128)(2,1)}, u32[]{:S(2)}, u32[]{:S(2)}) %collective-permute-start.24) | collective-permute-done | bytes 1638432 | tf_op jit(solution)/shard_map/ppermute | solution.py:382
  523.3 9.0 %adamw.12 = (bf16[160,5120]{1,0:T(8,128)(2,1)}, f32[2,160,5120]{2,1,0:T(8,128)}, f32[2,160,5120]{2,1,0:T(8,128)}) custom-call(s32[1]{0:T(128)} %bitcast.me, f32[8,128]{1,0:T(8,128)} %get-tuple-element.43.squares, bf16[2,160,5120]{2,1,0:T(8,128)(2,1)} %get-tuple-element.44.g, ...), custom_call_target="tpu_custom_call", output_to_operand_aliasing={{1}: (6, {}), {2}: (7, {})} | custom-call | flops 12288000 | bytes 18022400 | tf_op jit(solution)/shard_map/adamw/pallas_call | solution.py:324
  533.6 18.3 %collective-permute-done.21.refs_1_ = bf16[160,5120]{1,0:T(8,128)(2,1)} collective-permute-done((bf16[160,5120]{1,0:T(8,128)(2,1)}, bf16[160,5120]{1,0:T(8,128)(2,1)}, u32[]{:S(2)}, u32[]{:S(2)}) %collective-permute-start.21) | collective-permute-done | bytes 1638432 | tf_op jit(solution)/shard_map/ppermute | solution.py:382
  551.8 4.0 collective-permute-done.27.refs_2_
  556.3 1.2 collective-permute-start.9
  559.5 1.2 collective-permute-start.4
  560.7 26.1 %collective-permute-done.refs_1_ = bf16[160,5120]{1,0:T(8,128)(2,1)S(1)} collective-permute-done((bf16[160,5120]{1,0:T(8,128)(2,1)}, bf16[160,5120]{1,0:T(8,128)(2,1)S(1)}, u32[]{:S(2)}, u32[]{:S(2)}) %collective-permute-start) | collective-permute-done | bytes 1638432 | tf_op jit(solution)/shard_map/ppermute | solution.py:382
  586.8 14.6 %collective-permute-done.7.refs_2_ = bf16[80,5120]{1,0:T(8,128)(2,1)S(1)} collective-permute-done((bf16[80,5120]{1,0:T(8,128)(2,1)}, bf16[80,5120]{1,0:T(8,128)(2,1)S(1)}, u32[]{:S(2)}, u32[]{:S(2)}) %collective-permute-start.7) | collective-permute-done | bytes 819232 | tf_op jit(solution)/shard_map/ppermute | solution.py:382
  601.4 10.4 %collective-permute-done.4.refs_0_ = bf16[80,5120]{1,0:T(8,128)(2,1)S(1)} collective-permute-done((bf16[80,5120]{1,0:T(8,128)(2,1)}, bf16[80,5120]{1,0:T(8,128)(2,1)S(1)}, u32[]{:S(2)}, u32[]{:S(2)}) %collective-permute-start.4) | collective-permute-done | bytes 819232 | tf_op jit(solution)/shard_map/ppermute | solution.py:382
  614.7 1.8 collective-permute-done.68.refs_4_
  616.6 33.7 %collective-permute-done.48.refs_0_ = bf16[640,1280]{1,0:T(8,128)(2,1)S(1)} collective-permute-done((bf16[640,1280]{1,0:T(8,128)(2,1)}, bf16[640,1280]{1,0:T(8,128)(2,1)S(1)}, u32[]{:S(2)}, u32[]{:S(2)}) %collective-permute-start.48) | collective-permute-done | bytes 1638432 | tf_op jit(solution)/shard_map/ppermute | solution.py:382
  651.4 1.1 collective-permute-start.22
  653.7 33.7 %collective-permute-done.25.refs_0_ = bf16[160,5120]{1,0:T(8,128)(2,1)S(1)} collective-permute-done((bf16[160,5120]{1,0:T(8,128)(2,1)}, bf16[160,5120]{1,0:T(8,128)(2,1)S(1)}, u32[]{:S(2)}, u32[]{:S(2)}) %collective-permute-start.25) | collective-permute-done | bytes 1638432 | tf_op jit(solution)/shard_map/ppermute | solution.py:382
  687.4 1.2 copy-done
  688.5 1.7 collective-permute-done.22.refs_0_
  690.3 1.2 copy-done.2
  692.0 1.3 copy-done.4
  693.2 30.2 %collective-permute-done.1.refs_0_ = bf16[160,5120]{1,0:T(8,128)(2,1)} collective-permute-done((bf16[160,5120]{1,0:T(8,128)(2,1)S(1)}, bf16[160,5120]{1,0:T(8,128)(2,1)}, u32[]{:S(2)}, u32[]{:S(2)}) %collective-permute-start.1) | collective-permute-done | bytes 1638432 | tf_op jit(solution)/shard_map/ppermute | solution.py:382
  723.9 1.2 copy-done.6
  725.2 1.2 copy-done.8
  726.9 1.2 copy-done.10
  728.1 4.2 place.17.refs_6_
  732.3 4.2 place.18.refs_6_
  736.4 7.7 place.26.refs_6_
  744.1 7.7 place.22.refs_6_
  751.7 7.7 place.19.refs_4_
  759.4 1.8 place.20.refs_2_
  761.2 2.5 place.27.refs_6_
  763.7 2.5 place.28.refs_6_
  766.3 2.5 place.29.refs_6_
  768.8 2.5 place.30.refs_2_
  771.4 7.8 place.23.refs_2_
  779.7 1.7 place.31.refs_4_
  782.8 1.7 place.24.refs_2_
  785.9 1.7 place.25
  787.7 3.7 place.21
  791.5 2.4 place.32.refs_4_
  793.9 2.4 place.33
  (208 shorter events, 32.5 us)
Async XLA Ops:
  347.2 13.5 %collective-permute-start.41 = (bf16[160,1280]{1,0:T(8,128)(2,1)}, bf16[160,1280]{1,0:T(8,128)(2,1)S(1)}, u32[]{:S(2)}, u32[]{:S(2)}) collective-permute-start(bf16[160,1280]{1,0:T(8,128)(2,1)} %get-tuple-element.68.refs_0_), channel_id=1, source_target_pairs={{0,4},{1,5},{2,6},{3,7},{4,0},{5,1},{6,2},{7,3}} | collective-permute-start | bytes 1228808 | tf_op jit(solution)/shard_map/ppermute | solution.py:382
  348.5 12.6 %collective-permute-start.62 = (bf16[160,1280]{1,0:T(8,128)(2,1)}, bf16[160,1280]{1,0:T(8,128)(2,1)S(1)}, u32[]{:S(2)}, u32[]{:S(2)}) collective-permute-start(bf16[160,1280]{1,0:T(8,128)(2,1)} %get-tuple-element.68.refs_0_), channel_id=1, source_target_pairs={{0,2},{1,3},{2,0},{3,1},{4,6},{5,7},{6,4},{7,5}} | collective-permute-start | bytes 1228808 | tf_op jit(solution)/shard_map/ppermute | solution.py:382
  349.3 12.8 %collective-permute-start.63 = (bf16[160,1280]{1,0:T(8,128)(2,1)}, bf16[160,1280]{1,0:T(8,128)(2,1)S(1)}, u32[]{:S(2)}, u32[]{:S(2)}) collective-permute-start(bf16[160,1280]{1,0:T(8,128)(2,1)} %get-tuple-element.68.refs_0_), channel_id=1, source_target_pairs={{0,1},{1,0},{2,3},{3,2},{4,5},{5,4},{6,7},{7,6}} | collective-permute-start | bytes 1228808 | tf_op jit(solution)/shard_map/ppermute | solution.py:382
  354.0 14.6 %collective-permute-start.58 = (bf16[160,1280]{1,0:T(8,128)(2,1)}, bf16[160,1280]{1,0:T(8,128)(2,1)S(1)}, u32[]{:S(2)}, u32[]{:S(2)}) collective-permute-start(bf16[160,1280]{1,0:T(8,128)(2,1)} %get-tuple-element.69.refs_0_), channel_id=1, source_target_pairs={{0,4},{1,5},{2,6},{3,7},{4,0},{5,1},{6,2},{7,3}} | collective-permute-start | bytes 1228808 | tf_op jit(solution)/shard_map/ppermute | solution.py:382
  355.1 14.8 %collective-permute-start.44 = (bf16[160,1280]{1,0:T(8,128)(2,1)}, bf16[160,1280]{1,0:T(8,128)(2,1)S(1)}, u32[]{:S(2)}, u32[]{:S(2)}) collective-permute-start(bf16[160,1280]{1,0:T(8,128)(2,1)} %get-tuple-element.69.refs_0_), channel_id=1, source_target_pairs={{0,2},{1,3},{2,0},{3,1},{4,6},{5,7},{6,4},{7,5}} | collective-permute-start | bytes 1228808 | tf_op jit(solution)/shard_map/ppermute | solution.py:382
  360.8 9.8 %collective-permute-start.59 = (bf16[160,1280]{1,0:T(8,128)(2,1)S(1)}, bf16[160,1280]{1,0:T(8,128)(2,1)S(1)}, u32[]{:S(2)}, u32[]{:S(2)}) collective-permute-start(bf16[160,1280]{1,0:T(8,128)(2,1)S(1)} %copy-done.38), channel_id=1, source_target_pairs={{0,1},{1,0},{2,3},{3,2},{4,5},{5,4},{6,7},{7,6}} | collective-permute-start | bytes 1228808 | tf_op jit(solution)/shard_map/ppermute | solution.py:382
  361.1 16.4 %collective-permute-start.35 = (bf16[160,1280]{1,0:T(8,128)(2,1)}, bf16[160,1280]{1,0:T(8,128)(2,1)}, u32[]{:S(2)}, u32[]{:S(2)}) collective-permute-start(bf16[160,1280]{1,0:T(8,128)(2,1)} %get-tuple-element.64.refs_0_), channel_id=1, source_target_pairs={{0,4},{1,5},{2,6},{3,7},{4,0},{5,1},{6,2},{7,3}} | collective-permute-start | bytes 1228808 | tf_op jit(solution)/shard_map/ppermute | solution.py:382
  362.1 16.6 %collective-permute-start.54 = (bf16[160,1280]{1,0:T(8,128)(2,1)}, bf16[160,1280]{1,0:T(8,128)(2,1)}, u32[]{:S(2)}, u32[]{:S(2)}) collective-permute-start(bf16[160,1280]{1,0:T(8,128)(2,1)} %get-tuple-element.64.refs_0_), channel_id=1, source_target_pairs={{0,2},{1,3},{2,0},{3,1},{4,6},{5,7},{6,4},{7,5}} | collective-permute-start | bytes 1228808 | tf_op jit(solution)/shard_map/ppermute | solution.py:382
  368.6 10.2 %collective-permute-start.55 = (bf16[160,1280]{1,0:T(8,128)(2,1)S(1)}, bf16[160,1280]{1,0:T(8,128)(2,1)S(1)}, u32[]{:S(2)}, u32[]{:S(2)}) collective-permute-start(bf16[160,1280]{1,0:T(8,128)(2,1)S(1)} %copy-done.40), channel_id=1, source_target_pairs={{0,1},{1,0},{2,3},{3,2},{4,5},{5,4},{6,7},{7,6}} | collective-permute-start | bytes 1228808 | tf_op jit(solution)/shard_map/ppermute | solution.py:382
  369.8 15.5 %collective-permute-start.50 = (bf16[160,1280]{1,0:T(8,128)(2,1)}, bf16[160,1280]{1,0:T(8,128)(2,1)}, u32[]{:S(2)}, u32[]{:S(2)}) collective-permute-start(bf16[160,1280]{1,0:T(8,128)(2,1)} %get-tuple-element.67.refs_0_), channel_id=1, source_target_pairs={{0,4},{1,5},{2,6},{3,7},{4,0},{5,1},{6,2},{7,3}} | collective-permute-start | bytes 1228808 | tf_op jit(solution)/shard_map/ppermute | solution.py:382
  370.6 15.7 %collective-permute-start.38 = (bf16[160,1280]{1,0:T(8,128)(2,1)}, bf16[160,1280]{1,0:T(8,128)(2,1)S(1)}, u32[]{:S(2)}, u32[]{:S(2)}) collective-permute-start(bf16[160,1280]{1,0:T(8,128)(2,1)} %get-tuple-element.67.refs_0_), channel_id=1, source_target_pairs={{0,2},{1,3},{2,0},{3,1},{4,6},{5,7},{6,4},{7,5}} | collective-permute-start | bytes 1228808 | tf_op jit(solution)/shard_map/ppermute | solution.py:382
  377.4 8.8 %collective-permute-start.51 = (bf16[160,1280]{1,0:T(8,128)(2,1)}, bf16[160,1280]{1,0:T(8,128)(2,1)S(1)}, u32[]{:S(2)}, u32[]{:S(2)}) collective-permute-start(bf16[160,1280]{1,0:T(8,128)(2,1)} %get-tuple-element.67.refs_0_), channel_id=1, source_target_pairs={{0,1},{1,0},{2,3},{3,2},{4,5},{5,4},{6,7},{7,6}} | collective-permute-start | bytes 1228808 | tf_op jit(solution)/shard_map/ppermute | solution.py:382
  378.7 8.1 %collective-permute-start.64 = (bf16[160,1280]{1,0:T(8,128)(2,1)S(1)}, bf16[160,1280]{1,0:T(8,128)(2,1)S(1)}, u32[]{:S(2)}, u32[]{:S(2)}) collective-permute-start(bf16[160,1280]{1,0:T(8,128)(2,1)S(1)} %collective-permute-done.41.refs_1_), channel_id=1, source_target_pairs={{0,1},{1,0},{2,3},{3,2},{4,5},{5,4},{6,7},{7,6}} | collective-permute-start | bytes 1228808 | tf_op jit(solution)/shard_map/ppermute | solution.py:382
  378.7 8.1 %collective-permute-start.65 = (bf16[160,1280]{1,0:T(8,128)(2,1)S(1)}, bf16[160,1280]{1,0:T(8,128)(2,1)S(1)}, u32[]{:S(2)}, u32[]{:S(2)}) collective-permute-start(bf16[160,1280]{1,0:T(8,128)(2,1)S(1)} %collective-permute-done.62.refs_2_), channel_id=1, source_target_pairs={{0,1},{1,0},{2,3},{3,2},{4,5},{5,4},{6,7},{7,6}} | collective-permute-start | bytes 1228808 | tf_op jit(solution)/shard_map/ppermute | solution.py:382
  386.8 3.1 collective-permute-start.57
  386.8 16.2 %collective-permute-start.52 = (bf16[160,1280]{1,0:T(8,128)(2,1)}, bf16[160,1280]{1,0:T(8,128)(2,1)}, u32[]{:S(2)}, u32[]{:S(2)}) collective-permute-start(bf16[160,1280]{1,0:T(8,128)(2,1)} %collective-permute-done.50.refs_1_), channel_id=1, source_target_pairs={{0,1},{1,0},{2,3},{3,2},{4,5},{5,4},{6,7},{7,6}} | collective-permute-start | bytes 1228808 | tf_op jit(solution)/shard_map/ppermute | solution.py:382
  387.3 17.0 %collective-permute-start.53 = (bf16[160,1280]{1,0:T(8,128)(2,1)S(1)}, bf16[160,1280]{1,0:T(8,128)(2,1)}, u32[]{:S(2)}, u32[]{:S(2)}) collective-permute-start(bf16[160,1280]{1,0:T(8,128)(2,1)S(1)} %collective-permute-done.38.refs_2_), channel_id=1, source_target_pairs={{0,1},{1,0},{2,3},{3,2},{4,5},{5,4},{6,7},{7,6}} | collective-permute-start | bytes 1228808 | tf_op jit(solution)/shard_map/ppermute | solution.py:382
  388.0 17.3 %collective-permute-start.45 = (bf16[160,1280]{1,0:T(8,128)(2,1)S(1)}, bf16[160,1280]{1,0:T(8,128)(2,1)S(1)}, u32[]{:S(2)}, u32[]{:S(2)}) collective-permute-start(bf16[160,1280]{1,0:T(8,128)(2,1)S(1)} %collective-permute-done.44.refs_2_), channel_id=1, source_target_pairs={{0,4},{1,5},{2,6},{3,7},{4,0},{5,1},{6,2},{7,3}} | collective-permute-start | bytes 1228808 | tf_op jit(solution)/shard_map/ppermute | solution.py:382
  389.0 17.2 %collective-permute-start.42 = (bf16[160,1280]{1,0:T(8,128)(2,1)S(1)}, bf16[160,1280]{1,0:T(8,128)(2,1)S(1)}, u32[]{:S(2)}, u32[]{:S(2)}) collective-permute-start(bf16[160,1280]{1,0:T(8,128)(2,1)S(1)} %collective-permute-done.41.refs_1_), channel_id=1, source_target_pairs={{0,2},{1,3},{2,0},{3,1},{4,6},{5,7},{6,4},{7,5}} | collective-permute-start | bytes 1228808 | tf_op jit(solution)/shard_map/ppermute | solution.py:382
  389.9 19.2 %collective-permute-start.39 = (bf16[160,1280]{1,0:T(8,128)(2,1)S(1)}, bf16[160,1280]{1,0:T(8,128)(2,1)S(1)}, u32[]{:S(2)}, u32[]{:S(2)}) collective-permute-start(bf16[160,1280]{1,0:T(8,128)(2,1)S(1)} %collective-permute-done.38.refs_2_), channel_id=1, source_target_pairs={{0,4},{1,5},{2,6},{3,7},{4,0},{5,1},{6,2},{7,3}} | collective-permute-start | bytes 1228808 | tf_op jit(solution)/shard_map/ppermute | solution.py:382
  403.1 38.9 %collective-permute-start.6 = (bf16[80,5120]{1,0:T(8,128)(2,1)}, bf16[80,5120]{1,0:T(8,128)(2,1)}, u32[]{:S(2)}, u32[]{:S(2)}) collective-permute-start(bf16[80,5120]{1,0:T(8,128)(2,1)} %get-tuple-element.51.refs_0_), channel_id=1, source_target_pairs={{0,2},{1,3},{2,0},{3,1},{4,6},{5,7},{6,4},{7,5}} | collective-permute-start | bytes 2457608 | tf_op jit(solution)/shard_map/ppermute | solution.py:382
  404.3 38.5 %collective-permute-start.13 = (bf16[80,5120]{1,0:T(8,128)(2,1)}, bf16[80,5120]{1,0:T(8,128)(2,1)}, u32[]{:S(2)}, u32[]{:S(2)}) collective-permute-start(bf16[80,5120]{1,0:T(8,128)(2,1)} %get-tuple-element.51.refs_0_), channel_id=1, source_target_pairs={{0,4},{1,5},{2,6},{3,7},{4,0},{5,1},{6,2},{7,3}} | collective-permute-start | bytes 2457608 | tf_op jit(solution)/shard_map/ppermute | solution.py:382
  405.3 26.4 %collective-permute-start.36 = (bf16[160,1280]{1,0:T(8,128)(2,1)}, bf16[160,1280]{1,0:T(8,128)(2,1)}, u32[]{:S(2)}, u32[]{:S(2)}) collective-permute-start(bf16[160,1280]{1,0:T(8,128)(2,1)} %collective-permute-done.35.refs_1_), channel_id=1, source_target_pairs={{0,2},{1,3},{2,0},{3,1},{4,6},{5,7},{6,4},{7,5}} | collective-permute-start | bytes 1228808 | tf_op jit(solution)/shard_map/ppermute | solution.py:382
  406.2 37.7 %collective-permute-start.14 = (bf16[80,5120]{1,0:T(8,128)(2,1)}, bf16[80,5120]{1,0:T(8,128)(2,1)}, u32[]{:S(2)}, u32[]{:S(2)}) collective-permute-start(bf16[80,5120]{1,0:T(8,128)(2,1)} %get-tuple-element.51.refs_0_), channel_id=1, source_target_pairs={{0,1},{1,0},{2,3},{3,2},{4,5},{5,4},{6,7},{7,6}} | collective-permute-start | bytes 2457608 | tf_op jit(solution)/shard_map/ppermute | solution.py:382
  409.1 34.8 %collective-permute-start.3 = (bf16[80,5120]{1,0:T(8,128)(2,1)}, bf16[80,5120]{1,0:T(8,128)(2,1)}, u32[]{:S(2)}, u32[]{:S(2)}) collective-permute-start(bf16[80,5120]{1,0:T(8,128)(2,1)} %get-tuple-element.50.refs_0_), channel_id=1, source_target_pairs={{0,4},{1,5},{2,6},{3,7},{4,0},{5,1},{6,2},{7,3}} | collective-permute-start | bytes 2457608 | tf_op jit(solution)/shard_map/ppermute | solution.py:382
  431.6 21.4 %collective-permute-start.17 = (bf16[80,5120]{1,0:T(8,128)(2,1)}, bf16[80,5120]{1,0:T(8,128)(2,1)}, u32[]{:S(2)}, u32[]{:S(2)}) collective-permute-start(bf16[80,5120]{1,0:T(8,128)(2,1)} %get-tuple-element.50.refs_0_), channel_id=1, source_target_pairs={{0,2},{1,3},{2,0},{3,1},{4,6},{5,7},{6,4},{7,5}} | collective-permute-start | bytes 2457608 | tf_op jit(solution)/shard_map/ppermute | solution.py:382
  442.0 46.2 %collective-permute-start.47 = (bf16[640,1280]{1,0:T(8,128)(2,1)S(1)}, bf16[640,1280]{1,0:T(8,128)(2,1)}, u32[]{:S(2)}, u32[]{:S(2)}) collective-permute-start(bf16[640,1280]{1,0:T(8,128)(2,1)S(1)} %copy-done.18), channel_id=1, source_target_pairs={{0,2},{1,3},{2,0},{3,1},{4,6},{5,7},{6,4},{7,5}} | collective-permute-start | bytes 4915208 | tf_op jit(solution)/shard_map/ppermute | solution.py:382
  442.8 45.4 %collective-permute-start.66 = (bf16[640,1280]{1,0:T(8,128)(2,1)S(1)}, bf16[640,1280]{1,0:T(8,128)(2,1)}, u32[]{:S(2)}, u32[]{:S(2)}) collective-permute-start(bf16[640,1280]{1,0:T(8,128)(2,1)S(1)} %copy-done.18), channel_id=1, source_target_pairs={{0,4},{1,5},{2,6},{3,7},{4,0},{5,1},{6,2},{7,3}} | collective-permute-start | bytes 4915208 | tf_op jit(solution)/shard_map/ppermute | solution.py:382
  443.9 45.4 %collective-permute-start.67 = (bf16[640,1280]{1,0:T(8,128)(2,1)S(1)}, bf16[640,1280]{1,0:T(8,128)(2,1)}, u32[]{:S(2)}, u32[]{:S(2)}) collective-permute-start(bf16[640,1280]{1,0:T(8,128)(2,1)S(1)} %copy-done.18), channel_id=1, source_target_pairs={{0,1},{1,0},{2,3},{3,2},{4,5},{5,4},{6,7},{7,6}} | collective-permute-start | bytes 4915208 | tf_op jit(solution)/shard_map/ppermute | solution.py:382
  443.9 79.4 %collective-permute-start.24 = (bf16[160,5120]{1,0:T(8,128)(2,1)}, bf16[160,5120]{1,0:T(8,128)(2,1)}, u32[]{:S(2)}, u32[]{:S(2)}) collective-permute-start(bf16[160,5120]{1,0:T(8,128)(2,1)} %get-tuple-element.56.refs_0_), channel_id=1, source_target_pairs={{0,2},{1,3},{2,0},{3,1},{4,6},{5,7},{6,4},{7,5}} | collective-permute-start | bytes 4915208 | tf_op jit(solution)/shard_map/ppermute | solution.py:382
  455.7 76.5 %collective-permute-start.31 = (bf16[160,5120]{1,0:T(8,128)(2,1)}, bf16[160,5120]{1,0:T(8,128)(2,1)}, u32[]{:S(2)}, u32[]{:S(2)}) collective-permute-start(bf16[160,5120]{1,0:T(8,128)(2,1)} %get-tuple-element.56.refs_0_), channel_id=1, source_target_pairs={{0,4},{1,5},{2,6},{3,7},{4,0},{5,1},{6,2},{7,3}} | collective-permute-start | bytes 4915208 | tf_op jit(solution)/shard_map/ppermute | solution.py:382
  488.2 45.2 %collective-permute-start.32 = (bf16[160,5120]{1,0:T(8,128)(2,1)}, bf16[160,5120]{1,0:T(8,128)(2,1)}, u32[]{:S(2)}, u32[]{:S(2)}) collective-permute-start(bf16[160,5120]{1,0:T(8,128)(2,1)} %get-tuple-element.56.refs_0_), channel_id=1, source_target_pairs={{0,1},{1,0},{2,3},{3,2},{4,5},{5,4},{6,7},{7,6}} | collective-permute-start | bytes 4915208 | tf_op jit(solution)/shard_map/ppermute | solution.py:382
  488.2 63.6 %collective-permute-start.21 = (bf16[160,5120]{1,0:T(8,128)(2,1)}, bf16[160,5120]{1,0:T(8,128)(2,1)}, u32[]{:S(2)}, u32[]{:S(2)}) collective-permute-start(bf16[160,5120]{1,0:T(8,128)(2,1)} %get-tuple-element.55.refs_0_), channel_id=1, source_target_pairs={{0,4},{1,5},{2,6},{3,7},{4,0},{5,1},{6,2},{7,3}} | collective-permute-start | bytes 4915208 | tf_op jit(solution)/shard_map/ppermute | solution.py:382
  489.2 66.5 %collective-permute-start.27 = (bf16[160,5120]{1,0:T(8,128)(2,1)}, bf16[160,5120]{1,0:T(8,128)(2,1)S(1)}, u32[]{:S(2)}, u32[]{:S(2)}) collective-permute-start(bf16[160,5120]{1,0:T(8,128)(2,1)} %get-tuple-element.55.refs_0_), channel_id=1, source_target_pairs={{0,2},{1,3},{2,0},{3,1},{4,6},{5,7},{6,4},{7,5}} | collective-permute-start | bytes 4915208 | tf_op jit(solution)/shard_map/ppermute | solution.py:382
  523.3 32.5 %collective-permute-start.28 = (bf16[160,5120]{1,0:T(8,128)(2,1)}, bf16[160,5120]{1,0:T(8,128)(2,1)S(1)}, u32[]{:S(2)}, u32[]{:S(2)}) collective-permute-start(bf16[160,5120]{1,0:T(8,128)(2,1)} %get-tuple-element.55.refs_0_), channel_id=1, source_target_pairs={{0,1},{1,0},{2,3},{3,2},{4,5},{5,4},{6,7},{7,6}} | collective-permute-start | bytes 4915208 | tf_op jit(solution)/shard_map/ppermute | solution.py:382
  532.3 54.6 %collective-permute-start = (bf16[160,5120]{1,0:T(8,128)(2,1)}, bf16[160,5120]{1,0:T(8,128)(2,1)S(1)}, u32[]{:S(2)}, u32[]{:S(2)}) collective-permute-start(bf16[160,5120]{1,0:T(8,128)(2,1)} %get-tuple-element.49.refs_0_), channel_id=1, source_target_pairs={{0,4},{1,5},{2,6},{3,7},{4,0},{5,1},{6,2},{7,3}} | collective-permute-start | bytes 4915208 | tf_op jit(solution)/shard_map/ppermute | solution.py:382
  533.3 22.9 %collective-permute-start.16 = (bf16[80,5120]{1,0:T(8,128)(2,1)}, bf16[80,5120]{1,0:T(8,128)(2,1)S(1)}, u32[]{:S(2)}, u32[]{:S(2)}) collective-permute-start(bf16[80,5120]{1,0:T(8,128)(2,1)} %collective-permute-done.6.refs_2_), channel_id=1, source_target_pairs={{0,1},{1,0},{2,3},{3,2},{4,5},{5,4},{6,7},{7,6}} | collective-permute-start | bytes 2457608 | tf_op jit(solution)/shard_map/ppermute | solution.py:382
  551.8 5.7 collective-permute-start.15
  555.8 3.7 collective-permute-start.20
  556.3 55.5 %collective-permute-start.9 = (bf16[160,5120]{1,0:T(8,128)(2,1)}, bf16[160,5120]{1,0:T(8,128)(2,1)S(1)}, u32[]{:S(2)}, u32[]{:S(2)}) collective-permute-start(bf16[160,5120]{1,0:T(8,128)(2,1)} %get-tuple-element.49.refs_0_), channel_id=1, source_target_pairs={{0,2},{1,3},{2,0},{3,1},{4,6},{5,7},{6,4},{7,5}} | collective-permute-start | bytes 4915208 | tf_op jit(solution)/shard_map/ppermute | solution.py:382
  557.5 54.8 %collective-permute-start.10 = (bf16[160,5120]{1,0:T(8,128)(2,1)}, bf16[160,5120]{1,0:T(8,128)(2,1)}, u32[]{:S(2)}, u32[]{:S(2)}) collective-permute-start(bf16[160,5120]{1,0:T(8,128)(2,1)} %get-tuple-element.49.refs_0_), channel_id=1, source_target_pairs={{0,1},{1,0},{2,3},{3,2},{4,5},{5,4},{6,7},{7,6}} | collective-permute-start | bytes 4915208 | tf_op jit(solution)/shard_map/ppermute | solution.py:382
  558.3 43.1 %collective-permute-start.7 = (bf16[80,5120]{1,0:T(8,128)(2,1)}, bf16[80,5120]{1,0:T(8,128)(2,1)S(1)}, u32[]{:S(2)}, u32[]{:S(2)}) collective-permute-start(bf16[80,5120]{1,0:T(8,128)(2,1)} %collective-permute-done.6.refs_2_), channel_id=1, source_target_pairs={{0,4},{1,5},{2,6},{3,7},{4,0},{5,1},{6,2},{7,3}} | collective-permute-start | bytes 2457608 | tf_op jit(solution)/shard_map/ppermute | solution.py:382
  559.5 52.3 %collective-permute-start.4 = (bf16[80,5120]{1,0:T(8,128)(2,1)}, bf16[80,5120]{1,0:T(8,128)(2,1)S(1)}, u32[]{:S(2)}, u32[]{:S(2)}) collective-permute-start(bf16[80,5120]{1,0:T(8,128)(2,1)} %collective-permute-done.3.refs_1_), channel_id=1, source_target_pairs={{0,2},{1,3},{2,0},{3,1},{4,6},{5,7},{6,4},{7,5}} | collective-permute-start | bytes 2457608 | tf_op jit(solution)/shard_map/ppermute | solution.py:382
  586.8 27.5 %collective-permute-start.69 = (bf16[640,1280]{1,0:T(8,128)(2,1)}, bf16[640,1280]{1,0:T(8,128)(2,1)S(1)}, u32[]{:S(2)}, u32[]{:S(2)}) collective-permute-start(bf16[640,1280]{1,0:T(8,128)(2,1)} %collective-permute-done.47.refs_2_), channel_id=1, source_target_pairs={{0,1},{1,0},{2,3},{3,2},{4,5},{5,4},{6,7},{7,6}} | collective-permute-start | bytes 4915208 | tf_op jit(solution)/shard_map/ppermute | solution.py:382
  601.4 12.0 %collective-permute-start.8 = (bf16[80,5120]{1,0:T(8,128)(2,1)S(1)}, bf16[80,5120]{1,0:T(8,128)(2,1)S(1)}, u32[]{:S(2)}, u32[]{:S(2)}) collective-permute-start(bf16[80,5120]{1,0:T(8,128)(2,1)S(1)} %collective-permute-done.7.refs_2_), channel_id=1, source_target_pairs={{0,1},{1,0},{2,3},{3,2},{4,5},{5,4},{6,7},{7,6}} | collective-permute-start | bytes 2457608 | tf_op jit(solution)/shard_map/ppermute | solution.py:382
  611.8 4.7 collective-permute-start.68
  612.3 38.0 %collective-permute-start.48 = (bf16[640,1280]{1,0:T(8,128)(2,1)}, bf16[640,1280]{1,0:T(8,128)(2,1)S(1)}, u32[]{:S(2)}, u32[]{:S(2)}) collective-permute-start(bf16[640,1280]{1,0:T(8,128)(2,1)} %collective-permute-done.47.refs_2_), channel_id=1, source_target_pairs={{0,4},{1,5},{2,6},{3,7},{4,0},{5,1},{6,2},{7,3}} | collective-permute-start | bytes 4915208 | tf_op jit(solution)/shard_map/ppermute | solution.py:382
  613.4 37.9 %collective-permute-start.34 = (bf16[160,5120]{1,0:T(8,128)(2,1)}, bf16[160,5120]{1,0:T(8,128)(2,1)S(1)}, u32[]{:S(2)}, u32[]{:S(2)}) collective-permute-start(bf16[160,5120]{1,0:T(8,128)(2,1)} %collective-permute-done.24.refs_2_), channel_id=1, source_target_pairs={{0,1},{1,0},{2,3},{3,2},{4,5},{5,4},{6,7},{7,6}} | collective-permute-start | bytes 4915208 | tf_op jit(solution)/shard_map/ppermute | solution.py:382
  614.1 38.4 %collective-permute-start.33 = (bf16[160,5120]{1,0:T(8,128)(2,1)}, bf16[160,5120]{1,0:T(8,128)(2,1)S(1)}, u32[]{:S(2)}, u32[]{:S(2)}) collective-permute-start(bf16[160,5120]{1,0:T(8,128)(2,1)} %collective-permute-done.31.refs_1_), channel_id=1, source_target_pairs={{0,1},{1,0},{2,3},{3,2},{4,5},{5,4},{6,7},{7,6}} | collective-permute-start | bytes 4915208 | tf_op jit(solution)/shard_map/ppermute | solution.py:382
  614.3 38.2 %collective-permute-start.29 = (bf16[160,5120]{1,0:T(8,128)(2,1)}, bf16[160,5120]{1,0:T(8,128)(2,1)S(1)}, u32[]{:S(2)}, u32[]{:S(2)}) collective-permute-start(bf16[160,5120]{1,0:T(8,128)(2,1)} %collective-permute-done.21.refs_1_), channel_id=1, source_target_pairs={{0,1},{1,0},{2,3},{3,2},{4,5},{5,4},{6,7},{7,6}} | collective-permute-start | bytes 4915208 | tf_op jit(solution)/shard_map/ppermute | solution.py:382
  616.5 37.0 %collective-permute-start.30 = (bf16[160,5120]{1,0:T(8,128)(2,1)}, bf16[160,5120]{1,0:T(8,128)(2,1)S(1)}, u32[]{:S(2)}, u32[]{:S(2)}) collective-permute-start(bf16[160,5120]{1,0:T(8,128)(2,1)} %copy-done.19), channel_id=1, source_target_pairs={{0,1},{1,0},{2,3},{3,2},{4,5},{5,4},{6,7},{7,6}} | collective-permute-start | bytes 4915208 | tf_op jit(solution)/shard_map/ppermute | solution.py:382
  650.3 37.1 %collective-permute-start.25 = (bf16[160,5120]{1,0:T(8,128)(2,1)}, bf16[160,5120]{1,0:T(8,128)(2,1)S(1)}, u32[]{:S(2)}, u32[]{:S(2)}) collective-permute-start(bf16[160,5120]{1,0:T(8,128)(2,1)} %collective-permute-done.24.refs_2_), channel_id=1, source_target_pairs={{0,4},{1,5},{2,6},{3,7},{4,0},{5,1},{6,2},{7,3}} | collective-permute-start | bytes 4915208 | tf_op jit(solution)/shard_map/ppermute | solution.py:382
  651.4 38.9 %collective-permute-start.22 = (bf16[160,5120]{1,0:T(8,128)(2,1)}, bf16[160,5120]{1,0:T(8,128)(2,1)S(1)}, u32[]{:S(2)}, u32[]{:S(2)}) collective-permute-start(bf16[160,5120]{1,0:T(8,128)(2,1)} %collective-permute-done.21.refs_1_), channel_id=1, source_target_pairs={{0,2},{1,3},{2,0},{3,1},{4,6},{5,7},{6,4},{7,5}} | collective-permute-start | bytes 4915208 | tf_op jit(solution)/shard_map/ppermute | solution.py:382
  652.5 38.9 %collective-permute-start.11 = (bf16[160,5120]{1,0:T(8,128)(2,1)S(1)}, bf16[160,5120]{1,0:T(8,128)(2,1)S(1)}, u32[]{:S(2)}, u32[]{:S(2)}) collective-permute-start(bf16[160,5120]{1,0:T(8,128)(2,1)S(1)} %collective-permute-done.refs_1_), channel_id=1, source_target_pairs={{0,1},{1,0},{2,3},{3,2},{4,5},{5,4},{6,7},{7,6}} | collective-permute-start | bytes 4915208 | tf_op jit(solution)/shard_map/ppermute | solution.py:382
  652.5 70.9 %collective-permute-start.1 = (bf16[160,5120]{1,0:T(8,128)(2,1)S(1)}, bf16[160,5120]{1,0:T(8,128)(2,1)}, u32[]{:S(2)}, u32[]{:S(2)}) collective-permute-start(bf16[160,5120]{1,0:T(8,128)(2,1)S(1)} %collective-permute-done.refs_1_), channel_id=1, source_target_pairs={{0,2},{1,3},{2,0},{3,1},{4,6},{5,7},{6,4},{7,5}} | collective-permute-start | bytes 4915208 | tf_op jit(solution)/shard_map/ppermute | solution.py:382
  653.5 69.9 %collective-permute-start.12 = (bf16[160,5120]{1,0:T(8,128)(2,1)S(1)}, bf16[160,5120]{1,0:T(8,128)(2,1)S(1)}, u32[]{:S(2)}, u32[]{:S(2)}) collective-permute-start(bf16[160,5120]{1,0:T(8,128)(2,1)S(1)} %collective-permute-done.9.refs_2_), channel_id=1, source_target_pairs={{0,1},{1,0},{2,3},{3,2},{4,5},{5,4},{6,7},{7,6}} | collective-permute-start | bytes 4915208 | tf_op jit(solution)/shard_map/ppermute | solution.py:382
  687.4 36.5 %collective-permute-start.49 = (bf16[640,1280]{1,0:T(8,128)(2,1)S(1)}, bf16[640,1280]{1,0:T(8,128)(2,1)S(1)}, u32[]{:S(2)}, u32[]{:S(2)}) collective-permute-start(bf16[640,1280]{1,0:T(8,128)(2,1)S(1)} %collective-permute-done.48.refs_0_), channel_id=1, source_target_pairs={{0,1},{1,0},{2,3},{3,2},{4,5},{5,4},{6,7},{7,6}} | collective-permute-start | bytes 4915208 | tf_op jit(solution)/shard_map/ppermute | solution.py:382
  690.3 34.9 %collective-permute-start.26 = (bf16[160,5120]{1,0:T(8,128)(2,1)S(1)}, bf16[160,5120]{1,0:T(8,128)(2,1)S(1)}, u32[]{:S(2)}, u32[]{:S(2)}) collective-permute-start(bf16[160,5120]{1,0:T(8,128)(2,1)S(1)} %collective-permute-done.25.refs_0_), channel_id=1, source_target_pairs={{0,1},{1,0},{2,3},{3,2},{4,5},{5,4},{6,7},{7,6}} | collective-permute-start | bytes 4915208 | tf_op jit(solution)/shard_map/ppermute | solution.py:382
  691.4 35.4 %collective-permute-start.23 = (bf16[160,5120]{1,0:T(8,128)(2,1)S(1)}, bf16[160,5120]{1,0:T(8,128)(2,1)S(1)}, u32[]{:S(2)}, u32[]{:S(2)}) collective-permute-start(bf16[160,5120]{1,0:T(8,128)(2,1)S(1)} %collective-permute-done.22.refs_0_), channel_id=1, source_target_pairs={{0,1},{1,0},{2,3},{3,2},{4,5},{5,4},{6,7},{7,6}} | collective-permute-start | bytes 4915208 | tf_op jit(solution)/shard_map/ppermute | solution.py:382
  723.4 64.3 %collective-permute-start.2 = (bf16[160,5120]{1,0:T(8,128)(2,1)}, bf16[160,5120]{1,0:T(8,128)(2,1)}, u32[]{:S(2)}, u32[]{:S(2)}) collective-permute-start(bf16[160,5120]{1,0:T(8,128)(2,1)} %collective-permute-done.1.refs_0_), channel_id=1, source_target_pairs={{0,1},{1,0},{2,3},{3,2},{4,5},{5,4},{6,7},{7,6}} | collective-permute-start | bytes 4915208 | tf_op jit(solution)/shard_map/ppermute | solution.py:382
  723.4 68.0 %collective-permute-start.46 = (bf16[160,1280]{1,0:T(8,128)(2,1)}, bf16[160,1280]{1,0:T(8,128)(2,1)}, u32[]{:S(2)}, u32[]{:S(2)}) collective-permute-start(bf16[160,1280]{1,0:T(8,128)(2,1)} %copy-done.12), channel_id=1, source_target_pairs={{0,1},{1,0},{2,3},{3,2},{4,5},{5,4},{6,7},{7,6}} | collective-permute-start | bytes 1228808 | tf_op jit(solution)/shard_map/ppermute | solution.py:382
  725.1 66.3 %collective-permute-start.43 = (bf16[160,1280]{1,0:T(8,128)(2,1)}, bf16[160,1280]{1,0:T(8,128)(2,1)}, u32[]{:S(2)}, u32[]{:S(2)}) collective-permute-start(bf16[160,1280]{1,0:T(8,128)(2,1)} %copy-done.16), channel_id=1, source_target_pairs={{0,1},{1,0},{2,3},{3,2},{4,5},{5,4},{6,7},{7,6}} | collective-permute-start | bytes 1228808 | tf_op jit(solution)/shard_map/ppermute | solution.py:382
  726.4 67.5 %collective-permute-start.40 = (bf16[160,1280]{1,0:T(8,128)(2,1)}, bf16[160,1280]{1,0:T(8,128)(2,1)}, u32[]{:S(2)}, u32[]{:S(2)}) collective-permute-start(bf16[160,1280]{1,0:T(8,128)(2,1)} %copy-done.14), channel_id=1, source_target_pairs={{0,1},{1,0},{2,3},{3,2},{4,5},{5,4},{6,7},{7,6}} | collective-permute-start | bytes 1228808 | tf_op jit(solution)/shard_map/ppermute | solution.py:382
  728.0 65.8 %collective-permute-start.37 = (bf16[160,1280]{1,0:T(8,128)(2,1)}, bf16[160,1280]{1,0:T(8,128)(2,1)}, u32[]{:S(2)}, u32[]{:S(2)}) collective-permute-start(bf16[160,1280]{1,0:T(8,128)(2,1)} %collective-permute-done.36.refs_0_), channel_id=1, source_target_pairs={{0,1},{1,0},{2,3},{3,2},{4,5},{5,4},{6,7},{7,6}} | collective-permute-start | bytes 1228808 | tf_op jit(solution)/shard_map/ppermute | solution.py:382
  (58 other events, 984.4 us)

commit v5 on v4

--- a/solution.py
+++ b/solution.py
@@ -56,8 +56,8 @@
     out, squares, new0, refs = refs[:3], refs[3], refs[4], refs[5:]
     near, refs = refs[:3], refs[3:]
     snd, rcv, own, par, refs = refs[0:2], refs[2:4], refs[4:6], refs[6:8], refs[8:]
-    first, refs = refs[:4], refs[4:]
-    acc, norms, d2d_s, d2d_r, link_s, link_r, own_sem, par_sem, out_sem, norm_s, norm_r, first_sem = refs
+    first, early, refs = refs[:4], refs[4], refs[5:]
+    acc, norms, d2d_s, d2d_r, link_s, link_r, own_sem, par_sem, out_sem, norm_s, norm_r, first_sem, early_sem, ready = refs
     layers = g[0].shape[1]
     units = [(a, l) for a in range(3) for l in range(layers)]
     end = len(units) - 1
@@ -70,9 +70,12 @@
     xn, yn, cn = place(dx=1), place(dy=1), place(dc=1)
 
     barrier = pltpu.get_barrier_semaphore()
-    others = [lax.rem(me + k, 8) for k in range(1, 8)]
-    for d in others:
-        pl.semaphore_signal(barrier, inc=1, device_id=(rep, d), device_id_type=MESH)
+
+    def tell(sem):
+        for d in (cn, xn, yn):
+            pl.semaphore_signal(sem, inc=1, device_id=(rep, d), device_id_type=MESH)
+
+    tell(barrier)
 
     mine = pl.ds(pl.multiple_of(me * shapes[0][0], 16), head)
     ahead = [
@@ -89,34 +92,28 @@
             return [(0, n - n // 5), (n - n // 5, n // 5)]
         return [(0, n)]
 
-    d2d = {}
-
-    def cut(s, h):
-        return {(0, 0): 0, (0, 1): 1, (1, 0): 2, (2, 1): 3, (1, 1): 4, (2, 0): 5}.get((s, h))
-
     def rows(u, device, h, piece):
         a, l = u
         n = shapes[a][0] // 2
         return g[a].at[0, l, pl.ds(pl.multiple_of(device * (2 * n) + h * n + piece[0], 16), piece[1])]
 
-    sends = []
-    for i, u in enumerate(units):
-        n = shapes[u[0]][0] // 2
-        halves = [(s, h) for s in range(4) for h in range(2)]
-        todo = [(s, h, p) for s, h in halves for p in (split(i, cut(s, h)) if i == 0 and s == 0 else [(0, n)])]
-        if i == 0:
-            todo.sort(key=lambda one: one[2] != (0, 16))
-        sends += [(i, *one) for one in todo]
-    for k, (i, s, h, p) in enumerate(sends):
-        a, l = units[i]
-        d2d[i, s, h, p] = pltpu.make_async_remote_copy(
-            src_ref=rows(units[i], place(*CHIPS[s], 1), h, p),
-            dst_ref=near[a].at[l, s, h, pl.ds(*p)],
-            send_sem=d2d_s.at[k],
-            recv_sem=d2d_r.at[k],
-            device_id=(rep, cn),
-            device_id_type=MESH,
+    def all_of(ref, sem):
+        pltpu.make_async_copy(ref, ref, sem).wait()
+
+    opening = [(0, h, p) for p in split(0, 0) for h in range(2)]
+    near_sends = []
+    for k, (s, h, p) in enumerate(opening):
+        near_sends.append((early.at[h] if k < 2 else rows(units[0], place(*CHIPS[s], 1), h, p), par[0].at[h, pl.ds(*p)], 0, k))
+    for i, (a, l) in enumerate(units):
+        for s in range(4):
+            if (i, s) != (0, 0):
+                near_sends.append((rows(units[i], place(*CHIPS[s], 1), 0, (0, shapes[a][0])), near[a].at[l, s], a, 4 + i))
+    near_sends = [
+        pltpu.make_async_remote_copy(
+            src_ref=src, dst_ref=dst, send_sem=d2d_s.at[a], recv_sem=d2d_r.at[k], device_id=(rep, cn), device_id_type=MESH
         )
+        for src, dst, a, k in near_sends
+    ]
 
     tasks = []
     for i in range(end + 1):
@@ -130,7 +127,8 @@
         for p4, p5 in zip(split(i, 4), split(i, 5)):
             tasks += [(i, 3, 0, p5, (2, 5), None), (i, 3, 1, p4, (3, 4), None)]
 
-    numbers = {key: k for k, key in enumerate((i, j, p) for i in range(end + 1) for j in range(6) for p in split(i, j))}
+    def arrival(i, j, p):
+        return link_r.at[3 * len(units) if j >= 4 and i == end and p[0] else 3 * i + j // 2]
 
     def link(i, j, p):
         a, l = units[i]
@@ -138,8 +136,8 @@
         return pltpu.make_async_remote_copy(
             src_ref=snd[k].at[slot[a, l], j % 4, pl.ds(*p)],
             dst_ref=rcv[k].at[slot[a, l], j, pl.ds(*p)],
-            send_sem=link_s.at[numbers[i, j, p]],
-            recv_sem=link_r.at[numbers[i, j, p]],
+            send_sem=link_s.at[j // 4, i],
+            recv_sem=arrival(i, j, p),
             device_id=(rep, xn if j % 2 == 0 else yn),
             device_id_type=MESH,
         )
@@ -151,87 +149,110 @@
             done.add(what)
             wait()
 
-    def arrived(i, j, piece):
-        for p in split(i, j):
-            if p[0] < piece[0] + piece[1] and piece[0] < p[0] + p[1]:
-                once(("arrived", i, j, p), lambda: link(i, j, p).wait_recv())
-
-    def left(i, j):
-        for p in split(i, j):
-            once(("left", i, j, p), lambda: link(i, j, p).wait_send())
+    def arrived(i, j, p):
+        a, l = units[i]
+        into = rcv[kind[a]].at[slot[a, l], pl.ds(j - j % 2, 2)]
+        if j >= 4:
+            into = into.at[:, pl.ds(*p)]
+            once(("arrived", i, 4, p), lambda: all_of(into, arrival(i, j, p)))
+        else:
+            once(("arrived", i, j // 2), lambda: all_of(into, arrival(i, j, p)))
+
+    def left(i):
+        a, l = units[i]
+        once(("left", i), lambda: all_of(snd[kind[a]].at[slot[a, l]], link_s.at[0, i]))
 
     loads = {}
 
     def load_mine(t):
         i, s, h, p, _, _ = tasks[t]
         k, b = kind[units[i][0]], t % 2
-        loads[t] = [pltpu.make_async_copy(rows(units[i], place(*CHIPS[s], 0), h, p), own[k].at[b, pl.ds(0, p[1])], own_sem.at[b])]
+        at = pl.ds(*p) if t < 4 else pl.ds(0, p[1])
+        loads[t] = [pltpu.make_async_copy(rows(units[i], place(*CHIPS[s], 0), h, p), own[k].at[b, at], own_sem.at[t if t < 4 else b])]
         loads[t][0].start()
 
     def load_theirs(t):
         i, s, h, p, _, _ = tasks[t]
         a, l = units[i]
         k, b = kind[a], t % 2
-        whole = p if (i, s, h, p) in d2d else (0, shapes[a][0] // 2)
-        once(("near", i, s, h, whole), d2d[i, s, h, whole].wait_recv)
-        loads[t] += [pltpu.make_async_copy(near[a].at[l, s, h, pl.ds(*p)], par[k].at[b, pl.ds(0, p[1])], par_sem.at[b])]
+        all_near = near[a].at[l] if i else near[a].at[l, pl.ds(1, 3)]
+        once(("near", i), lambda: all_of(all_near, d2d_r.at[4 + i]))
+        at = pl.ds(h * (shapes[a][0] // 2) + p[0], p[1])
+        loads[t] += [pltpu.make_async_copy(near[a].at[l, s, at], par[k].at[b, pl.ds(0, p[1])], par_sem.at[b])]
         loads[t][1].start()
 
-    load_mine(0)
+    taken = [pltpu.make_async_copy(rows(units[0], place(*CHIPS[0], 1), h, (0, 16)), early.at[h], early_sem.at[0]) for h in range(2)]
+    for one in taken:
+        one.start()
+    for t in range(4):
+        load_mine(t)
     acc[...] = jnp.zeros_like(acc)
-    pl.semaphore_wait(barrier, 7)
-    for one in d2d.values():
+    all_of(early, early_sem.at[0])
+    pl.semaphore_wait(barrier, 3)
+    for one in near_sends[:4]:
         one.start()
-    for one in ahead:
-        one.start()
-    load_theirs(0)
-    stores = []
     for t, (i, s, h, p, added, j) in enumerate(tasks):
-        if t + 1 < len(tasks):
+        if t == 2:
+            for one in near_sends[4:]:
+                one.start()
+            tell(ready.at[0])
+        if t == 12:
+            for one in ahead:
+                one.start()
+        here = t > 3 and t + 1 < len(tasks) and ("near", tasks[t + 1][0]) in done
+        late = t > 2 and t + 1 < len(tasks) and not here
+        if here:
             load_mine(t + 1)
             load_theirs(t + 1)
+        if t in (8, 16):
+            pl.semaphore_wait(ready.at[t // 8 - 1], 3)
+            if t == 8:
+                tell(ready.at[1])
         a, l = units[i]
         k = kind[a]
         for one in loads[t]:
             one.wait()
+        if t < 4:
+            near_sends[t].wait_recv()
         for r in added:
             arrived(i, r, p)
-        parts = [own[k].at[t % 2, pl.ds(0, p[1])], par[k].at[t % 2, pl.ds(0, p[1])]]
+        held = pl.ds(p[0] if t < 4 else 0, p[1])
+        parts = [own[k].at[t % 2, held], par[k].at[t % 2, held]]
         parts += [rcv[k].at[slot[a, l], r, pl.ds(*p)] for r in added]
         if j is None:
             dst = snd[k].at[slot[a, l], 2 + h, pl.ds(*p)]
-            left(i, 2 + h)
+            left(i)
             add_square(dst, parts, shapes[a][1], acc)
-            store = pltpu.make_async_copy(dst, out[a].at[l, pl.ds(h * (shapes[a][0] // 2) + p[0], p[1])], out_sem.at[len(stores)])
+            store = pltpu.make_async_copy(dst, out[a].at[l, pl.ds(h * (shapes[a][0] // 2) + p[0], p[1])], out_sem.at[a])
             store.start()
-            stores.append(store)
         else:
             dst = snd[k].at[slot[a, l], j % 4, pl.ds(*p)]
             if j >= 4:
-                left(i, j - 4)
+                left(i)
             add_into(dst, parts)
             link(i, j, p).start()
-
-    sent = []
+        if late:
+            load_mine(t + 1)
+            load_theirs(t + 1)
+
     for k in range(1, 8):
-        to = lax.rem(me + k, 8)
-        copy = pltpu.make_async_remote_copy(
-            src_ref=acc, dst_ref=norms.at[me], send_sem=norm_s.at[k - 1], recv_sem=norm_r.at[k - 1], device_id=(rep, to), device_id_type=MESH
-        )
-        copy.start()
-        sent.append(copy)
+        pltpu.make_async_remote_copy(
+            src_ref=acc,
+            dst_ref=norms.at[me],
+            send_sem=norm_s.at[0],
+            recv_sem=norm_r.at[0],
+            device_id=(rep, lax.rem(me + k, 8)),
+            device_id_type=MESH,
+        ).start()
     norms[me] = acc[...]
     for one in ahead:
         one.wait()
-    for store in stores:
-        store.wait()
-    for copy in d2d.values():
-        copy.wait_send()
-    for i in range(end + 1):
-        for j in range(6):
-            left(i, j)
-    for copy in sent:
-        copy.wait_recv()
+    for a in range(3):
+        all_of(out[a], out_sem.at[a])
+        all_of(near[a], d2d_s.at[a])
+    for i, (a, l) in enumerate(units):
+        all_of(snd[kind[a]].at[slot[a, l], pl.ds(0, 2)], link_s.at[1, i])
+    all_of(norms.at[pl.ds(0, 7)], norm_r.at[0])
     total = norms[0]
     for d in range(1, 8):
         total = total + norms[d]
@@ -241,17 +262,12 @@
 
     half = snd[0].at[slot[0, 0], 2]
 
-    def body(i, carry):
-        r = pl.ds(pl.multiple_of(i * 16, 16), 16)
+    for i in range(head // 16):
+        r = pl.ds(i * 16, 16)
         first[3][r, :] = stepped_block(total, count, half[r, :], first[0][r, :], first[1][r, :], first[2][r, :])[0]
-        return carry
-
-    lax.fori_loop(0, head // 16, body, 0)
-    last = pltpu.make_async_copy(first[3], new0, first_sem.at[3])
-    last.start()
-    for copy in sent:
-        copy.wait_send()
-    last.wait()
+        pltpu.make_async_copy(first[3].at[r], new0.at[r], first_sem.at[3]).start()
+    all_of(norms.at[pl.ds(0, 7)], norm_s.at[0])
+    all_of(new0, first_sem.at[3])
 
 
 def summed(terms, count, head, w, m, v):
@@ -265,26 +281,29 @@
         out_shape=[jax.ShapeDtypeStruct((layers, *s), BF16) for s in shapes]
         + [jax.ShapeDtypeStruct((8, 128), F32)]
         + [jax.ShapeDtypeStruct((head, shapes[0][1]), BF16)]
-        + [jax.ShapeDtypeStruct((layers, 4, 2, s[0] // 2, s[1]), BF16) for s in shapes],
+        + [jax.ShapeDtypeStruct((layers, 4, *s), BF16) for s in shapes],
         in_specs=[any_] * 6,
         out_specs=[any_] * 3 + [pl.BlockSpec(memory_space=pltpu.VMEM)] + [any_] * 4,
         scratch_shapes=[pltpu.VMEM((n, 4, *s), BF16) for n, s in zip(counts, halves)]
         + [pltpu.VMEM((n, 6, *s), BF16) for n, s in zip(counts, halves)]
         + [pltpu.VMEM((2, *s), BF16) for s in halves] * 2
         + [pltpu.VMEM((head, shapes[0][1]), t) for t in (BF16, F32, F32, BF16)]
+        + [pltpu.VMEM((2, 16, shapes[0][1]), BF16)]
         + [
             pltpu.VMEM((16, 128), F32),
             pltpu.VMEM((8, 16, 128), F32),
-            pltpu.SemaphoreType.DMA((24 * layers + 2,)),
-            pltpu.SemaphoreType.DMA((24 * layers + 2,)),
-            pltpu.SemaphoreType.DMA((18 * layers + 4,)),
-            pltpu.SemaphoreType.DMA((18 * layers + 4,)),
+            pltpu.SemaphoreType.DMA((3,)),
+            pltpu.SemaphoreType.DMA((4 + 3 * layers,)),
+            pltpu.SemaphoreType.DMA((2, 3 * layers)),
+            pltpu.SemaphoreType.DMA((9 * layers + 1,)),
+            pltpu.SemaphoreType.DMA((4,)),
             pltpu.SemaphoreType.DMA((2,)),
-            pltpu.SemaphoreType.DMA((2,)),
-            pltpu.SemaphoreType.DMA((6 * layers + 2,)),
-            pltpu.SemaphoreType.DMA((7,)),
-            pltpu.SemaphoreType.DMA((7,)),
+            pltpu.SemaphoreType.DMA((3,)),
+            pltpu.SemaphoreType.DMA((1,)),
+            pltpu.SemaphoreType.DMA((1,)),
             pltpu.SemaphoreType.DMA((4,)),
+            pltpu.SemaphoreType.DMA((1,)),
+            pltpu.SemaphoreType.REGULAR((2,)),
         ],
         compiler_params=pltpu.CompilerParams(collective_id=0, has_side_effects=True, vmem_limit_bytes=62 * 1024 * 1024),
         name="sum_terms",

time: 798 us -> 796 us (level)
  transfers between devices with their start and end apart: 70 -> 70, of which waited for: 27 -> 27; matrix products, arithmetic and copies ran while one was open for 0% -> 0% of each run, Pallas kernels for 14% -> 15%
where the time goes in v5:
time: 796 us; the launch traced here: 794 us
  Pallas kernels  462 us (58%)
  waiting for transfers between devices  284 us (36%)
  starting transfers between devices  36.1 us (5%)
  local copies, waits for them, and re-layouts  10.6 us (1%)
    pallas_call x1, Pallas kernels, summed(): pl.pallas_call(functools.partial(sum_kernel, shapes, count, head), out_sh...  330 us
    ppermute x70, waiting for transfers between devices, send(): return lax.ppermute(block, 'dp', [(d, d ^ flip) for d in range(8)])  284 us
    pallas_call x10, Pallas kernels, stepped(): pl.pallas_call(functools.partial(step_kernel, count, with_weight), out_sh...  66.9 us
    pallas_call x17, Pallas kernels, placed(): pl.pallas_call(functools.partial(place_kernel, places, len(before), in_vm...  64.6 us
    ppermute x70, starting transfers between devices, send(): return lax.ppermute(block, 'dp', [(d, d ^ flip) for d in range(8)])  36.1 us
  transfers between devices with their start and end apart: 70, of which 27 were waited for; matrix products, arithmetic and copies ran while one was open for 0% of the time, Pallas kernels for 15%

profile of v5, /device:TPU:0, one launch (start us, length us, event | category | flops | bytes accessed | tf_op | source)
XLA Modules:
  0.0 794.2 jit_solution(15417949378026510111)
XLA Ops:
  0.6 330.1 %sum_terms.1 = (bf16[2,160,5120]{2,1,0:T(8,128)(2,1)}, bf16[2,160,5120]{2,1,0:T(8,128)(2,1)}, bf16[2,640,1280]{2,1,0:T(8,128)(2,1)}, f32[8,128]{1,0:T(8,128)}, b...) custom-call(bf16[1,2,1280,5120]{3,2,1,0:T(8,128)(2,1)} %refs_0_.1, ...), custom_call_target="tpu_custom_call" | custom-call | tf_op jit(solution)/shard_map/sum_terms/pallas_call | solution.py:279
  330.8 9.0 %adamw.15 = (bf16[640,1280]{1,0:T(8,128)(2,1)}, f32[2,640,1280]{2,1,0:T(8,128)}, f32[2,640,1280]{2,1,0:T(8,128)}) custom-call(s32[1]{0:T(128)} %bitcast.me, f32[8,128]{1,0:T(8,128)} %get-tuple-element.43.squares, bf16[2,640,1280]{2,1,0:T(8,128)(2,1)} %get-tuple-element.57.g, bf16[2,5120,1280]{2,1,0:T(8,128)(2,1)} %w.19, f32[2,640,1280]{2,1,0:T(8,128)} %m.19, ...), custom_call_target="tpu_custom_call" | custom-call | flops 12288000 | bytes 18022400 | tf_op jit(solution)/shard_map/adamw/pallas_call | solution.py:343
  339.7 4.7 adamw.16
  344.4 1.2 collective-permute-start.41
  346.6 4.7 adamw.17
  351.3 1.5 collective-permute-start.58
  353.2 4.7 adamw.18
  359.3 1.4 collective-permute-start.54
  360.7 4.7 adamw.19
  365.8 1.2 collective-permute-done.44.refs_2_
  367.8 1.6 collective-permute-start.38
  369.4 5.2 collective-permute-done.35.refs_1_
  374.7 1.2 collective-permute-done.54.refs_2_
  376.4 6.2 collective-permute-done.50.refs_1_
  386.1 1.5 collective-permute-start.42
  388.7 5.9 adamw.10
  394.6 6.2 adamw.11
  402.4 1.5 collective-permute-start.36
  403.9 2.3 collective-permute-done.39.refs_2_
  407.2 22.1 %collective-permute-done.36.refs_0_ = bf16[160,1280]{1,0:T(8,128)(2,1)} collective-permute-done((bf16[160,1280]{1,0:T(8,128)(2,1)}, bf16[160,1280]{1,0:T(8,128)(2,1)}, u32[]{:S(2)}, u32[]{:S(2)}) %collective-permute-start.36) | collective-permute-done | bytes 409632 | tf_op jit(solution)/shard_map/ppermute | solution.py:401
  430.1 9.1 %adamw.13 = (bf16[160,5120]{1,0:T(8,128)(2,1)}, f32[2,160,5120]{2,1,0:T(8,128)}, f32[2,160,5120]{2,1,0:T(8,128)}) custom-call(s32[1]{0:T(128)} %bitcast.me, f32[8,128]{1,0:T(8,128)} %get-tuple-element.43.squares, bf16[2,160,5120]{2,1,0:T(8,128)(2,1)} %get-tuple-element.52.g, bf16[2,1280,5120]{2,1,0:T(8,128)(2,1)} %w.14, f32[2,160,5120]{2,1,0:T(8,128)} %m.14, ...), custom_call_target="tpu_custom_call" | custom-call | flops 12288000 | bytes 18022400 | tf_op jit(solution)/shard_map/adamw/pallas_call | solution.py:343
  439.2 1.4 collective-permute-start.47
  442.3 8.5 %collective-permute-done.17.refs_2_ = bf16[80,5120]{1,0:T(8,128)(2,1)} collective-permute-done((bf16[80,5120]{1,0:T(8,128)(2,1)}, bf16[80,5120]{1,0:T(8,128)(2,1)}, u32[]{:S(2)}, u32[]{:S(2)}) %collective-permute-start.17) | collective-permute-done | bytes 819232 | tf_op jit(solution)/shard_map/ppermute | solution.py:401
  450.8 2.7 collective-permute-done.18.refs_3_
  454.5 9.0 %adamw.14 = (bf16[160,5120]{1,0:T(8,128)(2,1)}, f32[2,160,5120]{2,1,0:T(8,128)}, f32[2,160,5120]{2,1,0:T(8,128)}) custom-call(s32[1]{0:T(128)} %bitcast.me, f32[8,128]{1,0:T(8,128)} %get-tuple-element.43.squares, bf16[2,160,5120]{2,1,0:T(8,128)(2,1)} %get-tuple-element.52.g, ...), custom_call_target="tpu_custom_call", output_to_operand_aliasing={{1}: (6, {}), {2}: (7, {})} | custom-call | flops 12288000 | bytes 18022400 | tf_op jit(solution)/shard_map/adamw/pallas_call | solution.py:343
  463.5 22.4 %collective-permute-done.47.refs_2_ = bf16[640,1280]{1,0:T(8,128)(2,1)} collective-permute-done((bf16[640,1280]{1,0:T(8,128)(2,1)S(1)}, bf16[640,1280]{1,0:T(8,128)(2,1)}, u32[]{:S(2)}, u32[]{:S(2)}) %collective-permute-start.47) | collective-permute-done | bytes 1638432 | tf_op jit(solution)/shard_map/ppermute | solution.py:401
  487.6 33.4 %collective-permute-done.24.refs_2_ = bf16[160,5120]{1,0:T(8,128)(2,1)} collective-permute-done((bf16[160,5120]{1,0:T(8,128)(2,1)}, bf16[160,5120]{1,0:T(8,128)(2,1)}, u32[]{:S(2)}, u32[]{:S(2)}) %collective-permute-start.24) | collective-permute-done | bytes 1638432 | tf_op jit(solution)/shard_map/ppermute | solution.py:401
  521.0 9.0 %adamw.12 = (bf16[160,5120]{1,0:T(8,128)(2,1)}, f32[2,160,5120]{2,1,0:T(8,128)}, f32[2,160,5120]{2,1,0:T(8,128)}) custom-call(s32[1]{0:T(128)} %bitcast.me, f32[8,128]{1,0:T(8,128)} %get-tuple-element.43.squares, bf16[2,160,5120]{2,1,0:T(8,128)(2,1)} %get-tuple-element.44.g, ...), custom_call_target="tpu_custom_call", output_to_operand_aliasing={{1}: (6, {}), {2}: (7, {})} | custom-call | flops 12288000 | bytes 18022400 | tf_op jit(solution)/shard_map/adamw/pallas_call | solution.py:343
  530.0 1.1 collective-permute-start
  531.3 18.2 %collective-permute-done.21.refs_1_ = bf16[160,5120]{1,0:T(8,128)(2,1)} collective-permute-done((bf16[160,5120]{1,0:T(8,128)(2,1)}, bf16[160,5120]{1,0:T(8,128)(2,1)}, u32[]{:S(2)}, u32[]{:S(2)}) %collective-permute-start.21) | collective-permute-done | bytes 1638432 | tf_op jit(solution)/shard_map/ppermute | solution.py:401
  549.5 4.0 collective-permute-done.27.refs_2_
  554.8 1.3 collective-permute-done.19.refs_4_
  558.0 26.6 %collective-permute-done.refs_1_ = bf16[160,5120]{1,0:T(8,128)(2,1)S(1)} collective-permute-done((bf16[160,5120]{1,0:T(8,128)(2,1)}, bf16[160,5120]{1,0:T(8,128)(2,1)S(1)}, u32[]{:S(2)}, u32[]{:S(2)}) %collective-permute-start) | collective-permute-done | bytes 1638432 | tf_op jit(solution)/shard_map/ppermute | solution.py:401
  584.6 14.5 %collective-permute-done.7.refs_2_ = bf16[80,5120]{1,0:T(8,128)(2,1)S(1)} collective-permute-done((bf16[80,5120]{1,0:T(8,128)(2,1)}, bf16[80,5120]{1,0:T(8,128)(2,1)S(1)}, u32[]{:S(2)}, u32[]{:S(2)}) %collective-permute-start.7) | collective-permute-done | bytes 819232 | tf_op jit(solution)/shard_map/ppermute | solution.py:401
  599.0 10.5 %collective-permute-done.4.refs_0_ = bf16[80,5120]{1,0:T(8,128)(2,1)S(1)} collective-permute-done((bf16[80,5120]{1,0:T(8,128)(2,1)}, bf16[80,5120]{1,0:T(8,128)(2,1)S(1)}, u32[]{:S(2)}, u32[]{:S(2)}) %collective-permute-start.4) | collective-permute-done | bytes 819232 | tf_op jit(solution)/shard_map/ppermute | solution.py:401
  612.4 1.8 collective-permute-done.68.refs_4_
  614.4 33.7 %collective-permute-done.48.refs_0_ = bf16[640,1280]{1,0:T(8,128)(2,1)S(1)} collective-permute-done((bf16[640,1280]{1,0:T(8,128)(2,1)}, bf16[640,1280]{1,0:T(8,128)(2,1)S(1)}, u32[]{:S(2)}, u32[]{:S(2)}) %collective-permute-start.48) | collective-permute-done | bytes 1638432 | tf_op jit(solution)/shard_map/ppermute | solution.py:401
  649.8 1.3 collective-permute-start.1
  651.4 33.7 %collective-permute-done.25.refs_0_ = bf16[160,5120]{1,0:T(8,128)(2,1)S(1)} collective-permute-done((bf16[160,5120]{1,0:T(8,128)(2,1)}, bf16[160,5120]{1,0:T(8,128)(2,1)S(1)}, u32[]{:S(2)}, u32[]{:S(2)}) %collective-permute-start.25) | collective-permute-done | bytes 1638432 | tf_op jit(solution)/shard_map/ppermute | solution.py:401
  685.1 1.2 copy-done
  686.3 1.7 collective-permute-done.22.refs_0_
  688.0 1.2 copy-done.2
  689.7 1.3 copy-done.4
  690.9 30.2 %collective-permute-done.1.refs_0_ = bf16[160,5120]{1,0:T(8,128)(2,1)} collective-permute-done((bf16[160,5120]{1,0:T(8,128)(2,1)S(1)}, bf16[160,5120]{1,0:T(8,128)(2,1)}, u32[]{:S(2)}, u32[]{:S(2)}) %collective-permute-start.1) | collective-permute-done | bytes 1638432 | tf_op jit(solution)/shard_map/ppermute | solution.py:401
  721.6 1.2 copy-done.6
  722.9 1.2 copy-done.8
  724.6 1.2 copy-done.10
  725.8 4.2 place.17.refs_6_
  730.0 4.2 place.18.refs_6_
  734.2 7.7 place.26.refs_6_
  741.8 7.7 place.22.refs_6_
  749.5 7.7 place.19.refs_4_
  757.1 1.8 place.20.refs_2_
  758.9 2.5 place.27.refs_6_
  761.5 2.5 place.28.refs_6_
  764.0 2.5 place.29.refs_6_
  766.5 2.5 place.30.refs_2_
  769.1 7.8 place.23.refs_2_
  777.4 1.7 place.31.refs_4_
  780.6 1.7 place.24.refs_2_
  783.7 1.7 place.25
  785.4 3.7 place.21
  789.2 2.4 place.32.refs_4_
  791.6 2.4 place.33
  (208 shorter events, 30.0 us)
Async XLA Ops:
  344.4 13.5 %collective-permute-start.41 = (bf16[160,1280]{1,0:T(8,128)(2,1)}, bf16[160,1280]{1,0:T(8,128)(2,1)S(1)}, u32[]{:S(2)}, u32[]{:S(2)}) collective-permute-start(bf16[160,1280]{1,0:T(8,128)(2,1)} %get-tuple-element.68.refs_0_), channel_id=1, source_target_pairs={{0,4},{1,5},{2,6},{3,7},{4,0},{5,1},{6,2},{7,3}} | collective-permute-start | bytes 1228808 | tf_op jit(solution)/shard_map/ppermute | solution.py:401
  345.7 12.5 %collective-permute-start.62 = (bf16[160,1280]{1,0:T(8,128)(2,1)}, bf16[160,1280]{1,0:T(8,128)(2,1)S(1)}, u32[]{:S(2)}, u32[]{:S(2)}) collective-permute-start(bf16[160,1280]{1,0:T(8,128)(2,1)} %get-tuple-element.68.refs_0_), channel_id=1, source_target_pairs={{0,2},{1,3},{2,0},{3,1},{4,6},{5,7},{6,4},{7,5}} | collective-permute-start | bytes 1228808 | tf_op jit(solution)/shard_map/ppermute | solution.py:401
  346.6 12.6 %collective-permute-start.63 = (bf16[160,1280]{1,0:T(8,128)(2,1)}, bf16[160,1280]{1,0:T(8,128)(2,1)S(1)}, u32[]{:S(2)}, u32[]{:S(2)}) collective-permute-start(bf16[160,1280]{1,0:T(8,128)(2,1)} %get-tuple-element.68.refs_0_), channel_id=1, source_target_pairs={{0,1},{1,0},{2,3},{3,2},{4,5},{5,4},{6,7},{7,6}} | collective-permute-start | bytes 1228808 | tf_op jit(solution)/shard_map/ppermute | solution.py:401
  351.3 14.4 %collective-permute-start.58 = (bf16[160,1280]{1,0:T(8,128)(2,1)}, bf16[160,1280]{1,0:T(8,128)(2,1)S(1)}, u32[]{:S(2)}, u32[]{:S(2)}) collective-permute-start(bf16[160,1280]{1,0:T(8,128)(2,1)} %get-tuple-element.69.refs_0_), channel_id=1, source_target_pairs={{0,4},{1,5},{2,6},{3,7},{4,0},{5,1},{6,2},{7,3}} | collective-permute-start | bytes 1228808 | tf_op jit(solution)/shard_map/ppermute | solution.py:401
  352.8 14.2 %collective-permute-start.44 = (bf16[160,1280]{1,0:T(8,128)(2,1)}, bf16[160,1280]{1,0:T(8,128)(2,1)S(1)}, u32[]{:S(2)}, u32[]{:S(2)}) collective-permute-start(bf16[160,1280]{1,0:T(8,128)(2,1)} %get-tuple-element.69.refs_0_), channel_id=1, source_target_pairs={{0,2},{1,3},{2,0},{3,1},{4,6},{5,7},{6,4},{7,5}} | collective-permute-start | bytes 1228808 | tf_op jit(solution)/shard_map/ppermute | solution.py:401
  358.0 9.8 %collective-permute-start.59 = (bf16[160,1280]{1,0:T(8,128)(2,1)S(1)}, bf16[160,1280]{1,0:T(8,128)(2,1)S(1)}, u32[]{:S(2)}, u32[]{:S(2)}) collective-permute-start(bf16[160,1280]{1,0:T(8,128)(2,1)S(1)} %copy-done.38), channel_id=1, source_target_pairs={{0,1},{1,0},{2,3},{3,2},{4,5},{5,4},{6,7},{7,6}} | collective-permute-start | bytes 1228808 | tf_op jit(solution)/shard_map/ppermute | solution.py:401
  358.2 16.4 %collective-permute-start.35 = (bf16[160,1280]{1,0:T(8,128)(2,1)}, bf16[160,1280]{1,0:T(8,128)(2,1)}, u32[]{:S(2)}, u32[]{:S(2)}) collective-permute-start(bf16[160,1280]{1,0:T(8,128)(2,1)} %get-tuple-element.64.refs_0_), channel_id=1, source_target_pairs={{0,4},{1,5},{2,6},{3,7},{4,0},{5,1},{6,2},{7,3}} | collective-permute-start | bytes 1228808 | tf_op jit(solution)/shard_map/ppermute | solution.py:401
  359.3 16.6 %collective-permute-start.54 = (bf16[160,1280]{1,0:T(8,128)(2,1)}, bf16[160,1280]{1,0:T(8,128)(2,1)}, u32[]{:S(2)}, u32[]{:S(2)}) collective-permute-start(bf16[160,1280]{1,0:T(8,128)(2,1)} %get-tuple-element.64.refs_0_), channel_id=1, source_target_pairs={{0,2},{1,3},{2,0},{3,1},{4,6},{5,7},{6,4},{7,5}} | collective-permute-start | bytes 1228808 | tf_op jit(solution)/shard_map/ppermute | solution.py:401
  365.8 10.1 %collective-permute-start.55 = (bf16[160,1280]{1,0:T(8,128)(2,1)S(1)}, bf16[160,1280]{1,0:T(8,128)(2,1)S(1)}, u32[]{:S(2)}, u32[]{:S(2)}) collective-permute-start(bf16[160,1280]{1,0:T(8,128)(2,1)S(1)} %copy-done.40), channel_id=1, source_target_pairs={{0,1},{1,0},{2,3},{3,2},{4,5},{5,4},{6,7},{7,6}} | collective-permute-start | bytes 1228808 | tf_op jit(solution)/shard_map/ppermute | solution.py:401
  367.0 15.6 %collective-permute-start.50 = (bf16[160,1280]{1,0:T(8,128)(2,1)}, bf16[160,1280]{1,0:T(8,128)(2,1)}, u32[]{:S(2)}, u32[]{:S(2)}) collective-permute-start(bf16[160,1280]{1,0:T(8,128)(2,1)} %get-tuple-element.67.refs_0_), channel_id=1, source_target_pairs={{0,4},{1,5},{2,6},{3,7},{4,0},{5,1},{6,2},{7,3}} | collective-permute-start | bytes 1228808 | tf_op jit(solution)/shard_map/ppermute | solution.py:401
  367.8 15.6 %collective-permute-start.38 = (bf16[160,1280]{1,0:T(8,128)(2,1)}, bf16[160,1280]{1,0:T(8,128)(2,1)S(1)}, u32[]{:S(2)}, u32[]{:S(2)}) collective-permute-start(bf16[160,1280]{1,0:T(8,128)(2,1)} %get-tuple-element.67.refs_0_), channel_id=1, source_target_pairs={{0,2},{1,3},{2,0},{3,1},{4,6},{5,7},{6,4},{7,5}} | collective-permute-start | bytes 1228808 | tf_op jit(solution)/shard_map/ppermute | solution.py:401
  374.7 8.8 %collective-permute-start.51 = (bf16[160,1280]{1,0:T(8,128)(2,1)}, bf16[160,1280]{1,0:T(8,128)(2,1)S(1)}, u32[]{:S(2)}, u32[]{:S(2)}) collective-permute-start(bf16[160,1280]{1,0:T(8,128)(2,1)} %get-tuple-element.67.refs_0_), channel_id=1, source_target_pairs={{0,1},{1,0},{2,3},{3,2},{4,5},{5,4},{6,7},{7,6}} | collective-permute-start | bytes 1228808 | tf_op jit(solution)/shard_map/ppermute | solution.py:401
  375.9 8.1 %collective-permute-start.64 = (bf16[160,1280]{1,0:T(8,128)(2,1)S(1)}, bf16[160,1280]{1,0:T(8,128)(2,1)S(1)}, u32[]{:S(2)}, u32[]{:S(2)}) collective-permute-start(bf16[160,1280]{1,0:T(8,128)(2,1)S(1)} %collective-permute-done.41.refs_1_), channel_id=1, source_target_pairs={{0,1},{1,0},{2,3},{3,2},{4,5},{5,4},{6,7},{7,6}} | collective-permute-start | bytes 1228808 | tf_op jit(solution)/shard_map/ppermute | solution.py:401
  375.9 8.1 %collective-permute-start.65 = (bf16[160,1280]{1,0:T(8,128)(2,1)S(1)}, bf16[160,1280]{1,0:T(8,128)(2,1)S(1)}, u32[]{:S(2)}, u32[]{:S(2)}) collective-permute-start(bf16[160,1280]{1,0:T(8,128)(2,1)S(1)} %collective-permute-done.62.refs_2_), channel_id=1, source_target_pairs={{0,1},{1,0},{2,3},{3,2},{4,5},{5,4},{6,7},{7,6}} | collective-permute-start | bytes 1228808 | tf_op jit(solution)/shard_map/ppermute | solution.py:401
  383.9 3.7 collective-permute-start.57
  384.0 16.8 %collective-permute-start.52 = (bf16[160,1280]{1,0:T(8,128)(2,1)}, bf16[160,1280]{1,0:T(8,128)(2,1)}, u32[]{:S(2)}, u32[]{:S(2)}) collective-permute-start(bf16[160,1280]{1,0:T(8,128)(2,1)} %collective-permute-done.50.refs_1_), channel_id=1, source_target_pairs={{0,1},{1,0},{2,3},{3,2},{4,5},{5,4},{6,7},{7,6}} | collective-permute-start | bytes 1228808 | tf_op jit(solution)/shard_map/ppermute | solution.py:401
  384.5 17.0 %collective-permute-start.53 = (bf16[160,1280]{1,0:T(8,128)(2,1)S(1)}, bf16[160,1280]{1,0:T(8,128)(2,1)}, u32[]{:S(2)}, u32[]{:S(2)}) collective-permute-start(bf16[160,1280]{1,0:T(8,128)(2,1)S(1)} %collective-permute-done.38.refs_2_), channel_id=1, source_target_pairs={{0,1},{1,0},{2,3},{3,2},{4,5},{5,4},{6,7},{7,6}} | collective-permute-start | bytes 1228808 | tf_op jit(solution)/shard_map/ppermute | solution.py:401
  385.2 17.3 %collective-permute-start.45 = (bf16[160,1280]{1,0:T(8,128)(2,1)S(1)}, bf16[160,1280]{1,0:T(8,128)(2,1)S(1)}, u32[]{:S(2)}, u32[]{:S(2)}) collective-permute-start(bf16[160,1280]{1,0:T(8,128)(2,1)S(1)} %collective-permute-done.44.refs_2_), channel_id=1, source_target_pairs={{0,4},{1,5},{2,6},{3,7},{4,0},{5,1},{6,2},{7,3}} | collective-permute-start | bytes 1228808 | tf_op jit(solution)/shard_map/ppermute | solution.py:401
  386.1 17.8 %collective-permute-start.42 = (bf16[160,1280]{1,0:T(8,128)(2,1)S(1)}, bf16[160,1280]{1,0:T(8,128)(2,1)S(1)}, u32[]{:S(2)}, u32[]{:S(2)}) collective-permute-start(bf16[160,1280]{1,0:T(8,128)(2,1)S(1)} %collective-permute-done.41.refs_1_), channel_id=1, source_target_pairs={{0,2},{1,3},{2,0},{3,1},{4,6},{5,7},{6,4},{7,5}} | collective-permute-start | bytes 1228808 | tf_op jit(solution)/shard_map/ppermute | solution.py:401
  387.7 18.6 %collective-permute-start.39 = (bf16[160,1280]{1,0:T(8,128)(2,1)S(1)}, bf16[160,1280]{1,0:T(8,128)(2,1)S(1)}, u32[]{:S(2)}, u32[]{:S(2)}) collective-permute-start(bf16[160,1280]{1,0:T(8,128)(2,1)S(1)} %collective-permute-done.38.refs_2_), channel_id=1, source_target_pairs={{0,4},{1,5},{2,6},{3,7},{4,0},{5,1},{6,2},{7,3}} | collective-permute-start | bytes 1228808 | tf_op jit(solution)/shard_map/ppermute | solution.py:401
  400.8 38.4 %collective-permute-start.6 = (bf16[80,5120]{1,0:T(8,128)(2,1)}, bf16[80,5120]{1,0:T(8,128)(2,1)}, u32[]{:S(2)}, u32[]{:S(2)}) collective-permute-start(bf16[80,5120]{1,0:T(8,128)(2,1)} %get-tuple-element.51.refs_0_), channel_id=1, source_target_pairs={{0,2},{1,3},{2,0},{3,1},{4,6},{5,7},{6,4},{7,5}} | collective-permute-start | bytes 2457608 | tf_op jit(solution)/shard_map/ppermute | solution.py:401
  401.5 39.1 %collective-permute-start.13 = (bf16[80,5120]{1,0:T(8,128)(2,1)}, bf16[80,5120]{1,0:T(8,128)(2,1)}, u32[]{:S(2)}, u32[]{:S(2)}) collective-permute-start(bf16[80,5120]{1,0:T(8,128)(2,1)} %get-tuple-element.51.refs_0_), channel_id=1, source_target_pairs={{0,4},{1,5},{2,6},{3,7},{4,0},{5,1},{6,2},{7,3}} | collective-permute-start | bytes 2457608 | tf_op jit(solution)/shard_map/ppermute | solution.py:401
  402.4 26.9 %collective-permute-start.36 = (bf16[160,1280]{1,0:T(8,128)(2,1)}, bf16[160,1280]{1,0:T(8,128)(2,1)}, u32[]{:S(2)}, u32[]{:S(2)}) collective-permute-start(bf16[160,1280]{1,0:T(8,128)(2,1)} %collective-permute-done.35.refs_1_), channel_id=1, source_target_pairs={{0,2},{1,3},{2,0},{3,1},{4,6},{5,7},{6,4},{7,5}} | collective-permute-start | bytes 1228808 | tf_op jit(solution)/shard_map/ppermute | solution.py:401
  403.9 37.7 %collective-permute-start.14 = (bf16[80,5120]{1,0:T(8,128)(2,1)}, bf16[80,5120]{1,0:T(8,128)(2,1)}, u32[]{:S(2)}, u32[]{:S(2)}) collective-permute-start(bf16[80,5120]{1,0:T(8,128)(2,1)} %get-tuple-element.51.refs_0_), channel_id=1, source_target_pairs={{0,1},{1,0},{2,3},{3,2},{4,5},{5,4},{6,7},{7,6}} | collective-permute-start | bytes 2457608 | tf_op jit(solution)/shard_map/ppermute | solution.py:401
  406.3 35.3 %collective-permute-start.3 = (bf16[80,5120]{1,0:T(8,128)(2,1)}, bf16[80,5120]{1,0:T(8,128)(2,1)}, u32[]{:S(2)}, u32[]{:S(2)}) collective-permute-start(bf16[80,5120]{1,0:T(8,128)(2,1)} %get-tuple-element.50.refs_0_), channel_id=1, source_target_pairs={{0,4},{1,5},{2,6},{3,7},{4,0},{5,1},{6,2},{7,3}} | collective-permute-start | bytes 2457608 | tf_op jit(solution)/shard_map/ppermute | solution.py:401
  429.4 21.4 %collective-permute-start.17 = (bf16[80,5120]{1,0:T(8,128)(2,1)}, bf16[80,5120]{1,0:T(8,128)(2,1)}, u32[]{:S(2)}, u32[]{:S(2)}) collective-permute-start(bf16[80,5120]{1,0:T(8,128)(2,1)} %get-tuple-element.50.refs_0_), channel_id=1, source_target_pairs={{0,2},{1,3},{2,0},{3,1},{4,6},{5,7},{6,4},{7,5}} | collective-permute-start | bytes 2457608 | tf_op jit(solution)/shard_map/ppermute | solution.py:401
  439.2 46.7 %collective-permute-start.47 = (bf16[640,1280]{1,0:T(8,128)(2,1)S(1)}, bf16[640,1280]{1,0:T(8,128)(2,1)}, u32[]{:S(2)}, u32[]{:S(2)}) collective-permute-start(bf16[640,1280]{1,0:T(8,128)(2,1)S(1)} %copy-done.18), channel_id=1, source_target_pairs={{0,2},{1,3},{2,0},{3,1},{4,6},{5,7},{6,4},{7,5}} | collective-permute-start | bytes 4915208 | tf_op jit(solution)/shard_map/ppermute | solution.py:401
  440.5 45.4 %collective-permute-start.66 = (bf16[640,1280]{1,0:T(8,128)(2,1)S(1)}, bf16[640,1280]{1,0:T(8,128)(2,1)}, u32[]{:S(2)}, u32[]{:S(2)}) collective-permute-start(bf16[640,1280]{1,0:T(8,128)(2,1)S(1)} %copy-done.18), channel_id=1, source_target_pairs={{0,4},{1,5},{2,6},{3,7},{4,0},{5,1},{6,2},{7,3}} | collective-permute-start | bytes 4915208 | tf_op jit(solution)/shard_map/ppermute | solution.py:401
  441.6 45.4 %collective-permute-start.67 = (bf16[640,1280]{1,0:T(8,128)(2,1)S(1)}, bf16[640,1280]{1,0:T(8,128)(2,1)}, u32[]{:S(2)}, u32[]{:S(2)}) collective-permute-start(bf16[640,1280]{1,0:T(8,128)(2,1)S(1)} %copy-done.18), channel_id=1, source_target_pairs={{0,1},{1,0},{2,3},{3,2},{4,5},{5,4},{6,7},{7,6}} | collective-permute-start | bytes 4915208 | tf_op jit(solution)/shard_map/ppermute | solution.py:401
  441.6 79.4 %collective-permute-start.24 = (bf16[160,5120]{1,0:T(8,128)(2,1)}, bf16[160,5120]{1,0:T(8,128)(2,1)}, u32[]{:S(2)}, u32[]{:S(2)}) collective-permute-start(bf16[160,5120]{1,0:T(8,128)(2,1)} %get-tuple-element.56.refs_0_), channel_id=1, source_target_pairs={{0,2},{1,3},{2,0},{3,1},{4,6},{5,7},{6,4},{7,5}} | collective-permute-start | bytes 4915208 | tf_op jit(solution)/shard_map/ppermute | solution.py:401
  453.5 76.5 %collective-permute-start.31 = (bf16[160,5120]{1,0:T(8,128)(2,1)}, bf16[160,5120]{1,0:T(8,128)(2,1)}, u32[]{:S(2)}, u32[]{:S(2)}) collective-permute-start(bf16[160,5120]{1,0:T(8,128)(2,1)} %get-tuple-element.56.refs_0_), channel_id=1, source_target_pairs={{0,4},{1,5},{2,6},{3,7},{4,0},{5,1},{6,2},{7,3}} | collective-permute-start | bytes 4915208 | tf_op jit(solution)/shard_map/ppermute | solution.py:401
  485.9 45.2 %collective-permute-start.32 = (bf16[160,5120]{1,0:T(8,128)(2,1)}, bf16[160,5120]{1,0:T(8,128)(2,1)}, u32[]{:S(2)}, u32[]{:S(2)}) collective-permute-start(bf16[160,5120]{1,0:T(8,128)(2,1)} %get-tuple-element.56.refs_0_), channel_id=1, source_target_pairs={{0,1},{1,0},{2,3},{3,2},{4,5},{5,4},{6,7},{7,6}} | collective-permute-start | bytes 4915208 | tf_op jit(solution)/shard_map/ppermute | solution.py:401
  485.9 63.6 %collective-permute-start.21 = (bf16[160,5120]{1,0:T(8,128)(2,1)}, bf16[160,5120]{1,0:T(8,128)(2,1)}, u32[]{:S(2)}, u32[]{:S(2)}) collective-permute-start(bf16[160,5120]{1,0:T(8,128)(2,1)} %get-tuple-element.55.refs_0_), channel_id=1, source_target_pairs={{0,4},{1,5},{2,6},{3,7},{4,0},{5,1},{6,2},{7,3}} | collective-permute-start | bytes 4915208 | tf_op jit(solution)/shard_map/ppermute | solution.py:401
  487.0 66.5 %collective-permute-start.27 = (bf16[160,5120]{1,0:T(8,128)(2,1)}, bf16[160,5120]{1,0:T(8,128)(2,1)S(1)}, u32[]{:S(2)}, u32[]{:S(2)}) collective-permute-start(bf16[160,5120]{1,0:T(8,128)(2,1)} %get-tuple-element.55.refs_0_), channel_id=1, source_target_pairs={{0,2},{1,3},{2,0},{3,1},{4,6},{5,7},{6,4},{7,5}} | collective-permute-start | bytes 4915208 | tf_op jit(solution)/shard_map/ppermute | solution.py:401
  521.0 32.5 %collective-permute-start.28 = (bf16[160,5120]{1,0:T(8,128)(2,1)}, bf16[160,5120]{1,0:T(8,128)(2,1)S(1)}, u32[]{:S(2)}, u32[]{:S(2)}) collective-permute-start(bf16[160,5120]{1,0:T(8,128)(2,1)} %get-tuple-element.55.refs_0_), channel_id=1, source_target_pairs={{0,1},{1,0},{2,3},{3,2},{4,5},{5,4},{6,7},{7,6}} | collective-permute-start | bytes 4915208 | tf_op jit(solution)/shard_map/ppermute | solution.py:401
  530.0 54.6 %collective-permute-start = (bf16[160,5120]{1,0:T(8,128)(2,1)}, bf16[160,5120]{1,0:T(8,128)(2,1)S(1)}, u32[]{:S(2)}, u32[]{:S(2)}) collective-permute-start(bf16[160,5120]{1,0:T(8,128)(2,1)} %get-tuple-element.49.refs_0_), channel_id=1, source_target_pairs={{0,4},{1,5},{2,6},{3,7},{4,0},{5,1},{6,2},{7,3}} | collective-permute-start | bytes 4915208 | tf_op jit(solution)/shard_map/ppermute | solution.py:401
  531.1 22.9 %collective-permute-start.16 = (bf16[80,5120]{1,0:T(8,128)(2,1)}, bf16[80,5120]{1,0:T(8,128)(2,1)S(1)}, u32[]{:S(2)}, u32[]{:S(2)}) collective-permute-start(bf16[80,5120]{1,0:T(8,128)(2,1)} %collective-permute-done.6.refs_2_), channel_id=1, source_target_pairs={{0,1},{1,0},{2,3},{3,2},{4,5},{5,4},{6,7},{7,6}} | collective-permute-start | bytes 2457608 | tf_op jit(solution)/shard_map/ppermute | solution.py:401
  549.5 5.2 collective-permute-start.15
  553.5 3.7 collective-permute-start.20
  554.0 55.5 %collective-permute-start.9 = (bf16[160,5120]{1,0:T(8,128)(2,1)}, bf16[160,5120]{1,0:T(8,128)(2,1)S(1)}, u32[]{:S(2)}, u32[]{:S(2)}) collective-permute-start(bf16[160,5120]{1,0:T(8,128)(2,1)} %get-tuple-element.49.refs_0_), channel_id=1, source_target_pairs={{0,2},{1,3},{2,0},{3,1},{4,6},{5,7},{6,4},{7,5}} | collective-permute-start | bytes 4915208 | tf_op jit(solution)/shard_map/ppermute | solution.py:401
  554.8 55.3 %collective-permute-start.10 = (bf16[160,5120]{1,0:T(8,128)(2,1)}, bf16[160,5120]{1,0:T(8,128)(2,1)}, u32[]{:S(2)}, u32[]{:S(2)}) collective-permute-start(bf16[160,5120]{1,0:T(8,128)(2,1)} %get-tuple-element.49.refs_0_), channel_id=1, source_target_pairs={{0,1},{1,0},{2,3},{3,2},{4,5},{5,4},{6,7},{7,6}} | collective-permute-start | bytes 4915208 | tf_op jit(solution)/shard_map/ppermute | solution.py:401
  556.0 43.0 %collective-permute-start.7 = (bf16[80,5120]{1,0:T(8,128)(2,1)}, bf16[80,5120]{1,0:T(8,128)(2,1)S(1)}, u32[]{:S(2)}, u32[]{:S(2)}) collective-permute-start(bf16[80,5120]{1,0:T(8,128)(2,1)} %collective-permute-done.6.refs_2_), channel_id=1, source_target_pairs={{0,4},{1,5},{2,6},{3,7},{4,0},{5,1},{6,2},{7,3}} | collective-permute-start | bytes 2457608 | tf_op jit(solution)/shard_map/ppermute | solution.py:401
  557.2 52.3 %collective-permute-start.4 = (bf16[80,5120]{1,0:T(8,128)(2,1)}, bf16[80,5120]{1,0:T(8,128)(2,1)S(1)}, u32[]{:S(2)}, u32[]{:S(2)}) collective-permute-start(bf16[80,5120]{1,0:T(8,128)(2,1)} %collective-permute-done.3.refs_1_), channel_id=1, source_target_pairs={{0,2},{1,3},{2,0},{3,1},{4,6},{5,7},{6,4},{7,5}} | collective-permute-start | bytes 2457608 | tf_op jit(solution)/shard_map/ppermute | solution.py:401
  584.5 27.5 %collective-permute-start.69 = (bf16[640,1280]{1,0:T(8,128)(2,1)}, bf16[640,1280]{1,0:T(8,128)(2,1)S(1)}, u32[]{:S(2)}, u32[]{:S(2)}) collective-permute-start(bf16[640,1280]{1,0:T(8,128)(2,1)} %collective-permute-done.47.refs_2_), channel_id=1, source_target_pairs={{0,1},{1,0},{2,3},{3,2},{4,5},{5,4},{6,7},{7,6}} | collective-permute-start | bytes 4915208 | tf_op jit(solution)/shard_map/ppermute | solution.py:401
  599.0 12.1 %collective-permute-start.8 = (bf16[80,5120]{1,0:T(8,128)(2,1)S(1)}, bf16[80,5120]{1,0:T(8,128)(2,1)S(1)}, u32[]{:S(2)}, u32[]{:S(2)}) collective-permute-start(bf16[80,5120]{1,0:T(8,128)(2,1)S(1)} %collective-permute-done.7.refs_2_), channel_id=1, source_target_pairs={{0,1},{1,0},{2,3},{3,2},{4,5},{5,4},{6,7},{7,6}} | collective-permute-start | bytes 2457608 | tf_op jit(solution)/shard_map/ppermute | solution.py:401
  609.5 4.7 collective-permute-start.68
  610.1 38.0 %collective-permute-start.48 = (bf16[640,1280]{1,0:T(8,128)(2,1)}, bf16[640,1280]{1,0:T(8,128)(2,1)S(1)}, u32[]{:S(2)}, u32[]{:S(2)}) collective-permute-start(bf16[640,1280]{1,0:T(8,128)(2,1)} %collective-permute-done.47.refs_2_), channel_id=1, source_target_pairs={{0,4},{1,5},{2,6},{3,7},{4,0},{5,1},{6,2},{7,3}} | collective-permute-start | bytes 4915208 | tf_op jit(solution)/shard_map/ppermute | solution.py:401
  611.1 37.9 %collective-permute-start.34 = (bf16[160,5120]{1,0:T(8,128)(2,1)}, bf16[160,5120]{1,0:T(8,128)(2,1)S(1)}, u32[]{:S(2)}, u32[]{:S(2)}) collective-permute-start(bf16[160,5120]{1,0:T(8,128)(2,1)} %collective-permute-done.24.refs_2_), channel_id=1, source_target_pairs={{0,1},{1,0},{2,3},{3,2},{4,5},{5,4},{6,7},{7,6}} | collective-permute-start | bytes 4915208 | tf_op jit(solution)/shard_map/ppermute | solution.py:401
  611.9 37.9 %collective-permute-start.33 = (bf16[160,5120]{1,0:T(8,128)(2,1)}, bf16[160,5120]{1,0:T(8,128)(2,1)S(1)}, u32[]{:S(2)}, u32[]{:S(2)}) collective-permute-start(bf16[160,5120]{1,0:T(8,128)(2,1)} %collective-permute-done.31.refs_1_), channel_id=1, source_target_pairs={{0,1},{1,0},{2,3},{3,2},{4,5},{5,4},{6,7},{7,6}} | collective-permute-start | bytes 4915208 | tf_op jit(solution)/shard_map/ppermute | solution.py:401
  612.0 37.8 %collective-permute-start.29 = (bf16[160,5120]{1,0:T(8,128)(2,1)}, bf16[160,5120]{1,0:T(8,128)(2,1)S(1)}, u32[]{:S(2)}, u32[]{:S(2)}) collective-permute-start(bf16[160,5120]{1,0:T(8,128)(2,1)} %collective-permute-done.21.refs_1_), channel_id=1, source_target_pairs={{0,1},{1,0},{2,3},{3,2},{4,5},{5,4},{6,7},{7,6}} | collective-permute-start | bytes 4915208 | tf_op jit(solution)/shard_map/ppermute | solution.py:401
  614.2 37.0 %collective-permute-start.30 = (bf16[160,5120]{1,0:T(8,128)(2,1)}, bf16[160,5120]{1,0:T(8,128)(2,1)S(1)}, u32[]{:S(2)}, u32[]{:S(2)}) collective-permute-start(bf16[160,5120]{1,0:T(8,128)(2,1)} %copy-done.19), channel_id=1, source_target_pairs={{0,1},{1,0},{2,3},{3,2},{4,5},{5,4},{6,7},{7,6}} | collective-permute-start | bytes 4915208 | tf_op jit(solution)/shard_map/ppermute | solution.py:401
  648.0 37.1 %collective-permute-start.25 = (bf16[160,5120]{1,0:T(8,128)(2,1)}, bf16[160,5120]{1,0:T(8,128)(2,1)S(1)}, u32[]{:S(2)}, u32[]{:S(2)}) collective-permute-start(bf16[160,5120]{1,0:T(8,128)(2,1)} %collective-permute-done.24.refs_2_), channel_id=1, source_target_pairs={{0,4},{1,5},{2,6},{3,7},{4,0},{5,1},{6,2},{7,3}} | collective-permute-start | bytes 4915208 | tf_op jit(solution)/shard_map/ppermute | solution.py:401
  649.1 38.9 %collective-permute-start.22 = (bf16[160,5120]{1,0:T(8,128)(2,1)}, bf16[160,5120]{1,0:T(8,128)(2,1)S(1)}, u32[]{:S(2)}, u32[]{:S(2)}) collective-permute-start(bf16[160,5120]{1,0:T(8,128)(2,1)} %collective-permute-done.21.refs_1_), channel_id=1, source_target_pairs={{0,2},{1,3},{2,0},{3,1},{4,6},{5,7},{6,4},{7,5}} | collective-permute-start | bytes 4915208 | tf_op jit(solution)/shard_map/ppermute | solution.py:401
  649.8 39.4 %collective-permute-start.11 = (bf16[160,5120]{1,0:T(8,128)(2,1)S(1)}, bf16[160,5120]{1,0:T(8,128)(2,1)S(1)}, u32[]{:S(2)}, u32[]{:S(2)}) collective-permute-start(bf16[160,5120]{1,0:T(8,128)(2,1)S(1)} %collective-permute-done.refs_1_), channel_id=1, source_target_pairs={{0,1},{1,0},{2,3},{3,2},{4,5},{5,4},{6,7},{7,6}} | collective-permute-start | bytes 4915208 | tf_op jit(solution)/shard_map/ppermute | solution.py:401
  649.8 71.3 %collective-permute-start.1 = (bf16[160,5120]{1,0:T(8,128)(2,1)S(1)}, bf16[160,5120]{1,0:T(8,128)(2,1)}, u32[]{:S(2)}, u32[]{:S(2)}) collective-permute-start(bf16[160,5120]{1,0:T(8,128)(2,1)S(1)} %collective-permute-done.refs_1_), channel_id=1, source_target_pairs={{0,2},{1,3},{2,0},{3,1},{4,6},{5,7},{6,4},{7,5}} | collective-permute-start | bytes 4915208 | tf_op jit(solution)/shard_map/ppermute | solution.py:401
  651.2 69.9 %collective-permute-start.12 = (bf16[160,5120]{1,0:T(8,128)(2,1)S(1)}, bf16[160,5120]{1,0:T(8,128)(2,1)S(1)}, u32[]{:S(2)}, u32[]{:S(2)}) collective-permute-start(bf16[160,5120]{1,0:T(8,128)(2,1)S(1)} %collective-permute-done.9.refs_2_), channel_id=1, source_target_pairs={{0,1},{1,0},{2,3},{3,2},{4,5},{5,4},{6,7},{7,6}} | collective-permute-start | bytes 4915208 | tf_op jit(solution)/shard_map/ppermute | solution.py:401
  685.1 36.5 %collective-permute-start.49 = (bf16[640,1280]{1,0:T(8,128)(2,1)S(1)}, bf16[640,1280]{1,0:T(8,128)(2,1)S(1)}, u32[]{:S(2)}, u32[]{:S(2)}) collective-permute-start(bf16[640,1280]{1,0:T(8,128)(2,1)S(1)} %collective-permute-done.48.refs_0_), channel_id=1, source_target_pairs={{0,1},{1,0},{2,3},{3,2},{4,5},{5,4},{6,7},{7,6}} | collective-permute-start | bytes 4915208 | tf_op jit(solution)/shard_map/ppermute | solution.py:401
  688.0 34.9 %collective-permute-start.26 = (bf16[160,5120]{1,0:T(8,128)(2,1)S(1)}, bf16[160,5120]{1,0:T(8,128)(2,1)S(1)}, u32[]{:S(2)}, u32[]{:S(2)}) collective-permute-start(bf16[160,5120]{1,0:T(8,128)(2,1)S(1)} %collective-permute-done.25.refs_0_), channel_id=1, source_target_pairs={{0,1},{1,0},{2,3},{3,2},{4,5},{5,4},{6,7},{7,6}} | collective-permute-start | bytes 4915208 | tf_op jit(solution)/shard_map/ppermute | solution.py:401
  689.2 35.4 %collective-permute-start.23 = (bf16[160,5120]{1,0:T(8,128)(2,1)S(1)}, bf16[160,5120]{1,0:T(8,128)(2,1)S(1)}, u32[]{:S(2)}, u32[]{:S(2)}) collective-permute-start(bf16[160,5120]{1,0:T(8,128)(2,1)S(1)} %collective-permute-done.22.refs_0_), channel_id=1, source_target_pairs={{0,1},{1,0},{2,3},{3,2},{4,5},{5,4},{6,7},{7,6}} | collective-permute-start | bytes 4915208 | tf_op jit(solution)/shard_map/ppermute | solution.py:401
  721.1 64.3 %collective-permute-start.2 = (bf16[160,5120]{1,0:T(8,128)(2,1)}, bf16[160,5120]{1,0:T(8,128)(2,1)}, u32[]{:S(2)}, u32[]{:S(2)}) collective-permute-start(bf16[160,5120]{1,0:T(8,128)(2,1)} %collective-permute-done.1.refs_0_), channel_id=1, source_target_pairs={{0,1},{1,0},{2,3},{3,2},{4,5},{5,4},{6,7},{7,6}} | collective-permute-start | bytes 4915208 | tf_op jit(solution)/shard_map/ppermute | solution.py:401
  721.1 68.0 %collective-permute-start.46 = (bf16[160,1280]{1,0:T(8,128)(2,1)}, bf16[160,1280]{1,0:T(8,128)(2,1)}, u32[]{:S(2)}, u32[]{:S(2)}) collective-permute-start(bf16[160,1280]{1,0:T(8,128)(2,1)} %copy-done.12), channel_id=1, source_target_pairs={{0,1},{1,0},{2,3},{3,2},{4,5},{5,4},{6,7},{7,6}} | collective-permute-start | bytes 1228808 | tf_op jit(solution)/shard_map/ppermute | solution.py:401
  722.8 66.3 %collective-permute-start.43 = (bf16[160,1280]{1,0:T(8,128)(2,1)}, bf16[160,1280]{1,0:T(8,128)(2,1)}, u32[]{:S(2)}, u32[]{:S(2)}) collective-permute-start(bf16[160,1280]{1,0:T(8,128)(2,1)} %copy-done.16), channel_id=1, source_target_pairs={{0,1},{1,0},{2,3},{3,2},{4,5},{5,4},{6,7},{7,6}} | collective-permute-start | bytes 1228808 | tf_op jit(solution)/shard_map/ppermute | solution.py:401
  724.1 67.5 %collective-permute-start.40 = (bf16[160,1280]{1,0:T(8,128)(2,1)}, bf16[160,1280]{1,0:T(8,128)(2,1)}, u32[]{:S(2)}, u32[]{:S(2)}) collective-permute-start(bf16[160,1280]{1,0:T(8,128)(2,1)} %copy-done.14), channel_id=1, source_target_pairs={{0,1},{1,0},{2,3},{3,2},{4,5},{5,4},{6,7},{7,6}} | collective-permute-start | bytes 1228808 | tf_op jit(solution)/shard_map/ppermute | solution.py:401
  725.8 65.8 %collective-permute-start.37 = (bf16[160,1280]{1,0:T(8,128)(2,1)}, bf16[160,1280]{1,0:T(8,128)(2,1)}, u32[]{:S(2)}, u32[]{:S(2)}) collective-permute-start(bf16[160,1280]{1,0:T(8,128)(2,1)} %collective-permute-done.36.refs_0_), channel_id=1, source_target_pairs={{0,1},{1,0},{2,3},{3,2},{4,5},{5,4},{6,7},{7,6}} | collective-permute-start | bytes 1228808 | tf_op jit(solution)/shard_map/ppermute | solution.py:401
  (58 other events, 989.4 us)

commit v6 on v5

--- a/solution.py
+++ b/solution.py
@@ -57,7 +57,7 @@
     near, refs = refs[:3], refs[3:]
     snd, rcv, own, par, refs = refs[0:2], refs[2:4], refs[4:6], refs[6:8], refs[8:]
     first, early, refs = refs[:4], refs[4], refs[5:]
-    acc, norms, d2d_s, d2d_r, link_s, link_r, own_sem, par_sem, out_sem, norm_s, norm_r, first_sem, early_sem, ready = refs
+    acc, mine_sum, norms, d2d_s, d2d_r, link_s, link_r, own_sem, par_sem, out_sem, norm_s, norm_r, first_sem, early_sem, ready = refs
     layers = g[0].shape[1]
     units = [(a, l) for a in range(3) for l in range(layers)]
     end = len(units) - 1
@@ -235,16 +235,18 @@
             load_mine(t + 1)
             load_theirs(t + 1)
 
+    ring = pl.ds(0, 7)
+    mine_sum[...] = jnp.sum(acc[...], axis=0, keepdims=True)
     for k in range(1, 8):
         pltpu.make_async_remote_copy(
-            src_ref=acc,
+            src_ref=mine_sum,
             dst_ref=norms.at[me],
             send_sem=norm_s.at[0],
             recv_sem=norm_r.at[0],
             device_id=(rep, lax.rem(me + k, 8)),
             device_id_type=MESH,
         ).start()
-    norms[me] = acc[...]
+    norms[me] = mine_sum[...]
     for one in ahead:
         one.wait()
     for a in range(3):
@@ -252,11 +254,10 @@
         all_of(near[a], d2d_s.at[a])
     for i, (a, l) in enumerate(units):
         all_of(snd[kind[a]].at[slot[a, l], pl.ds(0, 2)], link_s.at[1, i])
-    all_of(norms.at[pl.ds(0, 7)], norm_r.at[0])
+    all_of(norms.at[ring], norm_r.at[0])
     total = norms[0]
     for d in range(1, 8):
         total = total + norms[d]
-    total = jnp.sum(total, axis=0, keepdims=True)
     total = jnp.sum(total, axis=1, keepdims=True)
     squares[...] = jnp.broadcast_to(total, squares.shape)
 
@@ -264,16 +265,20 @@
 
     for i in range(head // 16):
         r = pl.ds(i * 16, 16)
-        first[3][r, :] = stepped_block(total, count, half[r, :], first[0][r, :], first[1][r, :], first[2][r, :])[0]
+        first[3][r, :] = stepped_block(total, count, half[r, :], *(one[r, :] for one in first[:3]))[0]
         pltpu.make_async_copy(first[3].at[r], new0.at[r], first_sem.at[3]).start()
-    all_of(norms.at[pl.ds(0, 7)], norm_s.at[0])
+    all_of(norms.at[ring], norm_s.at[0])
     all_of(new0, first_sem.at[3])
+
+
+def dma(*shape):
+    return pltpu.SemaphoreType.DMA(shape)
 
 
 def summed(terms, count, head, w, m, v):
     layers = terms[0].shape[1]
     shapes = [(t.shape[2] // 8, t.shape[3]) for t in terms]
-    halves = [(shapes[0][0] // 2, shapes[0][1]), (shapes[2][0] // 2, shapes[2][1])]
+    halves = [(n // 2, lanes) for n, lanes in shapes[::2]]
     counts = [2 * layers, layers]
     any_ = pl.BlockSpec(memory_space=pl.ANY)
     outs = pl.pallas_call(
@@ -291,18 +296,19 @@
         + [pltpu.VMEM((2, 16, shapes[0][1]), BF16)]
         + [
             pltpu.VMEM((16, 128), F32),
-            pltpu.VMEM((8, 16, 128), F32),
-            pltpu.SemaphoreType.DMA((3,)),
-            pltpu.SemaphoreType.DMA((4 + 3 * layers,)),
-            pltpu.SemaphoreType.DMA((2, 3 * layers)),
-            pltpu.SemaphoreType.DMA((9 * layers + 1,)),
-            pltpu.SemaphoreType.DMA((4,)),
-            pltpu.SemaphoreType.DMA((2,)),
-            pltpu.SemaphoreType.DMA((3,)),
-            pltpu.SemaphoreType.DMA((1,)),
-            pltpu.SemaphoreType.DMA((1,)),
-            pltpu.SemaphoreType.DMA((4,)),
-            pltpu.SemaphoreType.DMA((1,)),
+            pltpu.VMEM((1, 128), F32),
+            pltpu.VMEM((8, 1, 128), F32),
+            dma(3),
+            dma(4 + 3 * layers),
+            dma(2, 3 * layers),
+            dma(9 * layers + 1),
+            dma(4),
+            dma(2),
+            dma(3),
+            dma(1),
+            dma(1),
+            dma(4),
+            dma(1),
             pltpu.SemaphoreType.REGULAR((2,)),
         ],
         compiler_params=pltpu.CompilerParams(collective_id=0, has_side_effects=True, vmem_limit_bytes=62 * 1024 * 1024),
@@ -330,7 +336,7 @@
 def stepped(me, squares, count, unit, g, w, m, v, before, with_weight):
     layer, start, rows = unit
     whole, lanes = g.shape[1:]
-    n = rows // 5
+    n = rows if layer and rows < whole else rows // (2 if rows == whole else 5)
     here = pl.BlockSpec((1, n, lanes), lambda i, me: (layer, start // n + i, 0))
     specs = [
         pl.BlockSpec((8, 128), lambda i, me: (0, 0)),
@@ -359,17 +365,14 @@
     n = len(places)
     blocks, out = refs[:n], refs[n + n_before]
     out_sem, refs = refs[n + n_before + 1], refs[n + n_before + 2 :]
-    loads = []
     if not in_vmem:
-        held, in_sem = refs[:n], refs[n]
-        loads = [pltpu.make_async_copy(b, h, in_sem.at[i]) for i, (b, h) in enumerate(zip(blocks, held))]
-        blocks = held
-    for one in loads:
-        one.start()
+        held, in_sem = refs
+        for i in range(n):
+            pltpu.make_async_copy(blocks[i], held.at[i], in_sem.at[0]).start()
+        pltpu.make_async_copy(held, held, in_sem.at[0]).wait()
+        blocks = [held.at[i] for i in range(n)]
     stores = []
     for i, (offset, layer, start) in enumerate(places):
-        if loads:
-            loads[i].wait()
         at = pl.multiple_of(place(*offset) * (out.shape[1] // 8) + start, 16)
         stores.append(pltpu.make_async_copy(blocks[i], out.at[layer, pl.ds(at, blocks[i].shape[0])], out_sem.at[i]))
         stores[-1].start()
@@ -382,7 +385,7 @@
     any_ = pl.BlockSpec(memory_space=pl.ANY)
     scratch = [pltpu.SemaphoreType.DMA((n,))]
     if not in_vmem:
-        scratch += [pltpu.VMEM(b.shape, BF16) for b in blocks] + [pltpu.SemaphoreType.DMA((n,))]
+        scratch += [pltpu.VMEM((n, *blocks[0].shape), BF16), pltpu.SemaphoreType.DMA((1,))]
     return pl.pallas_call(
         functools.partial(place_kernel, places, len(before), in_vmem),
         out_shape=jax.ShapeDtypeStruct(shape, BF16),
@@ -438,15 +441,18 @@
         for i, (a, l, start, _) in enumerate(units):
             own, x, y, c = first[i]
             far, xc, yc = second[i]
-            places = [(at, l, start) for at in ((0, 0, 0), (1, 0, 0), (0, 1, 0), (0, 0, 1), (1, 0, 1), (0, 1, 1))]
-            whole[a] = placed([own, x, y, c, xc, yc], places, weights[a].shape, (whole[a],) if len(whole[a]) else ())
-        for group in groups:
+            places = [((*chip, core), l, start) for core in range(2) for chip in CHIPS[:0:-1]]
+            whole[a] = placed([own, y, x, c, yc, xc], places, weights[a].shape, (whole[a],) if len(whole[a]) else ())
+        for k, group in enumerate(groups):
             blocks, places = [], []
             for i in group:
                 a, l, start, _ = units[i]
                 far = second[i][0]
                 blocks += [far, send(far, dc=1)]
-                places += [((1, 1, 0), l, start), ((1, 1, 1), l, start)]
+                places += [((*CHIPS[0], core), l, start) for core in range(2)]
+            if k + 1 == len(groups):
+                whole[a] = placed(blocks[::2], places[::2], weights[a].shape, (whole[a],))
+                blocks, places = blocks[1::2], places[1::2]
             whole[a] = placed(blocks, places, weights[a].shape, (whole[a],), in_vmem=True)
         return (*whole, *new_m, *new_v)
 

time: 796 us -> 803 us (level)
  waiting for transfers between devices: 284 us -> 298 us
    ppermute x70, waiting for transfers between devices: 284 us -> 298 us  [send(): return lax.ppermute(block, 'dp', [(d, d ^ flip) for d in range(8)])]
    pallas_call x10, Pallas kernels: 66.9 us -> 55.6 us  [stepped(): pl.pallas_call(functools.partial(step_kernel, count, with_weight), out_sh...]
    pallas_call x17 -> x18, Pallas kernels: 64.6 us -> 72.4 us  [placed(): pl.pallas_call(functools.partial(place_kernel, places, len(before), in_vm...]
  transfers between devices with their start and end apart: 70 -> 70, of which waited for: 27 -> 28; matrix products, arithmetic and copies ran while one was open for 0% -> 0% of each run, Pallas kernels for 15% -> 14%
where the time goes in v6:
time: 803 us; the launch traced here: 802 us
  Pallas kernels  458 us (57%)
  waiting for transfers between devices  298 us (37%)
  starting transfers between devices  38.3 us (5%)
    pallas_call x1, Pallas kernels, summed(): pl.pallas_call(functools.partial(sum_kernel, shapes, count, head), out_sh...  330 us
    ppermute x70, waiting for transfers between devices, send(): return lax.ppermute(block, 'dp', [(d, d ^ flip) for d in range(8)])  298 us
    pallas_call x18, Pallas kernels, placed(): pl.pallas_call(functools.partial(place_kernel, places, len(before), in_vm...  72.4 us
    pallas_call x10, Pallas kernels, stepped(): pl.pallas_call(functools.partial(step_kernel, count, with_weight), out_sh...  55.6 us
    ppermute x70, starting transfers between devices, send(): return lax.ppermute(block, 'dp', [(d, d ^ flip) for d in range(8)])  38.3 us
  transfers between devices with their start and end apart: 70, of which 28 were waited for; matrix products, arithmetic and copies ran while one was open for 0% of the time, Pallas kernels for 14%

profile of v6, /device:TPU:0, one launch (start us, length us, event | category | flops | bytes accessed | tf_op | source)
XLA Modules:
  0.0 801.9 jit_solution(3846281994127531543)
XLA Ops:
  0.6 330.0 %sum_terms.1 = (bf16[2,160,5120]{2,1,0:T(8,128)(2,1)}, bf16[2,160,5120]{2,1,0:T(8,128)(2,1)}, bf16[2,640,1280]{2,1,0:T(8,128)(2,1)}, f32[8,128]{1,0:T(8,128)}, b...) custom-call(bf16[1,2,1280,5120]{3,2,1,0:T(8,128)(2,1)} %refs_0_.1, ...), custom_call_target="tpu_custom_call" | custom-call | tf_op jit(solution)/shard_map/sum_terms/pallas_call | solution.py:284
  330.7 7.5 adamw.15
  338.1 3.4 adamw.16
  341.5 1.3 collective-permute-start.41
  343.5 3.4 adamw.17
  346.9 1.3 collective-permute-start.44
  348.9 3.4 adamw.18
  352.3 1.7 collective-permute-done.41.refs_2_
  356.0 1.6 collective-permute-start.35
  357.6 3.4 adamw.19
  361.0 3.2 collective-permute-done.44.refs_1_
  364.9 1.6 collective-permute-start.50
  366.5 6.4 collective-permute-done.54.refs_1_
  373.5 6.7 collective-permute-done.38.refs_1_
  381.8 5.9 adamw.10
  387.7 6.3 adamw.11
  395.3 1.5 collective-permute-start.45
  397.3 1.3 collective-permute-start.39
  399.4 8.4 %collective-permute-done.45.refs_2_ = bf16[160,1280]{1,0:T(8,128)(2,1)S(1)} collective-permute-done((bf16[160,1280]{1,0:T(8,128)(2,1)}, bf16[160,1280]{1,0:T(8,128)(2,1)S(1)}, u32[]{:S(2)}, u32[]{:S(2)}) %collective-permute-start.45) | collective-permute-done | bytes 409632 | tf_op jit(solution)/shard_map/ppermute | solution.py:404
  407.8 1.5 collective-permute-start.13
  409.3 15.3 %collective-permute-done.42.refs_0_ = bf16[160,1280]{1,0:T(8,128)(2,1)S(1)} collective-permute-done((bf16[160,1280]{1,0:T(8,128)(2,1)}, bf16[160,1280]{1,0:T(8,128)(2,1)S(1)}, u32[]{:S(2)}, u32[]{:S(2)}) %collective-permute-start.42) | collective-permute-done | bytes 409632 | tf_op jit(solution)/shard_map/ppermute | solution.py:404
  425.4 7.3 collective-permute-done.36.refs_0_
  434.1 1.3 collective-permute-start.47
  436.6 7.4 adamw.13
  444.0 7.8 collective-permute-done.3.refs_2_
  451.8 2.2 collective-permute-done.17.refs_1_
  454.7 1.7 collective-permute-done.46.refs_3_
  457.3 1.6 collective-permute-done.43.refs_1_
  459.7 1.5 collective-permute-start.31
  461.2 7.5 adamw.14
  468.7 20.4 %collective-permute-done.47.refs_1_ = bf16[640,1280]{1,0:T(8,128)(2,1)} collective-permute-done((bf16[640,1280]{1,0:T(8,128)(2,1)S(1)}, bf16[640,1280]{1,0:T(8,128)(2,1)}, u32[]{:S(2)}, u32[]{:S(2)}) %collective-permute-start.47) | collective-permute-done | bytes 1638432 | tf_op jit(solution)/shard_map/ppermute | solution.py:404
  489.8 1.5 collective-permute-start.27
  491.3 32.8 %collective-permute-done.24.refs_1_ = bf16[160,5120]{1,0:T(8,128)(2,1)} collective-permute-done((bf16[160,5120]{1,0:T(8,128)(2,1)}, bf16[160,5120]{1,0:T(8,128)(2,1)}, u32[]{:S(2)}, u32[]{:S(2)}) %collective-permute-start.24) | collective-permute-done | bytes 1638432 | tf_op jit(solution)/shard_map/ppermute | solution.py:404
  524.2 7.4 adamw.12
  532.6 24.6 %collective-permute-done.21.refs_2_ = bf16[160,5120]{1,0:T(8,128)(2,1)} collective-permute-done((bf16[160,5120]{1,0:T(8,128)(2,1)}, bf16[160,5120]{1,0:T(8,128)(2,1)}, u32[]{:S(2)}, u32[]{:S(2)}) %collective-permute-start.21) | collective-permute-done | bytes 1638432 | tf_op jit(solution)/shard_map/ppermute | solution.py:404
  560.9 1.5 collective-permute-start.7
  563.4 28.8 %collective-permute-done.refs_2_ = bf16[160,5120]{1,0:T(8,128)(2,1)S(1)} collective-permute-done((bf16[160,5120]{1,0:T(8,128)(2,1)}, bf16[160,5120]{1,0:T(8,128)(2,1)S(1)}, u32[]{:S(2)}, u32[]{:S(2)}) %collective-permute-start) | collective-permute-done | bytes 1638432 | tf_op jit(solution)/shard_map/ppermute | solution.py:404
  592.1 16.6 %collective-permute-done.7.refs_2_ = bf16[80,5120]{1,0:T(8,128)(2,1)S(1)} collective-permute-done((bf16[80,5120]{1,0:T(8,128)(2,1)}, bf16[80,5120]{1,0:T(8,128)(2,1)S(1)}, u32[]{:S(2)}, u32[]{:S(2)}) %collective-permute-start.7) | collective-permute-done | bytes 819232 | tf_op jit(solution)/shard_map/ppermute | solution.py:404
  608.7 4.9 collective-permute-done.4.refs_0_
  614.2 1.5 collective-permute-start.48
  616.5 1.9 collective-permute-done.69.refs_5_
  618.6 33.5 %collective-permute-done.48.refs_0_ = bf16[640,1280]{1,0:T(8,128)(2,1)S(1)} collective-permute-done((bf16[640,1280]{1,0:T(8,128)(2,1)}, bf16[640,1280]{1,0:T(8,128)(2,1)S(1)}, u32[]{:S(2)}, u32[]{:S(2)}) %collective-permute-start.48) | collective-permute-done | bytes 1638432 | tf_op jit(solution)/shard_map/ppermute | solution.py:404
  652.2 1.5 collective-permute-start.25
  654.4 1.3 collective-permute-start.1
  656.0 33.4 %collective-permute-done.25.refs_0_ = bf16[160,5120]{1,0:T(8,128)(2,1)} collective-permute-done((bf16[160,5120]{1,0:T(8,128)(2,1)}, bf16[160,5120]{1,0:T(8,128)(2,1)}, u32[]{:S(2)}, u32[]{:S(2)}) %collective-permute-start.25) | collective-permute-done | bytes 1638432 | tf_op jit(solution)/shard_map/ppermute | solution.py:404
  690.6 2.1 collective-permute-done.22.refs_0_
  693.2 32.5 %collective-permute-done.1.refs_0_ = bf16[160,5120]{1,0:T(8,128)(2,1)} collective-permute-done((bf16[160,5120]{1,0:T(8,128)(2,1)S(1)}, bf16[160,5120]{1,0:T(8,128)(2,1)}, u32[]{:S(2)}, u32[]{:S(2)}) %collective-permute-start.1) | collective-permute-done | bytes 1638432 | tf_op jit(solution)/shard_map/ppermute | solution.py:404
  728.5 4.7 place.18.refs_6_
  733.2 4.7 place.19.refs_6_
  737.9 7.7 place.27.refs_6_
  745.6 7.7 place.23.refs_6_
  753.3 7.7 place.20.refs_4_
  761.0 1.8 place.21.refs_2_
  762.7 3.1 place.28.refs_6_
  765.9 3.1 place.29.refs_6_
  769.0 3.1 place.30.refs_6_
  772.1 3.1 place.31.refs_2_
  775.2 7.8 place.24.refs_2_
  783.1 1.7 place.32.refs_4_
  786.7 2.0 place.34.refs_2_
  788.7 3.6 place.25.refs_2_
  792.4 3.6 place.26
  796.1 3.6 place.22
  799.7 2.0 place.35
  (199 shorter events, 29.6 us)
Async XLA Ops:
  341.5 12.5 %collective-permute-start.41 = (bf16[160,1280]{1,0:T(8,128)(2,1)}, bf16[160,1280]{1,0:T(8,128)(2,1)S(1)}, u32[]{:S(2)}, u32[]{:S(2)}) collective-permute-start(bf16[160,1280]{1,0:T(8,128)(2,1)} %get-tuple-element.68.refs_0_), channel_id=1, source_target_pairs={{0,4},{1,5},{2,6},{3,7},{4,0},{5,1},{6,2},{7,3}} | collective-permute-start | bytes 1228808 | tf_op jit(solution)/shard_map/ppermute | solution.py:404
  342.8 12.6 %collective-permute-start.62 = (bf16[160,1280]{1,0:T(8,128)(2,1)}, bf16[160,1280]{1,0:T(8,128)(2,1)S(1)}, u32[]{:S(2)}, u32[]{:S(2)}) collective-permute-start(bf16[160,1280]{1,0:T(8,128)(2,1)} %get-tuple-element.68.refs_0_), channel_id=1, source_target_pairs={{0,2},{1,3},{2,0},{3,1},{4,6},{5,7},{6,4},{7,5}} | collective-permute-start | bytes 1228808 | tf_op jit(solution)/shard_map/ppermute | solution.py:404
  343.5 12.6 %collective-permute-start.63 = (bf16[160,1280]{1,0:T(8,128)(2,1)}, bf16[160,1280]{1,0:T(8,128)(2,1)S(1)}, u32[]{:S(2)}, u32[]{:S(2)}) collective-permute-start(bf16[160,1280]{1,0:T(8,128)(2,1)} %get-tuple-element.68.refs_0_), channel_id=1, source_target_pairs={{0,1},{1,0},{2,3},{3,2},{4,5},{5,4},{6,7},{7,6}} | collective-permute-start | bytes 1228808 | tf_op jit(solution)/shard_map/ppermute | solution.py:404
  346.9 17.3 %collective-permute-start.44 = (bf16[160,1280]{1,0:T(8,128)(2,1)}, bf16[160,1280]{1,0:T(8,128)(2,1)}, u32[]{:S(2)}, u32[]{:S(2)}) collective-permute-start(bf16[160,1280]{1,0:T(8,128)(2,1)} %get-tuple-element.69.refs_0_), channel_id=1, source_target_pairs={{0,2},{1,3},{2,0},{3,1},{4,6},{5,7},{6,4},{7,5}} | collective-permute-start | bytes 1228808 | tf_op jit(solution)/shard_map/ppermute | solution.py:404
  348.2 16.0 %collective-permute-start.58 = (bf16[160,1280]{1,0:T(8,128)(2,1)}, bf16[160,1280]{1,0:T(8,128)(2,1)S(1)}, u32[]{:S(2)}, u32[]{:S(2)}) collective-permute-start(bf16[160,1280]{1,0:T(8,128)(2,1)} %get-tuple-element.69.refs_0_), channel_id=1, source_target_pairs={{0,4},{1,5},{2,6},{3,7},{4,0},{5,1},{6,2},{7,3}} | collective-permute-start | bytes 1228808 | tf_op jit(solution)/shard_map/ppermute | solution.py:404
  354.1 10.9 %collective-permute-start.59 = (bf16[160,1280]{1,0:T(8,128)(2,1)S(1)}, bf16[160,1280]{1,0:T(8,128)(2,1)S(1)}, u32[]{:S(2)}, u32[]{:S(2)}) collective-permute-start(bf16[160,1280]{1,0:T(8,128)(2,1)S(1)} %copy-done.34), channel_id=1, source_target_pairs={{0,1},{1,0},{2,3},{3,2},{4,5},{5,4},{6,7},{7,6}} | collective-permute-start | bytes 1228808 | tf_op jit(solution)/shard_map/ppermute | solution.py:404
  355.3 17.7 %collective-permute-start.54 = (bf16[160,1280]{1,0:T(8,128)(2,1)}, bf16[160,1280]{1,0:T(8,128)(2,1)}, u32[]{:S(2)}, u32[]{:S(2)}) collective-permute-start(bf16[160,1280]{1,0:T(8,128)(2,1)} %get-tuple-element.64.refs_0_), channel_id=1, source_target_pairs={{0,2},{1,3},{2,0},{3,1},{4,6},{5,7},{6,4},{7,5}} | collective-permute-start | bytes 1228808 | tf_op jit(solution)/shard_map/ppermute | solution.py:404
  356.0 17.0 %collective-permute-start.35 = (bf16[160,1280]{1,0:T(8,128)(2,1)}, bf16[160,1280]{1,0:T(8,128)(2,1)}, u32[]{:S(2)}, u32[]{:S(2)}) collective-permute-start(bf16[160,1280]{1,0:T(8,128)(2,1)} %get-tuple-element.64.refs_0_), channel_id=1, source_target_pairs={{0,4},{1,5},{2,6},{3,7},{4,0},{5,1},{6,2},{7,3}} | collective-permute-start | bytes 1228808 | tf_op jit(solution)/shard_map/ppermute | solution.py:404
  364.2 9.3 %collective-permute-start.55 = (bf16[160,1280]{1,0:T(8,128)(2,1)S(1)}, bf16[160,1280]{1,0:T(8,128)(2,1)S(1)}, u32[]{:S(2)}, u32[]{:S(2)}) collective-permute-start(bf16[160,1280]{1,0:T(8,128)(2,1)S(1)} %copy-done.35), channel_id=1, source_target_pairs={{0,1},{1,0},{2,3},{3,2},{4,5},{5,4},{6,7},{7,6}} | collective-permute-start | bytes 1228808 | tf_op jit(solution)/shard_map/ppermute | solution.py:404
  364.2 16.0 %collective-permute-start.38 = (bf16[160,1280]{1,0:T(8,128)(2,1)}, bf16[160,1280]{1,0:T(8,128)(2,1)S(1)}, u32[]{:S(2)}, u32[]{:S(2)}) collective-permute-start(bf16[160,1280]{1,0:T(8,128)(2,1)} %get-tuple-element.67.refs_0_), channel_id=1, source_target_pairs={{0,2},{1,3},{2,0},{3,1},{4,6},{5,7},{6,4},{7,5}} | collective-permute-start | bytes 1228808 | tf_op jit(solution)/shard_map/ppermute | solution.py:404
  364.9 15.3 %collective-permute-start.50 = (bf16[160,1280]{1,0:T(8,128)(2,1)}, bf16[160,1280]{1,0:T(8,128)(2,1)S(1)}, u32[]{:S(2)}, u32[]{:S(2)}) collective-permute-start(bf16[160,1280]{1,0:T(8,128)(2,1)} %get-tuple-element.67.refs_0_), channel_id=1, source_target_pairs={{0,4},{1,5},{2,6},{3,7},{4,0},{5,1},{6,2},{7,3}} | collective-permute-start | bytes 1228808 | tf_op jit(solution)/shard_map/ppermute | solution.py:404
  373.0 7.8 collective-permute-start.51
  373.0 7.8 collective-permute-start.65
  373.5 20.5 %collective-permute-start.64 = (bf16[160,1280]{1,0:T(8,128)(2,1)S(1)}, bf16[160,1280]{1,0:T(8,128)(2,1)}, u32[]{:S(2)}, u32[]{:S(2)}) collective-permute-start(bf16[160,1280]{1,0:T(8,128)(2,1)S(1)} %collective-permute-done.62.refs_1_), channel_id=1, source_target_pairs={{0,1},{1,0},{2,3},{3,2},{4,5},{5,4},{6,7},{7,6}} | collective-permute-start | bytes 1228808 | tf_op jit(solution)/shard_map/ppermute | solution.py:404
  380.2 14.1 %collective-permute-start.60 = (bf16[160,1280]{1,0:T(8,128)(2,1)}, bf16[160,1280]{1,0:T(8,128)(2,1)}, u32[]{:S(2)}, u32[]{:S(2)}) collective-permute-start(bf16[160,1280]{1,0:T(8,128)(2,1)} %collective-permute-done.44.refs_1_), channel_id=1, source_target_pairs={{0,1},{1,0},{2,3},{3,2},{4,5},{5,4},{6,7},{7,6}} | collective-permute-start | bytes 1228808 | tf_op jit(solution)/shard_map/ppermute | solution.py:404
  380.2 14.3 %collective-permute-start.61 = (bf16[160,1280]{1,0:T(8,128)(2,1)S(1)}, bf16[160,1280]{1,0:T(8,128)(2,1)}, u32[]{:S(2)}, u32[]{:S(2)}) collective-permute-start(bf16[160,1280]{1,0:T(8,128)(2,1)S(1)} %collective-permute-done.58.refs_2_), channel_id=1, source_target_pairs={{0,1},{1,0},{2,3},{3,2},{4,5},{5,4},{6,7},{7,6}} | collective-permute-start | bytes 1228808 | tf_op jit(solution)/shard_map/ppermute | solution.py:404
  380.7 14.5 %collective-permute-start.56 = (bf16[160,1280]{1,0:T(8,128)(2,1)}, bf16[160,1280]{1,0:T(8,128)(2,1)}, u32[]{:S(2)}, u32[]{:S(2)}) collective-permute-start(bf16[160,1280]{1,0:T(8,128)(2,1)} %collective-permute-done.54.refs_1_), channel_id=1, source_target_pairs={{0,1},{1,0},{2,3},{3,2},{4,5},{5,4},{6,7},{7,6}} | collective-permute-start | bytes 1228808 | tf_op jit(solution)/shard_map/ppermute | solution.py:404
  381.0 15.8 %collective-permute-start.57 = (bf16[160,1280]{1,0:T(8,128)(2,1)}, bf16[160,1280]{1,0:T(8,128)(2,1)}, u32[]{:S(2)}, u32[]{:S(2)}) collective-permute-start(bf16[160,1280]{1,0:T(8,128)(2,1)} %collective-permute-done.35.refs_2_), channel_id=1, source_target_pairs={{0,1},{1,0},{2,3},{3,2},{4,5},{5,4},{6,7},{7,6}} | collective-permute-start | bytes 1228808 | tf_op jit(solution)/shard_map/ppermute | solution.py:404
  394.3 4.3 collective-permute-start.53
  394.6 38.9 %collective-permute-start.6 = (bf16[80,5120]{1,0:T(8,128)(2,1)}, bf16[80,5120]{1,0:T(8,128)(2,1)S(1)}, u32[]{:S(2)}, u32[]{:S(2)}) collective-permute-start(bf16[80,5120]{1,0:T(8,128)(2,1)} %get-tuple-element.51.refs_0_), channel_id=1, source_target_pairs={{0,2},{1,3},{2,0},{3,1},{4,6},{5,7},{6,4},{7,5}} | collective-permute-start | bytes 2457608 | tf_op jit(solution)/shard_map/ppermute | solution.py:404
  395.3 12.5 %collective-permute-start.45 = (bf16[160,1280]{1,0:T(8,128)(2,1)}, bf16[160,1280]{1,0:T(8,128)(2,1)S(1)}, u32[]{:S(2)}, u32[]{:S(2)}) collective-permute-start(bf16[160,1280]{1,0:T(8,128)(2,1)} %collective-permute-done.44.refs_1_), channel_id=1, source_target_pairs={{0,4},{1,5},{2,6},{3,7},{4,0},{5,1},{6,2},{7,3}} | collective-permute-start | bytes 1228808 | tf_op jit(solution)/shard_map/ppermute | solution.py:404
  396.8 27.9 %collective-permute-start.42 = (bf16[160,1280]{1,0:T(8,128)(2,1)}, bf16[160,1280]{1,0:T(8,128)(2,1)S(1)}, u32[]{:S(2)}, u32[]{:S(2)}) collective-permute-start(bf16[160,1280]{1,0:T(8,128)(2,1)} %copy-done.31), channel_id=1, source_target_pairs={{0,2},{1,3},{2,0},{3,1},{4,6},{5,7},{6,4},{7,5}} | collective-permute-start | bytes 1228808 | tf_op jit(solution)/shard_map/ppermute | solution.py:404
  397.3 27.4 %collective-permute-start.39 = (bf16[160,1280]{1,0:T(8,128)(2,1)}, bf16[160,1280]{1,0:T(8,128)(2,1)S(1)}, u32[]{:S(2)}, u32[]{:S(2)}) collective-permute-start(bf16[160,1280]{1,0:T(8,128)(2,1)} %copy-done.39), channel_id=1, source_target_pairs={{0,4},{1,5},{2,6},{3,7},{4,0},{5,1},{6,2},{7,3}} | collective-permute-start | bytes 1228808 | tf_op jit(solution)/shard_map/ppermute | solution.py:404
  398.6 34.1 %collective-permute-start.36 = (bf16[160,1280]{1,0:T(8,128)(2,1)}, bf16[160,1280]{1,0:T(8,128)(2,1)S(1)}, u32[]{:S(2)}, u32[]{:S(2)}) collective-permute-start(bf16[160,1280]{1,0:T(8,128)(2,1)} %collective-permute-done.35.refs_2_), channel_id=1, source_target_pairs={{0,2},{1,3},{2,0},{3,1},{4,6},{5,7},{6,4},{7,5}} | collective-permute-start | bytes 1228808 | tf_op jit(solution)/shard_map/ppermute | solution.py:404
  407.8 26.3 %collective-permute-start.13 = (bf16[80,5120]{1,0:T(8,128)(2,1)}, bf16[80,5120]{1,0:T(8,128)(2,1)S(1)}, u32[]{:S(2)}, u32[]{:S(2)}) collective-permute-start(bf16[80,5120]{1,0:T(8,128)(2,1)} %get-tuple-element.51.refs_0_), channel_id=1, source_target_pairs={{0,4},{1,5},{2,6},{3,7},{4,0},{5,1},{6,2},{7,3}} | collective-permute-start | bytes 2457608 | tf_op jit(solution)/shard_map/ppermute | solution.py:404
  424.7 10.8 %collective-permute-start.14 = (bf16[80,5120]{1,0:T(8,128)(2,1)}, bf16[80,5120]{1,0:T(8,128)(2,1)S(1)}, u32[]{:S(2)}, u32[]{:S(2)}) collective-permute-start(bf16[80,5120]{1,0:T(8,128)(2,1)} %get-tuple-element.51.refs_0_), channel_id=1, source_target_pairs={{0,1},{1,0},{2,3},{3,2},{4,5},{5,4},{6,7},{7,6}} | collective-permute-start | bytes 2457608 | tf_op jit(solution)/shard_map/ppermute | solution.py:404
  424.7 27.1 %collective-permute-start.3 = (bf16[80,5120]{1,0:T(8,128)(2,1)S(1)}, bf16[80,5120]{1,0:T(8,128)(2,1)}, u32[]{:S(2)}, u32[]{:S(2)}) collective-permute-start(bf16[80,5120]{1,0:T(8,128)(2,1)S(1)} %copy-done.23), channel_id=1, source_target_pairs={{0,4},{1,5},{2,6},{3,7},{4,0},{5,1},{6,2},{7,3}} | collective-permute-start | bytes 2457608 | tf_op jit(solution)/shard_map/ppermute | solution.py:404
  432.7 21.2 %collective-permute-start.17 = (bf16[80,5120]{1,0:T(8,128)(2,1)S(1)}, bf16[80,5120]{1,0:T(8,128)(2,1)}, u32[]{:S(2)}, u32[]{:S(2)}) collective-permute-start(bf16[80,5120]{1,0:T(8,128)(2,1)S(1)} %copy-done.23), channel_id=1, source_target_pairs={{0,2},{1,3},{2,0},{3,1},{4,6},{5,7},{6,4},{7,5}} | collective-permute-start | bytes 2457608 | tf_op jit(solution)/shard_map/ppermute | solution.py:404
  433.4 21.2 %collective-permute-start.18 = (bf16[80,5120]{1,0:T(8,128)(2,1)S(1)}, bf16[80,5120]{1,0:T(8,128)(2,1)}, u32[]{:S(2)}, u32[]{:S(2)}) collective-permute-start(bf16[80,5120]{1,0:T(8,128)(2,1)S(1)} %copy-done.23), channel_id=1, source_target_pairs={{0,1},{1,0},{2,3},{3,2},{4,5},{5,4},{6,7},{7,6}} | collective-permute-start | bytes 2457608 | tf_op jit(solution)/shard_map/ppermute | solution.py:404
  434.1 54.9 %collective-permute-start.47 = (bf16[640,1280]{1,0:T(8,128)(2,1)S(1)}, bf16[640,1280]{1,0:T(8,128)(2,1)}, u32[]{:S(2)}, u32[]{:S(2)}) collective-permute-start(bf16[640,1280]{1,0:T(8,128)(2,1)S(1)} %copy-done.12), channel_id=1, source_target_pairs={{0,2},{1,3},{2,0},{3,1},{4,6},{5,7},{6,4},{7,5}} | collective-permute-start | bytes 4915208 | tf_op jit(solution)/shard_map/ppermute | solution.py:404
  435.5 53.6 %collective-permute-start.66 = (bf16[640,1280]{1,0:T(8,128)(2,1)S(1)}, bf16[640,1280]{1,0:T(8,128)(2,1)}, u32[]{:S(2)}, u32[]{:S(2)}) collective-permute-start(bf16[640,1280]{1,0:T(8,128)(2,1)S(1)} %copy-done.12), channel_id=1, source_target_pairs={{0,4},{1,5},{2,6},{3,7},{4,0},{5,1},{6,2},{7,3}} | collective-permute-start | bytes 4915208 | tf_op jit(solution)/shard_map/ppermute | solution.py:404
  451.8 38.0 %collective-permute-start.67 = (bf16[640,1280]{1,0:T(8,128)(2,1)S(1)}, bf16[640,1280]{1,0:T(8,128)(2,1)}, u32[]{:S(2)}, u32[]{:S(2)}) collective-permute-start(bf16[640,1280]{1,0:T(8,128)(2,1)S(1)} %copy-done.12), channel_id=1, source_target_pairs={{0,1},{1,0},{2,3},{3,2},{4,5},{5,4},{6,7},{7,6}} | collective-permute-start | bytes 4915208 | tf_op jit(solution)/shard_map/ppermute | solution.py:404
  454.0 70.2 %collective-permute-start.24 = (bf16[160,5120]{1,0:T(8,128)(2,1)}, bf16[160,5120]{1,0:T(8,128)(2,1)}, u32[]{:S(2)}, u32[]{:S(2)}) collective-permute-start(bf16[160,5120]{1,0:T(8,128)(2,1)} %get-tuple-element.56.refs_0_), channel_id=1, source_target_pairs={{0,2},{1,3},{2,0},{3,1},{4,6},{5,7},{6,4},{7,5}} | collective-permute-start | bytes 4915208 | tf_op jit(solution)/shard_map/ppermute | solution.py:404
  459.7 71.9 %collective-permute-start.31 = (bf16[160,5120]{1,0:T(8,128)(2,1)}, bf16[160,5120]{1,0:T(8,128)(2,1)}, u32[]{:S(2)}, u32[]{:S(2)}) collective-permute-start(bf16[160,5120]{1,0:T(8,128)(2,1)} %get-tuple-element.56.refs_0_), channel_id=1, source_target_pairs={{0,4},{1,5},{2,6},{3,7},{4,0},{5,1},{6,2},{7,3}} | collective-permute-start | bytes 4915208 | tf_op jit(solution)/shard_map/ppermute | solution.py:404
  489.1 43.3 %collective-permute-start.32 = (bf16[160,5120]{1,0:T(8,128)(2,1)S(1)}, bf16[160,5120]{1,0:T(8,128)(2,1)}, u32[]{:S(2)}, u32[]{:S(2)}) collective-permute-start(bf16[160,5120]{1,0:T(8,128)(2,1)S(1)} %copy-done.13), channel_id=1, source_target_pairs={{0,1},{1,0},{2,3},{3,2},{4,5},{5,4},{6,7},{7,6}} | collective-permute-start | bytes 4915208 | tf_op jit(solution)/shard_map/ppermute | solution.py:404
  489.1 68.0 %collective-permute-start.21 = (bf16[160,5120]{1,0:T(8,128)(2,1)}, bf16[160,5120]{1,0:T(8,128)(2,1)}, u32[]{:S(2)}, u32[]{:S(2)}) collective-permute-start(bf16[160,5120]{1,0:T(8,128)(2,1)} %get-tuple-element.55.refs_0_), channel_id=1, source_target_pairs={{0,4},{1,5},{2,6},{3,7},{4,0},{5,1},{6,2},{7,3}} | collective-permute-start | bytes 4915208 | tf_op jit(solution)/shard_map/ppermute | solution.py:404
  489.8 67.8 %collective-permute-start.27 = (bf16[160,5120]{1,0:T(8,128)(2,1)}, bf16[160,5120]{1,0:T(8,128)(2,1)S(1)}, u32[]{:S(2)}, u32[]{:S(2)}) collective-permute-start(bf16[160,5120]{1,0:T(8,128)(2,1)} %get-tuple-element.55.refs_0_), channel_id=1, source_target_pairs={{0,2},{1,3},{2,0},{3,1},{4,6},{5,7},{6,4},{7,5}} | collective-permute-start | bytes 4915208 | tf_op jit(solution)/shard_map/ppermute | solution.py:404
  524.2 33.5 %collective-permute-start.28 = (bf16[160,5120]{1,0:T(8,128)(2,1)}, bf16[160,5120]{1,0:T(8,128)(2,1)}, u32[]{:S(2)}, u32[]{:S(2)}) collective-permute-start(bf16[160,5120]{1,0:T(8,128)(2,1)} %get-tuple-element.55.refs_0_), channel_id=1, source_target_pairs={{0,1},{1,0},{2,3},{3,2},{4,5},{5,4},{6,7},{7,6}} | collective-permute-start | bytes 4915208 | tf_op jit(solution)/shard_map/ppermute | solution.py:404
  531.6 60.5 %collective-permute-start = (bf16[160,5120]{1,0:T(8,128)(2,1)}, bf16[160,5120]{1,0:T(8,128)(2,1)S(1)}, u32[]{:S(2)}, u32[]{:S(2)}) collective-permute-start(bf16[160,5120]{1,0:T(8,128)(2,1)} %get-tuple-element.49.refs_0_), channel_id=1, source_target_pairs={{0,4},{1,5},{2,6},{3,7},{4,0},{5,1},{6,2},{7,3}} | collective-permute-start | bytes 4915208 | tf_op jit(solution)/shard_map/ppermute | solution.py:404
  532.3 25.8 %collective-permute-start.15 = (bf16[80,5120]{1,0:T(8,128)(2,1)}, bf16[80,5120]{1,0:T(8,128)(2,1)S(1)}, u32[]{:S(2)}, u32[]{:S(2)}) collective-permute-start(bf16[80,5120]{1,0:T(8,128)(2,1)} %copy-done.26), channel_id=1, source_target_pairs={{0,1},{1,0},{2,3},{3,2},{4,5},{5,4},{6,7},{7,6}} | collective-permute-start | bytes 2457608 | tf_op jit(solution)/shard_map/ppermute | solution.py:404
  557.7 4.7 collective-permute-start.19
  558.2 55.5 %collective-permute-start.9 = (bf16[160,5120]{1,0:T(8,128)(2,1)}, bf16[160,5120]{1,0:T(8,128)(2,1)S(1)}, u32[]{:S(2)}, u32[]{:S(2)}) collective-permute-start(bf16[160,5120]{1,0:T(8,128)(2,1)} %get-tuple-element.49.refs_0_), channel_id=1, source_target_pairs={{0,2},{1,3},{2,0},{3,1},{4,6},{5,7},{6,4},{7,5}} | collective-permute-start | bytes 4915208 | tf_op jit(solution)/shard_map/ppermute | solution.py:404
  559.7 54.5 %collective-permute-start.10 = (bf16[160,5120]{1,0:T(8,128)(2,1)}, bf16[160,5120]{1,0:T(8,128)(2,1)}, u32[]{:S(2)}, u32[]{:S(2)}) collective-permute-start(bf16[160,5120]{1,0:T(8,128)(2,1)} %get-tuple-element.49.refs_0_), channel_id=1, source_target_pairs={{0,1},{1,0},{2,3},{3,2},{4,5},{5,4},{6,7},{7,6}} | collective-permute-start | bytes 4915208 | tf_op jit(solution)/shard_map/ppermute | solution.py:404
  560.9 47.9 %collective-permute-start.7 = (bf16[80,5120]{1,0:T(8,128)(2,1)}, bf16[80,5120]{1,0:T(8,128)(2,1)S(1)}, u32[]{:S(2)}, u32[]{:S(2)}) collective-permute-start(bf16[80,5120]{1,0:T(8,128)(2,1)} %copy-done.26), channel_id=1, source_target_pairs={{0,4},{1,5},{2,6},{3,7},{4,0},{5,1},{6,2},{7,3}} | collective-permute-start | bytes 2457608 | tf_op jit(solution)/shard_map/ppermute | solution.py:404
  562.4 51.3 %collective-permute-start.4 = (bf16[80,5120]{1,0:T(8,128)(2,1)}, bf16[80,5120]{1,0:T(8,128)(2,1)S(1)}, u32[]{:S(2)}, u32[]{:S(2)}) collective-permute-start(bf16[80,5120]{1,0:T(8,128)(2,1)} %collective-permute-done.3.refs_2_), channel_id=1, source_target_pairs={{0,2},{1,3},{2,0},{3,1},{4,6},{5,7},{6,4},{7,5}} | collective-permute-start | bytes 2457608 | tf_op jit(solution)/shard_map/ppermute | solution.py:404
  592.1 24.1 %collective-permute-start.68 = (bf16[640,1280]{1,0:T(8,128)(2,1)}, bf16[640,1280]{1,0:T(8,128)(2,1)}, u32[]{:S(2)}, u32[]{:S(2)}) collective-permute-start(bf16[640,1280]{1,0:T(8,128)(2,1)} %collective-permute-done.47.refs_1_), channel_id=1, source_target_pairs={{0,1},{1,0},{2,3},{3,2},{4,5},{5,4},{6,7},{7,6}} | collective-permute-start | bytes 4915208 | tf_op jit(solution)/shard_map/ppermute | solution.py:404
  608.7 7.0 collective-permute-start.8
  613.7 4.8 collective-permute-start.69
  614.2 38.0 %collective-permute-start.48 = (bf16[640,1280]{1,0:T(8,128)(2,1)}, bf16[640,1280]{1,0:T(8,128)(2,1)S(1)}, u32[]{:S(2)}, u32[]{:S(2)}) collective-permute-start(bf16[640,1280]{1,0:T(8,128)(2,1)} %collective-permute-done.47.refs_1_), channel_id=1, source_target_pairs={{0,4},{1,5},{2,6},{3,7},{4,0},{5,1},{6,2},{7,3}} | collective-permute-start | bytes 4915208 | tf_op jit(solution)/shard_map/ppermute | solution.py:404
  615.7 37.9 %collective-permute-start.33 = (bf16[160,5120]{1,0:T(8,128)(2,1)}, bf16[160,5120]{1,0:T(8,128)(2,1)S(1)}, u32[]{:S(2)}, u32[]{:S(2)}) collective-permute-start(bf16[160,5120]{1,0:T(8,128)(2,1)} %collective-permute-done.24.refs_1_), channel_id=1, source_target_pairs={{0,1},{1,0},{2,3},{3,2},{4,5},{5,4},{6,7},{7,6}} | collective-permute-start | bytes 4915208 | tf_op jit(solution)/shard_map/ppermute | solution.py:404
  616.0 38.4 %collective-permute-start.34 = (bf16[160,5120]{1,0:T(8,128)(2,1)}, bf16[160,5120]{1,0:T(8,128)(2,1)S(1)}, u32[]{:S(2)}, u32[]{:S(2)}) collective-permute-start(bf16[160,5120]{1,0:T(8,128)(2,1)} %collective-permute-done.31.refs_2_), channel_id=1, source_target_pairs={{0,1},{1,0},{2,3},{3,2},{4,5},{5,4},{6,7},{7,6}} | collective-permute-start | bytes 4915208 | tf_op jit(solution)/shard_map/ppermute | solution.py:404
  616.3 38.2 %collective-permute-start.30 = (bf16[160,5120]{1,0:T(8,128)(2,1)}, bf16[160,5120]{1,0:T(8,128)(2,1)S(1)}, u32[]{:S(2)}, u32[]{:S(2)}) collective-permute-start(bf16[160,5120]{1,0:T(8,128)(2,1)} %collective-permute-done.21.refs_2_), channel_id=1, source_target_pairs={{0,1},{1,0},{2,3},{3,2},{4,5},{5,4},{6,7},{7,6}} | collective-permute-start | bytes 4915208 | tf_op jit(solution)/shard_map/ppermute | solution.py:404
  618.5 37.3 %collective-permute-start.29 = (bf16[160,5120]{1,0:T(8,128)(2,1)}, bf16[160,5120]{1,0:T(8,128)(2,1)S(1)}, u32[]{:S(2)}, u32[]{:S(2)}) collective-permute-start(bf16[160,5120]{1,0:T(8,128)(2,1)} %copy-done.14), channel_id=1, source_target_pairs={{0,1},{1,0},{2,3},{3,2},{4,5},{5,4},{6,7},{7,6}} | collective-permute-start | bytes 4915208 | tf_op jit(solution)/shard_map/ppermute | solution.py:404
  652.2 37.2 %collective-permute-start.25 = (bf16[160,5120]{1,0:T(8,128)(2,1)}, bf16[160,5120]{1,0:T(8,128)(2,1)}, u32[]{:S(2)}, u32[]{:S(2)}) collective-permute-start(bf16[160,5120]{1,0:T(8,128)(2,1)} %collective-permute-done.24.refs_1_), channel_id=1, source_target_pairs={{0,4},{1,5},{2,6},{3,7},{4,0},{5,1},{6,2},{7,3}} | collective-permute-start | bytes 4915208 | tf_op jit(solution)/shard_map/ppermute | solution.py:404
  653.7 39.0 %collective-permute-start.22 = (bf16[160,5120]{1,0:T(8,128)(2,1)}, bf16[160,5120]{1,0:T(8,128)(2,1)}, u32[]{:S(2)}, u32[]{:S(2)}) collective-permute-start(bf16[160,5120]{1,0:T(8,128)(2,1)} %collective-permute-done.21.refs_2_), channel_id=1, source_target_pairs={{0,2},{1,3},{2,0},{3,1},{4,6},{5,7},{6,4},{7,5}} | collective-permute-start | bytes 4915208 | tf_op jit(solution)/shard_map/ppermute | solution.py:404
  654.4 38.3 %collective-permute-start.12 = (bf16[160,5120]{1,0:T(8,128)(2,1)S(1)}, bf16[160,5120]{1,0:T(8,128)(2,1)S(1)}, u32[]{:S(2)}, u32[]{:S(2)}) collective-permute-start(bf16[160,5120]{1,0:T(8,128)(2,1)S(1)} %collective-permute-done.refs_2_), channel_id=1, source_target_pairs={{0,1},{1,0},{2,3},{3,2},{4,5},{5,4},{6,7},{7,6}} | collective-permute-start | bytes 4915208 | tf_op jit(solution)/shard_map/ppermute | solution.py:404
  654.4 71.3 %collective-permute-start.1 = (bf16[160,5120]{1,0:T(8,128)(2,1)S(1)}, bf16[160,5120]{1,0:T(8,128)(2,1)}, u32[]{:S(2)}, u32[]{:S(2)}) collective-permute-start(bf16[160,5120]{1,0:T(8,128)(2,1)S(1)} %collective-permute-done.refs_2_), channel_id=1, source_target_pairs={{0,2},{1,3},{2,0},{3,1},{4,6},{5,7},{6,4},{7,5}} | collective-permute-start | bytes 4915208 | tf_op jit(solution)/shard_map/ppermute | solution.py:404
  655.8 69.9 %collective-permute-start.11 = (bf16[160,5120]{1,0:T(8,128)(2,1)S(1)}, bf16[160,5120]{1,0:T(8,128)(2,1)S(1)}, u32[]{:S(2)}, u32[]{:S(2)}) collective-permute-start(bf16[160,5120]{1,0:T(8,128)(2,1)S(1)} %collective-permute-done.9.refs_1_), channel_id=1, source_target_pairs={{0,1},{1,0},{2,3},{3,2},{4,5},{5,4},{6,7},{7,6}} | collective-permute-start | bytes 4915208 | tf_op jit(solution)/shard_map/ppermute | solution.py:404
  689.3 36.9 %collective-permute-start.49 = (bf16[640,1280]{1,0:T(8,128)(2,1)S(1)}, bf16[640,1280]{1,0:T(8,128)(2,1)S(1)}, u32[]{:S(2)}, u32[]{:S(2)}) collective-permute-start(bf16[640,1280]{1,0:T(8,128)(2,1)S(1)} %collective-permute-done.48.refs_0_), channel_id=1, source_target_pairs={{0,1},{1,0},{2,3},{3,2},{4,5},{5,4},{6,7},{7,6}} | collective-permute-start | bytes 4915208 | tf_op jit(solution)/shard_map/ppermute | solution.py:404
  692.7 96.1 %collective-permute-start.26 = (bf16[160,5120]{1,0:T(8,128)(2,1)}, bf16[160,5120]{1,0:T(8,128)(2,1)}, u32[]{:S(2)}, u32[]{:S(2)}) collective-permute-start(bf16[160,5120]{1,0:T(8,128)(2,1)} %collective-permute-done.25.refs_0_), channel_id=1, source_target_pairs={{0,1},{1,0},{2,3},{3,2},{4,5},{5,4},{6,7},{7,6}} | collective-permute-start | bytes 4915208 | tf_op jit(solution)/shard_map/ppermute | solution.py:404
  692.7 99.7 %collective-permute-start.23 = (bf16[160,5120]{1,0:T(8,128)(2,1)}, bf16[160,5120]{1,0:T(8,128)(2,1)}, u32[]{:S(2)}, u32[]{:S(2)}) collective-permute-start(bf16[160,5120]{1,0:T(8,128)(2,1)} %collective-permute-done.22.refs_0_), channel_id=1, source_target_pairs={{0,1},{1,0},{2,3},{3,2},{4,5},{5,4},{6,7},{7,6}} | collective-permute-start | bytes 4915208 | tf_op jit(solution)/shard_map/ppermute | solution.py:404
  725.7 70.4 %collective-permute-start.2 = (bf16[160,5120]{1,0:T(8,128)(2,1)}, bf16[160,5120]{1,0:T(8,128)(2,1)}, u32[]{:S(2)}, u32[]{:S(2)}) collective-permute-start(bf16[160,5120]{1,0:T(8,128)(2,1)} %collective-permute-done.1.refs_0_), channel_id=1, source_target_pairs={{0,1},{1,0},{2,3},{3,2},{4,5},{5,4},{6,7},{7,6}} | collective-permute-start | bytes 4915208 | tf_op jit(solution)/shard_map/ppermute | solution.py:404
  725.7 74.0 %collective-permute-start.40 = (bf16[160,1280]{1,0:T(8,128)(2,1)}, bf16[160,1280]{1,0:T(8,128)(2,1)}, u32[]{:S(2)}, u32[]{:S(2)}) collective-permute-start(bf16[160,1280]{1,0:T(8,128)(2,1)} %copy-done.43), channel_id=1, source_target_pairs={{0,1},{1,0},{2,3},{3,2},{4,5},{5,4},{6,7},{7,6}} | collective-permute-start | bytes 1228808 | tf_op jit(solution)/shard_map/ppermute | solution.py:404
  728.0 71.7 %collective-permute-start.37 = (bf16[160,1280]{1,0:T(8,128)(2,1)}, bf16[160,1280]{1,0:T(8,128)(2,1)}, u32[]{:S(2)}, u32[]{:S(2)}) collective-permute-start(bf16[160,1280]{1,0:T(8,128)(2,1)} %copy-done.44), channel_id=1, source_target_pairs={{0,1},{1,0},{2,3},{3,2},{4,5},{5,4},{6,7},{7,6}} | collective-permute-start | bytes 1228808 | tf_op jit(solution)/shard_map/ppermute | solution.py:404
  (53 other events, 1098.9 us)

commit v7 on v6

--- a/solution.py
+++ b/solution.py
@@ -89,7 +89,7 @@
         if i == 0 and j < 2:
             return [(0, 16), (16, n - 16)]
         if i == end and j >= 4:
-            return [(0, n - n // 5), (n - n // 5, n // 5)]
+            return [(0, n - 48), (n - 48, 48)]
         return [(0, n)]
 
     def rows(u, device, h, piece):
@@ -237,13 +237,13 @@
 
     ring = pl.ds(0, 7)
     mine_sum[...] = jnp.sum(acc[...], axis=0, keepdims=True)
-    for k in range(1, 8):
+    for to in [place(*chip, core) for chip in CHIPS for core in (1, 0)][:7]:
         pltpu.make_async_remote_copy(
             src_ref=mine_sum,
             dst_ref=norms.at[me],
             send_sem=norm_s.at[0],
             recv_sem=norm_r.at[0],
-            device_id=(rep, lax.rem(me + k, 8)),
+            device_id=(rep, to),
             device_id_type=MESH,
         ).start()
     norms[me] = mine_sum[...]

time: 803 us -> 803 us (level)
  no operation moved by 1% of the time
where the time goes in v7:
time: 803 us; the launch traced here: 802 us
  Pallas kernels  458 us (57%)
  waiting for transfers between devices  299 us (37%)
  starting transfers between devices  38 us (5%)
    pallas_call x1, Pallas kernels, summed(): pl.pallas_call(functools.partial(sum_kernel, shapes, count, head), out_sh...  330 us
    ppermute x70, waiting for transfers between devices, send(): return lax.ppermute(block, 'dp', [(d, d ^ flip) for d in range(8)])  299 us
    pallas_call x18, Pallas kernels, placed(): pl.pallas_call(functools.partial(place_kernel, places, len(before), in_vm...  72.4 us
    pallas_call x10, Pallas kernels, stepped(): pl.pallas_call(functools.partial(step_kernel, count, with_weight), out_sh...  55.6 us
    ppermute x70, starting transfers between devices, send(): return lax.ppermute(block, 'dp', [(d, d ^ flip) for d in range(8)])  38 us
  transfers between devices with their start and end apart: 70, of which 28 were waited for; matrix products, arithmetic and copies ran while one was open for 0% of the time, Pallas kernels for 14%

profile of v7, /device:TPU:0, one launch (start us, length us, event | category | flops | bytes accessed | tf_op | source)
XLA Modules:
  0.0 801.8 jit_solution(7441629774436025172)
XLA Ops:
  0.6 329.9 %sum_terms.1 = (bf16[2,160,5120]{2,1,0:T(8,128)(2,1)}, bf16[2,160,5120]{2,1,0:T(8,128)(2,1)}, bf16[2,640,1280]{2,1,0:T(8,128)(2,1)}, f32[8,128]{1,0:T(8,128)}, b...) custom-call(bf16[1,2,1280,5120]{3,2,1,0:T(8,128)(2,1)} %refs_0_.1, ...), custom_call_target="tpu_custom_call" | custom-call | tf_op jit(solution)/shard_map/sum_terms/pallas_call | solution.py:284
  330.6 7.5 adamw.15
  338.1 3.4 adamw.16
  341.4 1.3 collective-permute-start.41
  343.4 3.4 adamw.17
  346.8 1.3 collective-permute-start.44
  348.9 3.4 adamw.18
  352.3 1.7 collective-permute-done.41.refs_2_
  356.0 1.5 collective-permute-start.35
  357.5 3.4 adamw.19
  360.9 3.2 collective-permute-done.44.refs_1_
  364.9 1.5 collective-permute-start.50
  366.4 6.5 collective-permute-done.54.refs_1_
  373.5 6.7 collective-permute-done.38.refs_1_
  381.7 5.9 adamw.10
  387.6 6.3 adamw.11
  395.2 1.5 collective-permute-start.45
  397.2 1.3 collective-permute-start.39
  399.3 8.4 %collective-permute-done.45.refs_2_ = bf16[160,1280]{1,0:T(8,128)(2,1)S(1)} collective-permute-done((bf16[160,1280]{1,0:T(8,128)(2,1)}, bf16[160,1280]{1,0:T(8,128)(2,1)S(1)}, u32[]{:S(2)}, u32[]{:S(2)}) %collective-permute-start.45) | collective-permute-done | bytes 409632 | tf_op jit(solution)/shard_map/ppermute | solution.py:404
  407.7 1.5 collective-permute-start.13
  409.2 15.3 %collective-permute-done.42.refs_0_ = bf16[160,1280]{1,0:T(8,128)(2,1)S(1)} collective-permute-done((bf16[160,1280]{1,0:T(8,128)(2,1)}, bf16[160,1280]{1,0:T(8,128)(2,1)S(1)}, u32[]{:S(2)}, u32[]{:S(2)}) %collective-permute-start.42) | collective-permute-done | bytes 409632 | tf_op jit(solution)/shard_map/ppermute | solution.py:404
  425.3 7.3 collective-permute-done.36.refs_0_
  434.1 1.3 collective-permute-start.47
  436.5 7.4 adamw.13
  443.9 7.8 collective-permute-done.3.refs_2_
  451.7 2.1 collective-permute-done.17.refs_1_
  454.6 1.7 collective-permute-done.46.refs_3_
  457.2 1.6 collective-permute-done.43.refs_1_
  459.6 1.5 collective-permute-start.31
  461.1 7.5 adamw.14
  468.6 20.4 %collective-permute-done.47.refs_1_ = bf16[640,1280]{1,0:T(8,128)(2,1)} collective-permute-done((bf16[640,1280]{1,0:T(8,128)(2,1)S(1)}, bf16[640,1280]{1,0:T(8,128)(2,1)}, u32[]{:S(2)}, u32[]{:S(2)}) %collective-permute-start.47) | collective-permute-done | bytes 1638432 | tf_op jit(solution)/shard_map/ppermute | solution.py:404
  489.7 1.5 collective-permute-start.27
  491.2 32.9 %collective-permute-done.24.refs_1_ = bf16[160,5120]{1,0:T(8,128)(2,1)} collective-permute-done((bf16[160,5120]{1,0:T(8,128)(2,1)}, bf16[160,5120]{1,0:T(8,128)(2,1)}, u32[]{:S(2)}, u32[]{:S(2)}) %collective-permute-start.24) | collective-permute-done | bytes 1638432 | tf_op jit(solution)/shard_map/ppermute | solution.py:404
  524.1 7.4 adamw.12
  532.5 24.6 %collective-permute-done.21.refs_2_ = bf16[160,5120]{1,0:T(8,128)(2,1)} collective-permute-done((bf16[160,5120]{1,0:T(8,128)(2,1)}, bf16[160,5120]{1,0:T(8,128)(2,1)}, u32[]{:S(2)}, u32[]{:S(2)}) %collective-permute-start.21) | collective-permute-done | bytes 1638432 | tf_op jit(solution)/shard_map/ppermute | solution.py:404
  560.8 1.5 collective-permute-start.7
  563.3 28.8 %collective-permute-done.refs_2_ = bf16[160,5120]{1,0:T(8,128)(2,1)S(1)} collective-permute-done((bf16[160,5120]{1,0:T(8,128)(2,1)}, bf16[160,5120]{1,0:T(8,128)(2,1)S(1)}, u32[]{:S(2)}, u32[]{:S(2)}) %collective-permute-start) | collective-permute-done | bytes 1638432 | tf_op jit(solution)/shard_map/ppermute | solution.py:404
  592.1 16.6 %collective-permute-done.7.refs_2_ = bf16[80,5120]{1,0:T(8,128)(2,1)S(1)} collective-permute-done((bf16[80,5120]{1,0:T(8,128)(2,1)}, bf16[80,5120]{1,0:T(8,128)(2,1)S(1)}, u32[]{:S(2)}, u32[]{:S(2)}) %collective-permute-start.7) | collective-permute-done | bytes 819232 | tf_op jit(solution)/shard_map/ppermute | solution.py:404
  608.7 4.9 collective-permute-done.4.refs_0_
  614.1 1.5 collective-permute-start.48
  616.5 1.9 collective-permute-done.69.refs_5_
  618.5 33.5 %collective-permute-done.48.refs_0_ = bf16[640,1280]{1,0:T(8,128)(2,1)S(1)} collective-permute-done((bf16[640,1280]{1,0:T(8,128)(2,1)}, bf16[640,1280]{1,0:T(8,128)(2,1)S(1)}, u32[]{:S(2)}, u32[]{:S(2)}) %collective-permute-start.48) | collective-permute-done | bytes 1638432 | tf_op jit(solution)/shard_map/ppermute | solution.py:404
  652.1 1.5 collective-permute-start.25
  654.3 1.3 collective-permute-start.1
  655.8 33.4 %collective-permute-done.25.refs_0_ = bf16[160,5120]{1,0:T(8,128)(2,1)} collective-permute-done((bf16[160,5120]{1,0:T(8,128)(2,1)}, bf16[160,5120]{1,0:T(8,128)(2,1)}, u32[]{:S(2)}, u32[]{:S(2)}) %collective-permute-start.25) | collective-permute-done | bytes 1638432 | tf_op jit(solution)/shard_map/ppermute | solution.py:404
  690.5 2.1 collective-permute-done.22.refs_0_
  693.1 32.5 %collective-permute-done.1.refs_0_ = bf16[160,5120]{1,0:T(8,128)(2,1)} collective-permute-done((bf16[160,5120]{1,0:T(8,128)(2,1)S(1)}, bf16[160,5120]{1,0:T(8,128)(2,1)}, u32[]{:S(2)}, u32[]{:S(2)}) %collective-permute-start.1) | collective-permute-done | bytes 1638432 | tf_op jit(solution)/shard_map/ppermute | solution.py:404
  728.4 4.7 place.18.refs_6_
  733.1 4.7 place.19.refs_6_
  737.8 7.7 place.27.refs_6_
  745.5 7.7 place.23.refs_6_
  753.2 7.7 place.20.refs_4_
  760.9 1.8 place.21.refs_2_
  762.6 3.1 place.28.refs_6_
  765.7 3.1 place.29.refs_6_
  768.9 3.1 place.30.refs_6_
  772.0 3.1 place.31.refs_2_
  775.1 7.8 place.24.refs_2_
  783.0 1.7 place.32.refs_4_
  786.6 2.0 place.34.refs_2_
  788.6 3.6 place.25.refs_2_
  792.3 3.6 place.26
  796.0 3.6 place.22
  799.6 2.0 place.35
  (199 shorter events, 29.8 us)
Async XLA Ops:
  341.4 12.6 %collective-permute-start.41 = (bf16[160,1280]{1,0:T(8,128)(2,1)}, bf16[160,1280]{1,0:T(8,128)(2,1)S(1)}, u32[]{:S(2)}, u32[]{:S(2)}) collective-permute-start(bf16[160,1280]{1,0:T(8,128)(2,1)} %get-tuple-element.68.refs_0_), channel_id=1, source_target_pairs={{0,4},{1,5},{2,6},{3,7},{4,0},{5,1},{6,2},{7,3}} | collective-permute-start | bytes 1228808 | tf_op jit(solution)/shard_map/ppermute | solution.py:404
  342.7 12.5 %collective-permute-start.62 = (bf16[160,1280]{1,0:T(8,128)(2,1)}, bf16[160,1280]{1,0:T(8,128)(2,1)S(1)}, u32[]{:S(2)}, u32[]{:S(2)}) collective-permute-start(bf16[160,1280]{1,0:T(8,128)(2,1)} %get-tuple-element.68.refs_0_), channel_id=1, source_target_pairs={{0,2},{1,3},{2,0},{3,1},{4,6},{5,7},{6,4},{7,5}} | collective-permute-start | bytes 1228808 | tf_op jit(solution)/shard_map/ppermute | solution.py:404
  343.4 12.6 %collective-permute-start.63 = (bf16[160,1280]{1,0:T(8,128)(2,1)}, bf16[160,1280]{1,0:T(8,128)(2,1)S(1)}, u32[]{:S(2)}, u32[]{:S(2)}) collective-permute-start(bf16[160,1280]{1,0:T(8,128)(2,1)} %get-tuple-element.68.refs_0_), channel_id=1, source_target_pairs={{0,1},{1,0},{2,3},{3,2},{4,5},{5,4},{6,7},{7,6}} | collective-permute-start | bytes 1228808 | tf_op jit(solution)/shard_map/ppermute | solution.py:404
  346.8 17.3 %collective-permute-start.44 = (bf16[160,1280]{1,0:T(8,128)(2,1)}, bf16[160,1280]{1,0:T(8,128)(2,1)}, u32[]{:S(2)}, u32[]{:S(2)}) collective-permute-start(bf16[160,1280]{1,0:T(8,128)(2,1)} %get-tuple-element.69.refs_0_), channel_id=1, source_target_pairs={{0,2},{1,3},{2,0},{3,1},{4,6},{5,7},{6,4},{7,5}} | collective-permute-start | bytes 1228808 | tf_op jit(solution)/shard_map/ppermute | solution.py:404
  348.1 16.0 %collective-permute-start.58 = (bf16[160,1280]{1,0:T(8,128)(2,1)}, bf16[160,1280]{1,0:T(8,128)(2,1)S(1)}, u32[]{:S(2)}, u32[]{:S(2)}) collective-permute-start(bf16[160,1280]{1,0:T(8,128)(2,1)} %get-tuple-element.69.refs_0_), channel_id=1, source_target_pairs={{0,4},{1,5},{2,6},{3,7},{4,0},{5,1},{6,2},{7,3}} | collective-permute-start | bytes 1228808 | tf_op jit(solution)/shard_map/ppermute | solution.py:404
  354.0 10.9 %collective-permute-start.59 = (bf16[160,1280]{1,0:T(8,128)(2,1)S(1)}, bf16[160,1280]{1,0:T(8,128)(2,1)S(1)}, u32[]{:S(2)}, u32[]{:S(2)}) collective-permute-start(bf16[160,1280]{1,0:T(8,128)(2,1)S(1)} %copy-done.34), channel_id=1, source_target_pairs={{0,1},{1,0},{2,3},{3,2},{4,5},{5,4},{6,7},{7,6}} | collective-permute-start | bytes 1228808 | tf_op jit(solution)/shard_map/ppermute | solution.py:404
  355.2 17.7 %collective-permute-start.54 = (bf16[160,1280]{1,0:T(8,128)(2,1)}, bf16[160,1280]{1,0:T(8,128)(2,1)}, u32[]{:S(2)}, u32[]{:S(2)}) collective-permute-start(bf16[160,1280]{1,0:T(8,128)(2,1)} %get-tuple-element.64.refs_0_), channel_id=1, source_target_pairs={{0,2},{1,3},{2,0},{3,1},{4,6},{5,7},{6,4},{7,5}} | collective-permute-start | bytes 1228808 | tf_op jit(solution)/shard_map/ppermute | solution.py:404
  356.0 16.9 %collective-permute-start.35 = (bf16[160,1280]{1,0:T(8,128)(2,1)}, bf16[160,1280]{1,0:T(8,128)(2,1)}, u32[]{:S(2)}, u32[]{:S(2)}) collective-permute-start(bf16[160,1280]{1,0:T(8,128)(2,1)} %get-tuple-element.64.refs_0_), channel_id=1, source_target_pairs={{0,4},{1,5},{2,6},{3,7},{4,0},{5,1},{6,2},{7,3}} | collective-permute-start | bytes 1228808 | tf_op jit(solution)/shard_map/ppermute | solution.py:404
  364.1 9.3 %collective-permute-start.55 = (bf16[160,1280]{1,0:T(8,128)(2,1)S(1)}, bf16[160,1280]{1,0:T(8,128)(2,1)S(1)}, u32[]{:S(2)}, u32[]{:S(2)}) collective-permute-start(bf16[160,1280]{1,0:T(8,128)(2,1)S(1)} %copy-done.35), channel_id=1, source_target_pairs={{0,1},{1,0},{2,3},{3,2},{4,5},{5,4},{6,7},{7,6}} | collective-permute-start | bytes 1228808 | tf_op jit(solution)/shard_map/ppermute | solution.py:404
  364.1 16.0 %collective-permute-start.38 = (bf16[160,1280]{1,0:T(8,128)(2,1)}, bf16[160,1280]{1,0:T(8,128)(2,1)S(1)}, u32[]{:S(2)}, u32[]{:S(2)}) collective-permute-start(bf16[160,1280]{1,0:T(8,128)(2,1)} %get-tuple-element.67.refs_0_), channel_id=1, source_target_pairs={{0,2},{1,3},{2,0},{3,1},{4,6},{5,7},{6,4},{7,5}} | collective-permute-start | bytes 1228808 | tf_op jit(solution)/shard_map/ppermute | solution.py:404
  364.9 15.2 %collective-permute-start.50 = (bf16[160,1280]{1,0:T(8,128)(2,1)}, bf16[160,1280]{1,0:T(8,128)(2,1)S(1)}, u32[]{:S(2)}, u32[]{:S(2)}) collective-permute-start(bf16[160,1280]{1,0:T(8,128)(2,1)} %get-tuple-element.67.refs_0_), channel_id=1, source_target_pairs={{0,4},{1,5},{2,6},{3,7},{4,0},{5,1},{6,2},{7,3}} | collective-permute-start | bytes 1228808 | tf_op jit(solution)/shard_map/ppermute | solution.py:404
  372.9 7.8 collective-permute-start.51
  372.9 7.8 collective-permute-start.65
  373.4 20.5 %collective-permute-start.64 = (bf16[160,1280]{1,0:T(8,128)(2,1)S(1)}, bf16[160,1280]{1,0:T(8,128)(2,1)}, u32[]{:S(2)}, u32[]{:S(2)}) collective-permute-start(bf16[160,1280]{1,0:T(8,128)(2,1)S(1)} %collective-permute-done.62.refs_1_), channel_id=1, source_target_pairs={{0,1},{1,0},{2,3},{3,2},{4,5},{5,4},{6,7},{7,6}} | collective-permute-start | bytes 1228808 | tf_op jit(solution)/shard_map/ppermute | solution.py:404
  380.1 14.1 %collective-permute-start.60 = (bf16[160,1280]{1,0:T(8,128)(2,1)}, bf16[160,1280]{1,0:T(8,128)(2,1)}, u32[]{:S(2)}, u32[]{:S(2)}) collective-permute-start(bf16[160,1280]{1,0:T(8,128)(2,1)} %collective-permute-done.44.refs_1_), channel_id=1, source_target_pairs={{0,1},{1,0},{2,3},{3,2},{4,5},{5,4},{6,7},{7,6}} | collective-permute-start | bytes 1228808 | tf_op jit(solution)/shard_map/ppermute | solution.py:404
  380.2 14.3 %collective-permute-start.61 = (bf16[160,1280]{1,0:T(8,128)(2,1)S(1)}, bf16[160,1280]{1,0:T(8,128)(2,1)}, u32[]{:S(2)}, u32[]{:S(2)}) collective-permute-start(bf16[160,1280]{1,0:T(8,128)(2,1)S(1)} %collective-permute-done.58.refs_2_), channel_id=1, source_target_pairs={{0,1},{1,0},{2,3},{3,2},{4,5},{5,4},{6,7},{7,6}} | collective-permute-start | bytes 1228808 | tf_op jit(solution)/shard_map/ppermute | solution.py:404
  380.7 14.5 %collective-permute-start.56 = (bf16[160,1280]{1,0:T(8,128)(2,1)}, bf16[160,1280]{1,0:T(8,128)(2,1)}, u32[]{:S(2)}, u32[]{:S(2)}) collective-permute-start(bf16[160,1280]{1,0:T(8,128)(2,1)} %collective-permute-done.54.refs_1_), channel_id=1, source_target_pairs={{0,1},{1,0},{2,3},{3,2},{4,5},{5,4},{6,7},{7,6}} | collective-permute-start | bytes 1228808 | tf_op jit(solution)/shard_map/ppermute | solution.py:404
  380.9 15.8 %collective-permute-start.57 = (bf16[160,1280]{1,0:T(8,128)(2,1)}, bf16[160,1280]{1,0:T(8,128)(2,1)}, u32[]{:S(2)}, u32[]{:S(2)}) collective-permute-start(bf16[160,1280]{1,0:T(8,128)(2,1)} %collective-permute-done.35.refs_2_), channel_id=1, source_target_pairs={{0,1},{1,0},{2,3},{3,2},{4,5},{5,4},{6,7},{7,6}} | collective-permute-start | bytes 1228808 | tf_op jit(solution)/shard_map/ppermute | solution.py:404
  394.2 4.3 collective-permute-start.53
  394.5 38.9 %collective-permute-start.6 = (bf16[80,5120]{1,0:T(8,128)(2,1)}, bf16[80,5120]{1,0:T(8,128)(2,1)S(1)}, u32[]{:S(2)}, u32[]{:S(2)}) collective-permute-start(bf16[80,5120]{1,0:T(8,128)(2,1)} %get-tuple-element.51.refs_0_), channel_id=1, source_target_pairs={{0,2},{1,3},{2,0},{3,1},{4,6},{5,7},{6,4},{7,5}} | collective-permute-start | bytes 2457608 | tf_op jit(solution)/shard_map/ppermute | solution.py:404
  395.2 12.5 %collective-permute-start.45 = (bf16[160,1280]{1,0:T(8,128)(2,1)}, bf16[160,1280]{1,0:T(8,128)(2,1)S(1)}, u32[]{:S(2)}, u32[]{:S(2)}) collective-permute-start(bf16[160,1280]{1,0:T(8,128)(2,1)} %collective-permute-done.44.refs_1_), channel_id=1, source_target_pairs={{0,4},{1,5},{2,6},{3,7},{4,0},{5,1},{6,2},{7,3}} | collective-permute-start | bytes 1228808 | tf_op jit(solution)/shard_map/ppermute | solution.py:404
  396.7 27.9 %collective-permute-start.42 = (bf16[160,1280]{1,0:T(8,128)(2,1)}, bf16[160,1280]{1,0:T(8,128)(2,1)S(1)}, u32[]{:S(2)}, u32[]{:S(2)}) collective-permute-start(bf16[160,1280]{1,0:T(8,128)(2,1)} %copy-done.31), channel_id=1, source_target_pairs={{0,2},{1,3},{2,0},{3,1},{4,6},{5,7},{6,4},{7,5}} | collective-permute-start | bytes 1228808 | tf_op jit(solution)/shard_map/ppermute | solution.py:404
  397.2 27.4 %collective-permute-start.39 = (bf16[160,1280]{1,0:T(8,128)(2,1)}, bf16[160,1280]{1,0:T(8,128)(2,1)S(1)}, u32[]{:S(2)}, u32[]{:S(2)}) collective-permute-start(bf16[160,1280]{1,0:T(8,128)(2,1)} %copy-done.39), channel_id=1, source_target_pairs={{0,4},{1,5},{2,6},{3,7},{4,0},{5,1},{6,2},{7,3}} | collective-permute-start | bytes 1228808 | tf_op jit(solution)/shard_map/ppermute | solution.py:404
  398.5 34.1 %collective-permute-start.36 = (bf16[160,1280]{1,0:T(8,128)(2,1)}, bf16[160,1280]{1,0:T(8,128)(2,1)S(1)}, u32[]{:S(2)}, u32[]{:S(2)}) collective-permute-start(bf16[160,1280]{1,0:T(8,128)(2,1)} %collective-permute-done.35.refs_2_), channel_id=1, source_target_pairs={{0,2},{1,3},{2,0},{3,1},{4,6},{5,7},{6,4},{7,5}} | collective-permute-start | bytes 1228808 | tf_op jit(solution)/shard_map/ppermute | solution.py:404
  407.7 26.3 %collective-permute-start.13 = (bf16[80,5120]{1,0:T(8,128)(2,1)}, bf16[80,5120]{1,0:T(8,128)(2,1)S(1)}, u32[]{:S(2)}, u32[]{:S(2)}) collective-permute-start(bf16[80,5120]{1,0:T(8,128)(2,1)} %get-tuple-element.51.refs_0_), channel_id=1, source_target_pairs={{0,4},{1,5},{2,6},{3,7},{4,0},{5,1},{6,2},{7,3}} | collective-permute-start | bytes 2457608 | tf_op jit(solution)/shard_map/ppermute | solution.py:404
  424.6 10.8 %collective-permute-start.14 = (bf16[80,5120]{1,0:T(8,128)(2,1)}, bf16[80,5120]{1,0:T(8,128)(2,1)S(1)}, u32[]{:S(2)}, u32[]{:S(2)}) collective-permute-start(bf16[80,5120]{1,0:T(8,128)(2,1)} %get-tuple-element.51.refs_0_), channel_id=1, source_target_pairs={{0,1},{1,0},{2,3},{3,2},{4,5},{5,4},{6,7},{7,6}} | collective-permute-start | bytes 2457608 | tf_op jit(solution)/shard_map/ppermute | solution.py:404
  424.6 27.1 %collective-permute-start.3 = (bf16[80,5120]{1,0:T(8,128)(2,1)S(1)}, bf16[80,5120]{1,0:T(8,128)(2,1)}, u32[]{:S(2)}, u32[]{:S(2)}) collective-permute-start(bf16[80,5120]{1,0:T(8,128)(2,1)S(1)} %copy-done.23), channel_id=1, source_target_pairs={{0,4},{1,5},{2,6},{3,7},{4,0},{5,1},{6,2},{7,3}} | collective-permute-start | bytes 2457608 | tf_op jit(solution)/shard_map/ppermute | solution.py:404
  432.7 21.2 %collective-permute-start.17 = (bf16[80,5120]{1,0:T(8,128)(2,1)S(1)}, bf16[80,5120]{1,0:T(8,128)(2,1)}, u32[]{:S(2)}, u32[]{:S(2)}) collective-permute-start(bf16[80,5120]{1,0:T(8,128)(2,1)S(1)} %copy-done.23), channel_id=1, source_target_pairs={{0,2},{1,3},{2,0},{3,1},{4,6},{5,7},{6,4},{7,5}} | collective-permute-start | bytes 2457608 | tf_op jit(solution)/shard_map/ppermute | solution.py:404
  433.4 21.2 %collective-permute-start.18 = (bf16[80,5120]{1,0:T(8,128)(2,1)S(1)}, bf16[80,5120]{1,0:T(8,128)(2,1)}, u32[]{:S(2)}, u32[]{:S(2)}) collective-permute-start(bf16[80,5120]{1,0:T(8,128)(2,1)S(1)} %copy-done.23), channel_id=1, source_target_pairs={{0,1},{1,0},{2,3},{3,2},{4,5},{5,4},{6,7},{7,6}} | collective-permute-start | bytes 2457608 | tf_op jit(solution)/shard_map/ppermute | solution.py:404
  434.1 54.9 %collective-permute-start.47 = (bf16[640,1280]{1,0:T(8,128)(2,1)S(1)}, bf16[640,1280]{1,0:T(8,128)(2,1)}, u32[]{:S(2)}, u32[]{:S(2)}) collective-permute-start(bf16[640,1280]{1,0:T(8,128)(2,1)S(1)} %copy-done.12), channel_id=1, source_target_pairs={{0,2},{1,3},{2,0},{3,1},{4,6},{5,7},{6,4},{7,5}} | collective-permute-start | bytes 4915208 | tf_op jit(solution)/shard_map/ppermute | solution.py:404
  435.4 53.6 %collective-permute-start.66 = (bf16[640,1280]{1,0:T(8,128)(2,1)S(1)}, bf16[640,1280]{1,0:T(8,128)(2,1)}, u32[]{:S(2)}, u32[]{:S(2)}) collective-permute-start(bf16[640,1280]{1,0:T(8,128)(2,1)S(1)} %copy-done.12), channel_id=1, source_target_pairs={{0,4},{1,5},{2,6},{3,7},{4,0},{5,1},{6,2},{7,3}} | collective-permute-start | bytes 4915208 | tf_op jit(solution)/shard_map/ppermute | solution.py:404
  451.7 38.0 %collective-permute-start.67 = (bf16[640,1280]{1,0:T(8,128)(2,1)S(1)}, bf16[640,1280]{1,0:T(8,128)(2,1)}, u32[]{:S(2)}, u32[]{:S(2)}) collective-permute-start(bf16[640,1280]{1,0:T(8,128)(2,1)S(1)} %copy-done.12), channel_id=1, source_target_pairs={{0,1},{1,0},{2,3},{3,2},{4,5},{5,4},{6,7},{7,6}} | collective-permute-start | bytes 4915208 | tf_op jit(solution)/shard_map/ppermute | solution.py:404
  453.9 70.2 %collective-permute-start.24 = (bf16[160,5120]{1,0:T(8,128)(2,1)}, bf16[160,5120]{1,0:T(8,128)(2,1)}, u32[]{:S(2)}, u32[]{:S(2)}) collective-permute-start(bf16[160,5120]{1,0:T(8,128)(2,1)} %get-tuple-element.56.refs_0_), channel_id=1, source_target_pairs={{0,2},{1,3},{2,0},{3,1},{4,6},{5,7},{6,4},{7,5}} | collective-permute-start | bytes 4915208 | tf_op jit(solution)/shard_map/ppermute | solution.py:404
  459.6 71.9 %collective-permute-start.31 = (bf16[160,5120]{1,0:T(8,128)(2,1)}, bf16[160,5120]{1,0:T(8,128)(2,1)}, u32[]{:S(2)}, u32[]{:S(2)}) collective-permute-start(bf16[160,5120]{1,0:T(8,128)(2,1)} %get-tuple-element.56.refs_0_), channel_id=1, source_target_pairs={{0,4},{1,5},{2,6},{3,7},{4,0},{5,1},{6,2},{7,3}} | collective-permute-start | bytes 4915208 | tf_op jit(solution)/shard_map/ppermute | solution.py:404
  489.0 43.3 %collective-permute-start.32 = (bf16[160,5120]{1,0:T(8,128)(2,1)S(1)}, bf16[160,5120]{1,0:T(8,128)(2,1)}, u32[]{:S(2)}, u32[]{:S(2)}) collective-permute-start(bf16[160,5120]{1,0:T(8,128)(2,1)S(1)} %copy-done.13), channel_id=1, source_target_pairs={{0,1},{1,0},{2,3},{3,2},{4,5},{5,4},{6,7},{7,6}} | collective-permute-start | bytes 4915208 | tf_op jit(solution)/shard_map/ppermute | solution.py:404
  489.0 68.1 %collective-permute-start.21 = (bf16[160,5120]{1,0:T(8,128)(2,1)}, bf16[160,5120]{1,0:T(8,128)(2,1)}, u32[]{:S(2)}, u32[]{:S(2)}) collective-permute-start(bf16[160,5120]{1,0:T(8,128)(2,1)} %get-tuple-element.55.refs_0_), channel_id=1, source_target_pairs={{0,4},{1,5},{2,6},{3,7},{4,0},{5,1},{6,2},{7,3}} | collective-permute-start | bytes 4915208 | tf_op jit(solution)/shard_map/ppermute | solution.py:404
  489.7 67.8 %collective-permute-start.27 = (bf16[160,5120]{1,0:T(8,128)(2,1)}, bf16[160,5120]{1,0:T(8,128)(2,1)S(1)}, u32[]{:S(2)}, u32[]{:S(2)}) collective-permute-start(bf16[160,5120]{1,0:T(8,128)(2,1)} %get-tuple-element.55.refs_0_), channel_id=1, source_target_pairs={{0,2},{1,3},{2,0},{3,1},{4,6},{5,7},{6,4},{7,5}} | collective-permute-start | bytes 4915208 | tf_op jit(solution)/shard_map/ppermute | solution.py:404
  524.1 33.5 %collective-permute-start.28 = (bf16[160,5120]{1,0:T(8,128)(2,1)}, bf16[160,5120]{1,0:T(8,128)(2,1)}, u32[]{:S(2)}, u32[]{:S(2)}) collective-permute-start(bf16[160,5120]{1,0:T(8,128)(2,1)} %get-tuple-element.55.refs_0_), channel_id=1, source_target_pairs={{0,1},{1,0},{2,3},{3,2},{4,5},{5,4},{6,7},{7,6}} | collective-permute-start | bytes 4915208 | tf_op jit(solution)/shard_map/ppermute | solution.py:404
  531.5 60.6 %collective-permute-start = (bf16[160,5120]{1,0:T(8,128)(2,1)}, bf16[160,5120]{1,0:T(8,128)(2,1)S(1)}, u32[]{:S(2)}, u32[]{:S(2)}) collective-permute-start(bf16[160,5120]{1,0:T(8,128)(2,1)} %get-tuple-element.49.refs_0_), channel_id=1, source_target_pairs={{0,4},{1,5},{2,6},{3,7},{4,0},{5,1},{6,2},{7,3}} | collective-permute-start | bytes 4915208 | tf_op jit(solution)/shard_map/ppermute | solution.py:404
  532.3 25.8 %collective-permute-start.15 = (bf16[80,5120]{1,0:T(8,128)(2,1)}, bf16[80,5120]{1,0:T(8,128)(2,1)S(1)}, u32[]{:S(2)}, u32[]{:S(2)}) collective-permute-start(bf16[80,5120]{1,0:T(8,128)(2,1)} %copy-done.26), channel_id=1, source_target_pairs={{0,1},{1,0},{2,3},{3,2},{4,5},{5,4},{6,7},{7,6}} | collective-permute-start | bytes 2457608 | tf_op jit(solution)/shard_map/ppermute | solution.py:404
  557.6 4.7 collective-permute-start.19
  558.1 55.5 %collective-permute-start.9 = (bf16[160,5120]{1,0:T(8,128)(2,1)}, bf16[160,5120]{1,0:T(8,128)(2,1)S(1)}, u32[]{:S(2)}, u32[]{:S(2)}) collective-permute-start(bf16[160,5120]{1,0:T(8,128)(2,1)} %get-tuple-element.49.refs_0_), channel_id=1, source_target_pairs={{0,2},{1,3},{2,0},{3,1},{4,6},{5,7},{6,4},{7,5}} | collective-permute-start | bytes 4915208 | tf_op jit(solution)/shard_map/ppermute | solution.py:404
  559.6 54.5 %collective-permute-start.10 = (bf16[160,5120]{1,0:T(8,128)(2,1)}, bf16[160,5120]{1,0:T(8,128)(2,1)}, u32[]{:S(2)}, u32[]{:S(2)}) collective-permute-start(bf16[160,5120]{1,0:T(8,128)(2,1)} %get-tuple-element.49.refs_0_), channel_id=1, source_target_pairs={{0,1},{1,0},{2,3},{3,2},{4,5},{5,4},{6,7},{7,6}} | collective-permute-start | bytes 4915208 | tf_op jit(solution)/shard_map/ppermute | solution.py:404
  560.8 47.9 %collective-permute-start.7 = (bf16[80,5120]{1,0:T(8,128)(2,1)}, bf16[80,5120]{1,0:T(8,128)(2,1)S(1)}, u32[]{:S(2)}, u32[]{:S(2)}) collective-permute-start(bf16[80,5120]{1,0:T(8,128)(2,1)} %copy-done.26), channel_id=1, source_target_pairs={{0,4},{1,5},{2,6},{3,7},{4,0},{5,1},{6,2},{7,3}} | collective-permute-start | bytes 2457608 | tf_op jit(solution)/shard_map/ppermute | solution.py:404
  562.3 51.3 %collective-permute-start.4 = (bf16[80,5120]{1,0:T(8,128)(2,1)}, bf16[80,5120]{1,0:T(8,128)(2,1)S(1)}, u32[]{:S(2)}, u32[]{:S(2)}) collective-permute-start(bf16[80,5120]{1,0:T(8,128)(2,1)} %collective-permute-done.3.refs_2_), channel_id=1, source_target_pairs={{0,2},{1,3},{2,0},{3,1},{4,6},{5,7},{6,4},{7,5}} | collective-permute-start | bytes 2457608 | tf_op jit(solution)/shard_map/ppermute | solution.py:404
  592.1 24.1 %collective-permute-start.68 = (bf16[640,1280]{1,0:T(8,128)(2,1)}, bf16[640,1280]{1,0:T(8,128)(2,1)}, u32[]{:S(2)}, u32[]{:S(2)}) collective-permute-start(bf16[640,1280]{1,0:T(8,128)(2,1)} %collective-permute-done.47.refs_1_), channel_id=1, source_target_pairs={{0,1},{1,0},{2,3},{3,2},{4,5},{5,4},{6,7},{7,6}} | collective-permute-start | bytes 4915208 | tf_op jit(solution)/shard_map/ppermute | solution.py:404
  608.7 7.0 collective-permute-start.8
  613.6 4.8 collective-permute-start.69
  614.1 38.0 %collective-permute-start.48 = (bf16[640,1280]{1,0:T(8,128)(2,1)}, bf16[640,1280]{1,0:T(8,128)(2,1)S(1)}, u32[]{:S(2)}, u32[]{:S(2)}) collective-permute-start(bf16[640,1280]{1,0:T(8,128)(2,1)} %collective-permute-done.47.refs_1_), channel_id=1, source_target_pairs={{0,4},{1,5},{2,6},{3,7},{4,0},{5,1},{6,2},{7,3}} | collective-permute-start | bytes 4915208 | tf_op jit(solution)/shard_map/ppermute | solution.py:404
  615.6 37.9 %collective-permute-start.33 = (bf16[160,5120]{1,0:T(8,128)(2,1)}, bf16[160,5120]{1,0:T(8,128)(2,1)S(1)}, u32[]{:S(2)}, u32[]{:S(2)}) collective-permute-start(bf16[160,5120]{1,0:T(8,128)(2,1)} %collective-permute-done.24.refs_1_), channel_id=1, source_target_pairs={{0,1},{1,0},{2,3},{3,2},{4,5},{5,4},{6,7},{7,6}} | collective-permute-start | bytes 4915208 | tf_op jit(solution)/shard_map/ppermute | solution.py:404
  615.9 38.4 %collective-permute-start.34 = (bf16[160,5120]{1,0:T(8,128)(2,1)}, bf16[160,5120]{1,0:T(8,128)(2,1)S(1)}, u32[]{:S(2)}, u32[]{:S(2)}) collective-permute-start(bf16[160,5120]{1,0:T(8,128)(2,1)} %collective-permute-done.31.refs_2_), channel_id=1, source_target_pairs={{0,1},{1,0},{2,3},{3,2},{4,5},{5,4},{6,7},{7,6}} | collective-permute-start | bytes 4915208 | tf_op jit(solution)/shard_map/ppermute | solution.py:404
  616.1 38.2 %collective-permute-start.30 = (bf16[160,5120]{1,0:T(8,128)(2,1)}, bf16[160,5120]{1,0:T(8,128)(2,1)S(1)}, u32[]{:S(2)}, u32[]{:S(2)}) collective-permute-start(bf16[160,5120]{1,0:T(8,128)(2,1)} %collective-permute-done.21.refs_2_), channel_id=1, source_target_pairs={{0,1},{1,0},{2,3},{3,2},{4,5},{5,4},{6,7},{7,6}} | collective-permute-start | bytes 4915208 | tf_op jit(solution)/shard_map/ppermute | solution.py:404
  618.4 37.3 %collective-permute-start.29 = (bf16[160,5120]{1,0:T(8,128)(2,1)}, bf16[160,5120]{1,0:T(8,128)(2,1)S(1)}, u32[]{:S(2)}, u32[]{:S(2)}) collective-permute-start(bf16[160,5120]{1,0:T(8,128)(2,1)} %copy-done.14), channel_id=1, source_target_pairs={{0,1},{1,0},{2,3},{3,2},{4,5},{5,4},{6,7},{7,6}} | collective-permute-start | bytes 4915208 | tf_op jit(solution)/shard_map/ppermute | solution.py:404
  652.1 37.2 %collective-permute-start.25 = (bf16[160,5120]{1,0:T(8,128)(2,1)}, bf16[160,5120]{1,0:T(8,128)(2,1)}, u32[]{:S(2)}, u32[]{:S(2)}) collective-permute-start(bf16[160,5120]{1,0:T(8,128)(2,1)} %collective-permute-done.24.refs_1_), channel_id=1, source_target_pairs={{0,4},{1,5},{2,6},{3,7},{4,0},{5,1},{6,2},{7,3}} | collective-permute-start | bytes 4915208 | tf_op jit(solution)/shard_map/ppermute | solution.py:404
  653.6 39.0 %collective-permute-start.22 = (bf16[160,5120]{1,0:T(8,128)(2,1)}, bf16[160,5120]{1,0:T(8,128)(2,1)}, u32[]{:S(2)}, u32[]{:S(2)}) collective-permute-start(bf16[160,5120]{1,0:T(8,128)(2,1)} %collective-permute-done.21.refs_2_), channel_id=1, source_target_pairs={{0,2},{1,3},{2,0},{3,1},{4,6},{5,7},{6,4},{7,5}} | collective-permute-start | bytes 4915208 | tf_op jit(solution)/shard_map/ppermute | solution.py:404
  654.3 38.3 %collective-permute-start.12 = (bf16[160,5120]{1,0:T(8,128)(2,1)S(1)}, bf16[160,5120]{1,0:T(8,128)(2,1)S(1)}, u32[]{:S(2)}, u32[]{:S(2)}) collective-permute-start(bf16[160,5120]{1,0:T(8,128)(2,1)S(1)} %collective-permute-done.refs_2_), channel_id=1, source_target_pairs={{0,1},{1,0},{2,3},{3,2},{4,5},{5,4},{6,7},{7,6}} | collective-permute-start | bytes 4915208 | tf_op jit(solution)/shard_map/ppermute | solution.py:404
  654.3 71.3 %collective-permute-start.1 = (bf16[160,5120]{1,0:T(8,128)(2,1)S(1)}, bf16[160,5120]{1,0:T(8,128)(2,1)}, u32[]{:S(2)}, u32[]{:S(2)}) collective-permute-start(bf16[160,5120]{1,0:T(8,128)(2,1)S(1)} %collective-permute-done.refs_2_), channel_id=1, source_target_pairs={{0,2},{1,3},{2,0},{3,1},{4,6},{5,7},{6,4},{7,5}} | collective-permute-start | bytes 4915208 | tf_op jit(solution)/shard_map/ppermute | solution.py:404
  655.6 69.9 %collective-permute-start.11 = (bf16[160,5120]{1,0:T(8,128)(2,1)S(1)}, bf16[160,5120]{1,0:T(8,128)(2,1)S(1)}, u32[]{:S(2)}, u32[]{:S(2)}) collective-permute-start(bf16[160,5120]{1,0:T(8,128)(2,1)S(1)} %collective-permute-done.9.refs_1_), channel_id=1, source_target_pairs={{0,1},{1,0},{2,3},{3,2},{4,5},{5,4},{6,7},{7,6}} | collective-permute-start | bytes 4915208 | tf_op jit(solution)/shard_map/ppermute | solution.py:404
  689.3 36.8 %collective-permute-start.49 = (bf16[640,1280]{1,0:T(8,128)(2,1)S(1)}, bf16[640,1280]{1,0:T(8,128)(2,1)S(1)}, u32[]{:S(2)}, u32[]{:S(2)}) collective-permute-start(bf16[640,1280]{1,0:T(8,128)(2,1)S(1)} %collective-permute-done.48.refs_0_), channel_id=1, source_target_pairs={{0,1},{1,0},{2,3},{3,2},{4,5},{5,4},{6,7},{7,6}} | collective-permute-start | bytes 4915208 | tf_op jit(solution)/shard_map/ppermute | solution.py:404
  692.5 96.1 %collective-permute-start.26 = (bf16[160,5120]{1,0:T(8,128)(2,1)}, bf16[160,5120]{1,0:T(8,128)(2,1)}, u32[]{:S(2)}, u32[]{:S(2)}) collective-permute-start(bf16[160,5120]{1,0:T(8,128)(2,1)} %collective-permute-done.25.refs_0_), channel_id=1, source_target_pairs={{0,1},{1,0},{2,3},{3,2},{4,5},{5,4},{6,7},{7,6}} | collective-permute-start | bytes 4915208 | tf_op jit(solution)/shard_map/ppermute | solution.py:404
  692.6 99.7 %collective-permute-start.23 = (bf16[160,5120]{1,0:T(8,128)(2,1)}, bf16[160,5120]{1,0:T(8,128)(2,1)}, u32[]{:S(2)}, u32[]{:S(2)}) collective-permute-start(bf16[160,5120]{1,0:T(8,128)(2,1)} %collective-permute-done.22.refs_0_), channel_id=1, source_target_pairs={{0,1},{1,0},{2,3},{3,2},{4,5},{5,4},{6,7},{7,6}} | collective-permute-start | bytes 4915208 | tf_op jit(solution)/shard_map/ppermute | solution.py:404
  725.6 70.4 %collective-permute-start.2 = (bf16[160,5120]{1,0:T(8,128)(2,1)}, bf16[160,5120]{1,0:T(8,128)(2,1)}, u32[]{:S(2)}, u32[]{:S(2)}) collective-permute-start(bf16[160,5120]{1,0:T(8,128)(2,1)} %collective-permute-done.1.refs_0_), channel_id=1, source_target_pairs={{0,1},{1,0},{2,3},{3,2},{4,5},{5,4},{6,7},{7,6}} | collective-permute-start | bytes 4915208 | tf_op jit(solution)/shard_map/ppermute | solution.py:404
  725.6 74.0 %collective-permute-start.40 = (bf16[160,1280]{1,0:T(8,128)(2,1)}, bf16[160,1280]{1,0:T(8,128)(2,1)}, u32[]{:S(2)}, u32[]{:S(2)}) collective-permute-start(bf16[160,1280]{1,0:T(8,128)(2,1)} %copy-done.43), channel_id=1, source_target_pairs={{0,1},{1,0},{2,3},{3,2},{4,5},{5,4},{6,7},{7,6}} | collective-permute-start | bytes 1228808 | tf_op jit(solution)/shard_map/ppermute | solution.py:404
  727.9 71.7 %collective-permute-start.37 = (bf16[160,1280]{1,0:T(8,128)(2,1)}, bf16[160,1280]{1,0:T(8,128)(2,1)}, u32[]{:S(2)}, u32[]{:S(2)}) collective-permute-start(bf16[160,1280]{1,0:T(8,128)(2,1)} %copy-done.44), channel_id=1, source_target_pairs={{0,1},{1,0},{2,3},{3,2},{4,5},{5,4},{6,7},{7,6}} | collective-permute-start | bytes 1228808 | tf_op jit(solution)/shard_map/ppermute | solution.py:404
  (53 other events, 1098.7 us)
